TPU v7x, 32 devices: a whole 2x2x4 slice. The times are simulated.
32 devices in a mesh: seq: 4 (over y, x), dp: 8 (over z, core).
Axes of the slice: x: 2, y: 2, z: 4, core: 2. Of those that a mesh axis runs over, the one named last changes fastest.
Arguments:
- tokens: bfloat16 [8, 1024, 2304], P('dp', 'seq'), may hold values from -6 to 6
- cotangent: bfloat16 [8, 1024, 2304], P('dp', 'seq'), may hold values from -6 to 6
- qkv_weight: float32 [256, 9, 4096], P(('seq', 'dp')), may hold values from -0.125 to 0.125
- out_weight: float32 [256, 8, 2304], P(('seq', 'dp')), may hold values from -0.125 to 0.125
- geglu_weight: float32 [256, 9, 18432], P(('seq', 'dp')), may hold values from -0.125 to 0.125
- down_weight: float32 [256, 36, 2304], P(('seq', 'dp')), may hold values from -0.0625 to 0.0625
- norm_gains: float32 [2304, 4], P(('seq', 'dp')), may hold values from 0.5 to 1.5
- seq_lengths: int32 [8], P('dp'), may hold values from 129 to 1024, as said below
- prefix_lengths: int32 [8], P('dp'), may hold values from 0 to 256, as said below
- block_owners: int32 [1188], replicated, may hold values from 0 to 31, as said below
- first_moment: float32 [1216, 256, 256], P(('seq', 'dp')), may hold values from -0.0068359375 to 0.0068359375
- second_moment: float32 [1216, 256, 256], P(('seq', 'dp')), may hold values from 8e-07 to 3.2e-06
- left_basis: float32 [1216, 256, 256], P(('seq', 'dp')), may hold values from -0.375 to 0.375
- right_basis: float32 [1216, 256, 256], P(('seq', 'dp')), may hold values from -0.375 to 0.375
- slot_weight: float32 [1216, 256, 256], P(('seq', 'dp')), may hold values from -1.5 to 1.5
Outputs:
- layer_out: bfloat16 [8, 1024, 2304], P('dp', 'seq')
- row_rms: float32 [8, 1024], P('dp', 'seq')
- token_grad: float32 [8, 1024, 2304], P('dp', 'seq')
- qkv_grad: float32 [256, 9, 4096], P(('seq', 'dp'))
- out_grad: float32 [256, 8, 2304], P(('seq', 'dp'))
- geglu_grad: float32 [256, 9, 18432], P(('seq', 'dp'))
- down_grad: float32 [256, 36, 2304], P(('seq', 'dp'))
- gains_grad: float32 [2304, 4], P(('seq', 'dp'))
- first_new: float32 [1216, 256, 256], P(('seq', 'dp'))
- second_new: float32 [1216, 256, 256], P(('seq', 'dp'))
- weight_new: float32 [1216, 256, 256], P(('seq', 'dp'))
Inputs may be any that keep to these rules, and one draw needn't show every extreme that they name: `seq_lengths`: one sequence is full, with length 1024. `prefix_lengths`: each prefix is at most its sequence's length; the full sequence's prefix is 256. `block_owners`: each owner is listed for at most 38 blocks, and some owner for exactly 38.
All inputs are finite; a program needn't handle non-finite values.
Results may differ from a plain program's by a relative error of at most 0.017.
Values may be sent and summed in bfloat16 or wider, within the bound.
A program may use at most 512 MiB of HBM per device.

v0:
```python
import jax
import jax.numpy as jnp
from jax import lax
from jax.sharding import PartitionSpec as P

D = 2304
QUERY_HEADS = 8
KV_HEAD_COUNT = 4
HEAD_SIZE = 256
FF = 9216
BLK = 256
QUERY_FEATURES = 2048
KEY_FEATURES = 1024


EPSILON = 1e-06
SOFT_CAP = 50.0
NEGATIVE = -1e30
BETA_ONE = 0.9
BETA_TWO = 0.95
STEP_RATE = 0.05
TINY_ADD = 1e-08
CLIP_NORM = 1.0


def norm_forward(value_rows, gain):
    inverse = lax.rsqrt(jnp.mean(value_rows * value_rows, axis=-1, keepdims=True) + EPSILON)
    return (value_rows * inverse * gain, inverse)


def norm_backward(value_rows, inverse, gain, upstream):
    weighted = upstream * gain
    cubed = inverse * inverse * inverse
    grad_in = inverse * weighted - value_rows * cubed * jnp.mean(
        value_rows * weighted, axis=-1, keepdims=True
    )
    return (grad_in, jnp.sum(upstream * value_rows * inverse, axis=0))


def rows_major(left, groups):
    return jnp.transpose(left.reshape(left.shape[0], groups, BLK), (0, 2, 1))


def rows_back(result):
    return jnp.transpose(result, (0, 2, 1)).reshape(
        result.shape[0], result.shape[1] * result.shape[2]
    )


def apply_rows(left, weight):
    blocks, groups, width = weight.shape
    flat = rows_major(left, groups).reshape(left.shape[0], blocks * groups)
    return jnp.dot(flat, weight.reshape(blocks * groups, width), preferred_element_type=jnp.float32)


def apply_back(gradient, weight):
    blocks, groups, width = weight.shape
    result = lax.dot_general(
        gradient,
        weight.reshape(blocks * groups, width),
        (((1,), (1,)), ((), ())),
        preferred_element_type=jnp.float32,
    )
    return rows_back(result.reshape(gradient.shape[0], blocks, groups))


def apply_piece(left, piece):
    count, groups, width = piece.shape
    part_rows = rows_major(left, groups).reshape(left.shape[0], count * groups)
    return jnp.dot(
        part_rows, piece.reshape(count * groups, width), preferred_element_type=jnp.float32
    )


def back_piece(gradient, piece):
    count, groups, width = piece.shape
    result = lax.dot_general(
        gradient,
        piece.reshape(count * groups, width),
        (((1,), (1,)), ((), ())),
        preferred_element_type=jnp.float32,
    )
    return result.reshape(gradient.shape[0], count, groups)


def weight_term(left, gradient, start, count):
    groups = left.shape[1] // BLK
    part_rows = lax.dynamic_slice_in_dim(rows_major(left, groups), start, count, 1).reshape(
        left.shape[0], count * groups
    )
    result = lax.dot_general(
        part_rows, gradient, (((0,), (0,)), ((), ())), preferred_element_type=jnp.float32
    )
    return result.reshape(count, groups, gradient.shape[1])


def full_term(left, gradient):
    return weight_term(left, gradient, 0, BLK)


def to_pieces(gradient):
    count_of_rows, groups, col_count = gradient.shape
    shaped = gradient.reshape(count_of_rows, groups, col_count // BLK, BLK)
    return jnp.transpose(shaped, (1, 2, 0, 3)).reshape(-1, count_of_rows, BLK)


def body(
    tokens,
    cotangent,
    qkv_weight,
    out_weight,
    geglu_weight,
    down_weight,
    norm_gains,
    seq_lengths,
    prefix_lengths,
    block_owners,
    first_moment,
    second_moment,
    left_basis,
    right_basis,
    slot_weight,
):
    inputs = tokens[0].astype(jnp.float32)
    upstream = cotangent[0].astype(jnp.float32)
    count_of_rows = inputs.shape[0]
    length = seq_lengths[0]
    prefix = prefix_lengths[0]
    seq_count = lax.axis_size("seq")
    seq_index = lax.axis_index("seq")
    share = qkv_weight.shape[0]
    head_group = QUERY_HEADS // KV_HEAD_COUNT
    grouped_shape = (KV_HEAD_COUNT, head_group, count_of_rows, count_of_rows)
    per_head_shape = (count_of_rows, KV_HEAD_COUNT, head_group, HEAD_SIZE)
    key_value_shape = (count_of_rows, KV_HEAD_COUNT, HEAD_SIZE)
    qkv_low = qkv_weight.astype(jnp.bfloat16)
    out_low = out_weight.astype(jnp.bfloat16)
    geglu_low = geglu_weight.astype(jnp.bfloat16)
    down_low = down_weight.astype(jnp.bfloat16)
    qkv_full, out_full, gain_full = (
        lax.all_gather(qkv_low, ("seq", "dp"), axis=0, tiled=True),
        lax.all_gather(out_low, ("seq", "dp"), axis=0, tiled=True),
        lax.all_gather(norm_gains.astype(jnp.bfloat16), ("seq", "dp"), axis=0, tiled=True),
    )
    gains = gain_full.astype(jnp.float32)
    normed, inverse_one = norm_forward(inputs, gains[:, 0])
    normed_low = normed.astype(jnp.bfloat16)
    merged_heads = apply_rows(normed_low, qkv_full).astype(jnp.bfloat16)
    query_rows = merged_heads[:, :QUERY_FEATURES].reshape(per_head_shape)
    keys_own = merged_heads[:, QUERY_FEATURES : QUERY_FEATURES + KEY_FEATURES].reshape(
        key_value_shape
    )
    values_own = merged_heads[:, QUERY_FEATURES + KEY_FEATURES :].reshape(key_value_shape)
    keys_all, values_all = (
        lax.all_gather(keys_own, "seq", axis=0, tiled=True),
        lax.all_gather(values_own, "seq", axis=0, tiled=True),
    )
    query_pos = seq_index * count_of_rows + jnp.arange(count_of_rows, dtype=jnp.int32)

    def is_live(block):
        return (block <= seq_index) & (block * count_of_rows < length)

    def block_scores(block, key_source):
        key_block = key_source[block * count_of_rows : (block + 1) * count_of_rows]
        raw = jnp.einsum(
            "igrh,jgh->grij", query_rows, key_block, preferred_element_type=jnp.float32
        )
        bent = jnp.tanh(raw * HEAD_SIZE ** (-0.5) / SOFT_CAP)
        key_pos = block * count_of_rows + jnp.arange(count_of_rows, dtype=jnp.int32)
        visible = (key_pos[None, :] < length) & (
            (key_pos[None, :] <= query_pos[:, None]) | (key_pos[None, :] < prefix)
        )
        return (jnp.where(visible, SOFT_CAP * bent, NEGATIVE), bent)

    score_blocks = []
    for block in range(seq_count):
        score_blocks.append(
            lax.cond(
                is_live(block),
                lambda block=block: block_scores(block, keys_all)[0],
                lambda: jnp.full(grouped_shape, NEGATIVE, jnp.float32),
            )
        )
    scores = jnp.concatenate(score_blocks, axis=-1)
    highest = jnp.max(scores, axis=-1, keepdims=True)
    exponent = jnp.exp(scores - highest)
    total = jnp.sum(exponent, axis=-1, keepdims=True)
    probs_low = (exponent / total).astype(jnp.bfloat16)
    mixed = jnp.zeros(per_head_shape, jnp.float32)
    for block in range(seq_count):

        def mix_block(block=block):
            cols = slice(block * count_of_rows, (block + 1) * count_of_rows)
            return jnp.einsum(
                "grij,jgh->igrh",
                probs_low[..., cols],
                values_all[cols],
                preferred_element_type=jnp.float32,
            )

        mixed = mixed + lax.cond(
            is_live(block), mix_block, lambda: jnp.zeros(per_head_shape, jnp.float32)
        )
    mixed_low = mixed.reshape(count_of_rows, QUERY_FEATURES).astype(jnp.bfloat16)
    attended = apply_rows(mixed_low, out_full)
    attn_normed, inverse_two = norm_forward(attended, gains[:, 1])
    hidden = inputs + attn_normed
    ffn_normed, inverse_three = norm_forward(hidden, gains[:, 2])
    ffn_low = ffn_normed.astype(jnp.bfloat16)
    gate_up = apply_piece(ffn_low, lax.all_gather(geglu_low, ("seq", "dp"), axis=0, tiled=True))
    gate = gate_up[:, :FF]
    upper = gate_up[:, FF:]
    activated, gelu_pull = jax.vjp(lambda value: jax.nn.gelu(value, approximate=True), gate)
    product_low = (activated * upper).astype(jnp.bfloat16)
    branch = apply_piece(product_low, lax.all_gather(down_low, ("seq", "dp"), axis=0, tiled=True))
    branch_normed, inverse_four = norm_forward(branch, gains[:, 3])
    live_rows = (query_pos < length).astype(jnp.float32)[:, None]
    layer_out = ((hidden + branch_normed) * live_rows).astype(jnp.bfloat16)
    row_rms = jnp.sqrt(jnp.mean(inputs * inputs, axis=-1) + EPSILON)
    upstream = upstream * live_rows
    grad_branch, gain_four = norm_backward(branch, inverse_four, gains[:, 3], upstream)
    branch_low = grad_branch.astype(jnp.bfloat16)
    grad_product = rows_back(
        back_piece(branch_low, lax.all_gather(down_low, ("seq", "dp"), axis=0, tiled=True))
    )
    grad_gate = gelu_pull(grad_product * upper)[0]
    grad_upper = grad_product * activated
    gate_up_low = jnp.concatenate([grad_gate, grad_upper], axis=1).astype(jnp.bfloat16)
    ffn_rows, gate_rows, product_rows, branch_rows = (
        lax.all_gather(ffn_low, "seq", axis=0, tiled=True),
        lax.all_gather(gate_up_low, "seq", axis=0, tiled=True),
        lax.all_gather(product_low, "seq", axis=0, tiled=True),
        lax.all_gather(branch_low, "seq", axis=0, tiled=True),
    )
    group_base = seq_index * share * lax.axis_size("dp")
    down_width = FF // BLK * D
    count = share * lax.axis_size("dp")
    down_part = weight_term(product_rows, branch_rows, group_base, count).reshape(count, down_width)
    geglu_part = weight_term(ffn_rows, gate_rows, group_base, count).reshape(
        count, D // BLK * 2 * FF
    )
    joined = lax.psum_scatter(
        jnp.concatenate([down_part, geglu_part], axis=1).astype(jnp.bfloat16),
        "dp",
        scatter_dimension=0,
        tiled=True,
    ).astype(jnp.float32)
    down_grad = joined[:, :down_width].reshape(share, FF // BLK, D)
    geglu_grad = joined[:, down_width:].reshape(share, D // BLK, 2 * FF)
    grad_ffn = rows_back(
        back_piece(gate_up_low, lax.all_gather(geglu_low, ("seq", "dp"), axis=0, tiled=True))
    )
    grad_hidden_norm, gain_three = norm_backward(hidden, inverse_three, gains[:, 2], grad_ffn)
    grad_hidden = upstream + grad_hidden_norm
    grad_attended, gain_two = norm_backward(attended, inverse_two, gains[:, 1], grad_hidden)
    attended_low = grad_attended.astype(jnp.bfloat16)
    qkv_back, out_back = (
        lax.all_gather(qkv_low, ("seq", "dp"), axis=0, tiled=True),
        lax.all_gather(out_low, ("seq", "dp"), axis=0, tiled=True),
    )
    grad_mixed = apply_back(attended_low, out_back).astype(jnp.bfloat16).reshape(per_head_shape)
    keys_back, values_back = (keys_all, values_all)
    zero_scores = jnp.zeros(grouped_shape, jnp.float32)
    prob_blocks = []
    dprob_blocks = []
    bent_blocks = []
    for block in range(seq_count):

        def first_pass(block=block):
            capped, bent = block_scores(block, keys_back)
            prob = jnp.exp(capped - highest) / total
            value_block = values_back[block * count_of_rows : (block + 1) * count_of_rows]
            dprob = jnp.einsum(
                "igrh,jgh->grij", grad_mixed, value_block, preferred_element_type=jnp.float32
            )
            return (prob, dprob, bent)

        prob, dprob, bent = lax.cond(
            is_live(block), first_pass, lambda: (zero_scores, zero_scores, zero_scores)
        )
        prob_blocks.append(prob)
        dprob_blocks.append(dprob)
        bent_blocks.append(bent)
    probs_full = jnp.concatenate(prob_blocks, axis=-1)
    dprobs_full = jnp.concatenate(dprob_blocks, axis=-1)
    balance = jnp.sum(probs_full * dprobs_full, axis=-1, keepdims=True)
    grad_queries = jnp.zeros(per_head_shape, jnp.float32)
    key_parts = []
    value_parts = []
    zero_kv = jnp.zeros(key_value_shape, jnp.float32)
    for block in range(seq_count):

        def second_pass(block=block):
            prob = prob_blocks[block]
            bent = bent_blocks[block]
            grad_raw = (
                prob * (dprob_blocks[block] - balance) * (1.0 - bent * bent) * HEAD_SIZE ** (-0.5)
            ).astype(jnp.bfloat16)
            key_block = keys_back[block * count_of_rows : (block + 1) * count_of_rows]
            query_part = jnp.einsum(
                "grij,jgh->igrh", grad_raw, key_block, preferred_element_type=jnp.float32
            )
            key_part = jnp.einsum(
                "grij,igrh->jgh", grad_raw, query_rows, preferred_element_type=jnp.float32
            )
            value_part = jnp.einsum(
                "grij,igrh->jgh",
                prob.astype(jnp.bfloat16),
                grad_mixed,
                preferred_element_type=jnp.float32,
            )
            return (query_part, key_part, value_part)

        query_part, key_part, value_part = lax.cond(
            is_live(block),
            second_pass,
            lambda: (jnp.zeros(per_head_shape, jnp.float32), zero_kv, zero_kv),
        )
        grad_queries = grad_queries + query_part
        key_parts.append(key_part)
        value_parts.append(value_part)
    grad_keys, grad_values = (
        lax.psum_scatter(
            jnp.concatenate(key_parts, axis=0).astype(jnp.bfloat16),
            "seq",
            scatter_dimension=0,
            tiled=True,
        ).astype(jnp.float32),
        lax.psum_scatter(
            jnp.concatenate(value_parts, axis=0).astype(jnp.bfloat16),
            "seq",
            scatter_dimension=0,
            tiled=True,
        ).astype(jnp.float32),
    )
    grad_merged = jnp.concatenate(
        [
            grad_queries.reshape(count_of_rows, QUERY_FEATURES),
            grad_keys.reshape(count_of_rows, KEY_FEATURES),
            grad_values.reshape(count_of_rows, KEY_FEATURES),
        ],
        axis=1,
    ).astype(jnp.bfloat16)
    grad_normed = apply_back(grad_merged, qkv_back)
    grad_input_norm, gain_one = norm_backward(inputs, inverse_one, gains[:, 0], grad_normed)
    token_grad = grad_hidden + grad_input_norm
    qkv_term = full_term(normed_low, grad_merged)
    out_term = full_term(mixed_low, attended_low)
    gain_term = jnp.stack([gain_one, gain_two, gain_three, gain_four], axis=1)
    qkv_grad, out_grad, gains_grad = (
        lax.psum_scatter(qkv_term, ("seq", "dp"), scatter_dimension=0, tiled=True),
        lax.psum_scatter(out_term, ("seq", "dp"), scatter_dimension=0, tiled=True),
        lax.psum_scatter(gain_term, ("seq", "dp"), scatter_dimension=0, tiled=True),
    )
    pieces = jnp.concatenate(
        [to_pieces(qkv_grad), to_pieces(out_grad), to_pieces(geglu_grad), to_pieces(down_grad)],
        axis=0,
    )
    devices = lax.axis_size(("seq", "dp"))
    capacity = first_moment.shape[0]
    onehot = (block_owners[:, None] == jnp.arange(devices, dtype=jnp.int32)[None, :]).astype(
        jnp.int32
    )
    before = jnp.cumsum(onehot, axis=0) - onehot
    rank = jnp.sum(before * onehot, axis=1)
    slots = block_owners * capacity + rank
    outgoing = jnp.zeros((devices * capacity, share, BLK), jnp.float32).at[slots].set(pieces)
    incoming = lax.all_to_all(
        outgoing.astype(jnp.bfloat16), ("seq", "dp"), split_axis=0, concat_axis=0, tiled=True
    ).astype(outgoing.dtype)
    blocks = jnp.transpose(incoming.reshape(devices, capacity, share, BLK), (1, 0, 2, 3)).reshape(
        capacity, BLK, BLK
    )
    block_size = jnp.sqrt(jnp.sum(blocks * blocks, axis=(1, 2), keepdims=True))
    clipped = blocks * (CLIP_NORM / jnp.maximum(block_size, CLIP_NORM))
    highest_prec = lax.Precision.HIGHEST
    turned = jnp.einsum(
        "kji,kjl->kil",
        left_basis,
        clipped,
        precision=highest_prec,
        preferred_element_type=jnp.float32,
    )
    rotated = jnp.einsum(
        "kil,klm->kim",
        turned,
        right_basis,
        precision=highest_prec,
        preferred_element_type=jnp.float32,
    )
    first_new = BETA_ONE * first_moment + (1.0 - BETA_ONE) * rotated
    second_new = BETA_TWO * second_moment + (1.0 - BETA_TWO) * rotated * rotated
    direction = first_new / (jnp.sqrt(second_new) + TINY_ADD)
    back_left = jnp.einsum(
        "kij,kjl->kil",
        left_basis,
        direction,
        precision=highest_prec,
        preferred_element_type=jnp.float32,
    )
    weight_new = slot_weight - STEP_RATE * jnp.einsum(
        "kil,kml->kim",
        back_left,
        right_basis,
        precision=highest_prec,
        preferred_element_type=jnp.float32,
    )
    return (
        layer_out[None],
        row_rms[None],
        token_grad[None],
        qkv_grad,
        out_grad,
        geglu_grad,
        down_grad,
        gains_grad,
        first_new,
        second_new,
        weight_new,
    )


def solution(mesh):
    in_specs = (
        P("dp", "seq", None),
        P("dp", "seq", None),
        P(("seq", "dp"), None, None),
        P(("seq", "dp"), None, None),
        P(("seq", "dp"), None, None),
        P(("seq", "dp"), None, None),
        P(("seq", "dp"), None),
        P("dp"),
        P("dp"),
        P(),
        P(("seq", "dp"), None, None),
        P(("seq", "dp"), None, None),
        P(("seq", "dp"), None, None),
        P(("seq", "dp"), None, None),
        P(("seq", "dp"), None, None),
    )
    out_specs = (
        P("dp", "seq", None),
        P("dp", "seq"),
        P("dp", "seq", None),
        P(("seq", "dp"), None, None),
        P(("seq", "dp"), None, None),
        P(("seq", "dp"), None, None),
        P(("seq", "dp"), None, None),
        P(("seq", "dp"), None),
        P(("seq", "dp"), None, None),
        P(("seq", "dp"), None, None),
        P(("seq", "dp"), None, None),
    )
    return jax.shard_map(body, mesh=mesh, in_specs=in_specs, out_specs=out_specs, check_vma=False)
```

profile of v0, /device:TPU:0, one launch (start us, length us, event | category | flops | bytes accessed | tf_op | source)
XLA Modules:
  0.0 3042.3 jit_solution(13477815825066676305)
XLA Ops:
  9.6 44.0 %all-gather = bf16[32,72,4]{1,2,0:T(4,128)(2,1)S(1)} all-gather(bf16[1,72,4]{1,2,0:T(4,128)(2,1)S(1)} %convert_bitcast_fusion.1), channel_id=1, replica_groups=mesh['seq'=4,'dp'=8] {'seq','dp'}, dimensions={0}, use_global_device_ids=true | all-gather | bytes 19008 | tf_op jit(solution)/shard_map/all_gather | solution.py:143
  59.1 78.9 %all-gather.12.cloned.1.call-done = bf16[256,9,4096]{2,0,1:T(8,128)(2,1)} async-done(((bf16[8,9,4096]{2,0,1:T(8,128)(2,1)}), bf16[256,9,4096]{2,0,1:T(8,128)(2,1)}) %all-gather.12.cloned.1.call-update) | async-done | bytes 18874384 | tf_op jit(solution)/shard_map/all_gather | solution.py:141
  138.0 9.8 fusion.104
  151.8 4.3 convert_element_type.170
  162.1 21.7 all-gather.16.cloned.1.call-done
  190.3 3.7 conditional.16
  196.0 4.4 fusion.107
  202.0 3.3 divide_convert_fusion
  205.2 16.3 all-gather.14.cloned.1.call-done
  223.2 7.1 conditional.20
  223.2 3.9 copy.337
  231.8 4.6 add_convert_fusion.1
  236.5 70.1 %all-gather.18.cloned.1.call-done = bf16[256,8,2304]{2,1,0:T(8,128)(2,1)} async-done(((bf16[8,8,2304]{2,1,0:T(8,128)(2,1)}), bf16[256,8,2304]{2,1,0:T(8,128)(2,1)}) %all-gather.18.cloned.1.call-update) | async-done | bytes 9437200 | tf_op jit(solution)/shard_map/all_gather | solution.py:142
  306.6 7.0 multiply_reduce_fusion.7
  319.5 430.3 %all-gather.20.cloned.1.call-done = bf16[256,9,18432]{2,0,1:T(8,128)(2,1)} async-done(((bf16[8,9,18432]{2,0,1:T(8,128)(2,1)}), bf16[256,9,18432]{2,0,1:T(8,128)(2,1)}) %all-gather.20.cloned.1.call-update) | async-done | bytes 84934672 | tf_op jit(solution)/shard_map/all_gather | solution.py:210
  749.9 39.6 %convolution_bitcast_fusion.20 = f32[256,18432]{1,0:T(8,128)} fusion(bf16[256,256,9]{0,1,2:T(8,128)(2,1)S(1)} %bitcast.474, bf16[256,9,18432]{2,0,1:T(8,128)(2,1)} %all-gather.20.cloned.1.call-done), kind=kOutput, calls=%fused_computation.145 | convolution fusion | flops 21743271936 | bytes 104988672 | tf_op jit(solution)/shard_map/dot_general | solution.py:70
  789.5 10.2 multiply_convert_fusion.5
  799.8 6.6 copy.344
  806.5 181.7 %all-gather.22.cloned.1.call-done = bf16[256,36,2304]{2,0,1:T(8,128)(2,1)} async-done(((bf16[8,36,2304]{2,0,1:T(8,128)(2,1)}), bf16[256,36,2304]{2,0,1:T(8,128)(2,1)}) %all-gather.22.cloned.1.call-update) | async-done | bytes 42467344 | tf_op jit(solution)/shard_map/all_gather | solution.py:215
  988.1 20.2 multiply_reduce_fusion.5
  1012.8 22.1 fusion.132
  1034.9 9.6 copy.346
  1044.5 12.4 fusion.97
  1061.5 4.7 pad_maximum_fusion.2
  1066.5 35.1 %fusion.98 = f32[256,256,9]{0,1,2:T(8,128)} fusion(bf16[256,9,18432]{2,0,1:T(8,128)(2,1)} %all-gather.20.cloned.1.call-done, bf16[256,9216]{1,0:T(8,128)(2,1)} %copy-done.9, bf16[256,9216]{1,0:T(8,128)(2,1)} %copy-done.8), kind=kOutput, calls=%fused_computation.171 | convolution fusion | flops 21762146304 | bytes 96731136 | tf_op jit(solution)/shard_map/dot_general | solution.py:77
  1111.9 6.8 fusion.126
  1130.2 7.0 conditional.24
  1131.6 3.7 exponential_divide_fusion
  1138.6 6.4 fusion.103
  1148.2 3.6 conditional.30
  1155.0 16.1 conditional.28
  1174.4 6.6 copy.383
  1186.9 37.0 %all-gather.24.cloned.1.call-done = bf16[1024,9216]{1,0:T(8,128)(2,1)} async-done(((bf16[256,9216]{1,0:T(8,128)(2,1)}), bf16[1024,9216]{1,0:T(8,128)(2,1)}) %all-gather.24.cloned.1.call-update) | async-done | bytes 18874384 | tf_op jit(solution)/shard_map/all_gather | solution.py:232
  1224.0 24.7 copy.381
  1251.7 5.2 copy.382
  1256.9 7.2 reshape.434
  1264.1 18.7 all-gather.26.cloned.1.call-done
  1282.8 17.8 convolution_convert_fusion.1
  1300.6 18.8 reshape_reshape.14
  1319.4 298.6 %all-gather.30.cloned.1.call-done = bf16[1024,18432]{1,0:T(8,128)(2,1)} async-done(((bf16[256,18432]{1,0:T(8,128)(2,1)}), bf16[1024,18432]{1,0:T(8,128)(2,1)}) %all-gather.30.cloned.1.call-update) | async-done | bytes 37748752 | tf_op jit(solution)/shard_map/all_gather | solution.py:231
  1618.0 37.0 %convolution_convert_fusion = bf16[576,18432]{1,0:T(8,128)(2,1)} fusion(bf16[1024,576]{0,1:T(8,128)(2,1)S(1)} %reshape.436, bf16[1024,18432]{1,0:T(8,128)(2,1)} %all-gather.30.cloned.1.call-done), kind=kOutput, calls=%fused_computation.144 | convolution fusion | flops 21753888768 | bytes 60162048 | tf_op jit(solution)/shard_map/dot_general | solution.py:91
  1655.0 34.0 %reshape_reshape.15 = bf16[64,165888]{1,0:T(8,128)(2,1)} reshape(bf16[576,18432]{1,0:T(8,128)(2,1)} %convolution_convert_fusion) | data formatting | bytes 42467328 | tf_op jit(solution)/shard_map/reshape;reshape | solution.py:239
  1689.0 22.4 pad_maximum_fusion
  1713.0 8.2 fusion.148
  1727.3 4.0 add_convert_fusion
  1739.7 16.0 fusion.134
  1756.5 9.1 reduce-window.6
  1766.3 255.8 %reduce-scatter.15.cloned.1.call-done = bf16[8,248832]{1,0:T(8,128)(2,1)} async-done(((bf16[64,248832]{1,0:T(8,128)(2,1)}), bf16[8,248832]{1,0:T(8,128)(2,1)}) %reduce-scatter.15.cloned.1.call-update) | async-done | bytes 3981328 | tf_op jit(solution)/shard_map/reduce_scatter | solution.py:242
  2022.1 4.0 slice.145
  2026.3 205.6 %reduce-scatter.13.cloned.1.call-done = f32[8,8,2304]{2,0,1:T(8,128)} async-done(((f32[256,8,2304]{2,0,1:T(8,128)}), f32[8,8,2304]{2,0,1:T(8,128)}) %reduce-scatter.13.cloned.1.call-update) | async-done | bytes 589840 | tf_op jit(solution)/shard_map/reduce_scatter | solution.py:352
  2231.9 406.6 %reduce-scatter.11.cloned.1.call-done = f32[8,9,4096]{2,0,1:T(8,128)} async-done(((f32[256,9,4096]{2,0,1:T(8,128)}), f32[8,9,4096]{2,0,1:T(8,128)}) %reduce-scatter.11.cloned.1.call-update) | async-done | bytes 1179664 | tf_op jit(solution)/shard_map/reduce_scatter | solution.py:351
  2638.6 9.2 pad_maximum_fusion.1
  2647.7 4.2 broadcast_in_dim.142
  2652.0 140.0 %scatter_fusion = f32[1216,8,256]{2,1,0:T(8,128)} fusion(f32[1216,8,256]{2,1,0:T(8,128)} %broadcast_in_dim.142, s32[1188]{0:T(1024)S(1)} %compare_select_fusion, f32[1188,8,256]{2,1,0:T(8,128)} %pad_maximum_fusion.1), kind=kCustom, calls=%fused_computation | custom fusion | bytes 29201040 | tf_op jit(solution)/shard_map/scatter | solution.py:367
  2792.0 6.2 convert_element_type.184
  2798.2 4.2 all-to-all-start
  2804.2 11.1 fusion.119
  2820.7 113.0 %all-reduce.1 = f32[2304,4]{0,1:T(4,128)} all-reduce(f32[2304,4]{0,1:T(4,128)} %pad_maximum_fusion.5), channel_id=7, replica_groups=mesh['seq'=4,'dp'=8] {'seq','dp'}, use_global_device_ids=true, to_apply=%region_55.56.clone | all-reduce | flops 9216 | bytes 73728
  2937.1 3.8 fusion.124
  2941.9 3.7 multiply_reduce_fusion
  2945.6 25.3 fusion.85
  2970.9 24.1 fusion.84
  2995.0 21.3 fusion.87
  3016.3 19.0 multiply_subtract_fusion
  (303 shorter events, 156.9 us)
Async XLA Ops:
  7.2 46.5 %copy-start.1 = (bf16[1,256,2304]{2,1,0:T(8,128)(2,1)S(1)}, bf16[1,256,2304]{2,1,0:T(8,128)(2,1)}, u32[]{:S(2)}) copy-start(bf16[1,256,2304]{2,1,0:T(8,128)(2,1)} %param.47) | copy-start | bytes 3538948
  7.2 130.8 %all-gather.12.cloned.1.call-start = ((), (), s32[]{:S(2)}) async-start(), calls=%async_computation.6 | async-start | bytes 19464192 | tf_op jit(solution)/shard_map/all_gather | solution.py:141
  9.5 174.4 %all-gather.16.cloned.1.call-start = ((), (), s32[]{:S(2)}) async-start(), calls=%async_computation.8 | async-start | bytes 2621440 | tf_op jit(solution)/shard_map/all_gather | solution.py:155
  56.2 258.0 %copy-start.45 = (f32[2304]{0:T(1024)}, f32[2304]{0:T(1024)S(1)}, u32[]{:S(2)}) copy-start(f32[2304]{0:T(1024)S(1)} %get-tuple-element.950) | copy-start | bytes 27652
  57.1 80.9 %copy-start.68 = (f32[256]{0:T(256)}, f32[256]{0:T(256)S(1)}, u32[]{:S(2)}) copy-start(f32[256]{0:T(256)S(1)} %get-tuple-element.989) | copy-start | bytes 3076
  59.1 88.7 %copy-start.21 = (bf16[256,256,9]{0,1,2:T(8,128)(2,1)}, bf16[256,256,9]{0,1,2:T(8,128)(2,1)S(1)}, u32[]{:S(2)}) copy-start(bf16[256,256,9]{0,1,2:T(8,128)(2,1)S(1)} %fusion.129) | copy-start | bytes 3538948
  150.0 71.5 %all-gather.14.cloned.1.call-start = ((), (), s32[]{:S(2)}) async-start(), calls=%async_computation.7 | async-start | bytes 2621440 | tf_op jit(solution)/shard_map/all_gather | solution.py:156
  150.9 155.6 %all-gather.18.cloned.1.call-start = ((), (), s32[]{:S(2)}) async-start(), calls=%async_computation.9 | async-start | bytes 9732096 | tf_op jit(solution)/shard_map/all_gather | solution.py:142
  151.8 598.1 %all-gather.20.cloned.1.call-start = ((), (), s32[]{:S(2)}) async-start(), calls=%async_computation.10 | async-start | bytes 87588864 | tf_op jit(solution)/shard_map/all_gather | solution.py:210
  156.1 832.0 %all-gather.22.cloned.1.call-start = ((), (), s32[]{:S(2)}) async-start(), calls=%async_computation.11 | async-start | bytes 43794432 | tf_op jit(solution)/shard_map/all_gather | solution.py:215
  159.3 1015.1 %all-gather.28.cloned.1.call-start = ((), (), s32[]{:S(2)}) async-start(), calls=%async_computation.18 | async-start | bytes 5898240 | tf_op jit(solution)/shard_map/all_gather | solution.py:230
  160.1 30.2 copy-start.55
  196.0 4.5 copy-start.53
  196.0 5.1 copy-start.10
  196.0 5.1 copy-start.11
  196.0 5.3 copy-start.12
  196.0 5.9 copy-start.13
  317.5 906.4 %all-gather.24.cloned.1.call-start = ((), (), s32[]{:S(2)}) async-start(), calls=%async_computation.16 | async-start | bytes 23592960 | tf_op jit(solution)/shard_map/all_gather | solution.py:232
  799.8 483.0 %all-gather.26.cloned.1.call-start = ((), (), s32[]{:S(2)}) async-start(), calls=%async_computation.17 | async-start | bytes 5898240 | tf_op jit(solution)/shard_map/all_gather | solution.py:233
  799.8 210.0 %copy-start.64 = (f32[256]{0:T(256)}, f32[256]{0:T(256)S(1)}, u32[]{:S(2)}) copy-start(f32[256]{0:T(256)S(1)} %compare_convert_fusion) | copy-start | bytes 3076
  988.1 20.2 copy-start.23
  988.1 20.2 copy-start.51
  1012.4 605.6 %all-gather.30.cloned.1.call-start = ((), (), s32[]{:S(2)}) async-start(), calls=%async_computation.19 | async-start | bytes 47185920 | tf_op jit(solution)/shard_map/all_gather | solution.py:231
  1056.9 2.8 copy-start.8
  1056.9 4.6 copy-start.9
  1066.2 669.1 %reduce-scatter.9.cloned.1.call-start = ((), (), s32[]{:S(2)}) async-start(), calls=%async_computation.13 | async-start | bytes 2621440 | tf_op jit(solution)/shard_map/reduce_scatter | solution.py:329
  1101.5 3.1 copy-start.48
  1101.5 3.1 copy-start.63
  1104.6 3.1 copy-start.3
  1104.6 3.1 copy-start.5
  1104.6 3.1 copy-start.46
  1104.6 3.1 copy-start.65
  1104.6 3.1 copy-start.67
  1104.6 3.1 copy-start.70
  1107.7 3.6 copy-start.71
  1111.9 6.8 copy-start.33
  1111.9 6.8 copy-start
  1111.9 6.8 copy-start.39
  1111.9 6.8 copy-start.54
  1111.9 6.8 copy-start.56
  1111.9 6.8 copy-start.61
  1119.4 3.6 copy-start.15
  1123.8 3.2 copy-start.29
  1127.5 2.7 copy-start.30
  1138.6 6.4 copy-start.28
  1165.4 2.9 copy-start.43
  1174.3 563.4 %reduce-scatter.7.cloned.1.call-start = ((), (), s32[]{:S(2)}) async-start(), calls=%async_computation.12 | async-start | bytes 2621440 | tf_op jit(solution)/shard_map/reduce_scatter | solution.py:323
  1186.7 835.4 %reduce-scatter.15.cloned.1.call-start = ((), (), s32[]{:S(2)}) async-start(), calls=%async_computation.20 | async-start | bytes 35831808 | tf_op jit(solution)/shard_map/reduce_scatter | solution.py:242
  1711.4 520.5 %reduce-scatter.13.cloned.1.call-start = ((), (), s32[]{:S(2)}) async-start(), calls=%async_computation.15 | async-start | bytes 19464192 | tf_op jit(solution)/shard_map/reduce_scatter | solution.py:352
  1721.2 917.3 %reduce-scatter.11.cloned.1.call-start = ((), (), s32[]{:S(2)}) async-start(), calls=%async_computation.14 | async-start | bytes 38928384 | tf_op jit(solution)/shard_map/reduce_scatter | solution.py:351
  1735.3 20.4 copy-start.35
  2022.1 4.0 copy-start.20
  2026.3 621.4 %copy-start.24 = (f32[8,82944]{1,0:T(8,128)}, f32[8,82944]{1,0:T(8,128)S(1)}, u32[]{:S(2)}) copy-start(f32[8,82944]{1,0:T(8,128)S(1)} %slice.146) | copy-start | bytes 7962628
  2798.2 4.2 copy-start.57
  2798.2 4.8 copy-start.59
  2798.2 5.4 copy-start.58
  2798.2 6.0 copy-start.25
  2798.2 6.0 copy-start.36
  2798.2 6.0 copy-start.69
  2798.2 143.7 %all-to-all-start = ((bf16[1216,8,256]{2,1,0:T(8,128)(2,1)}), bf16[1216,8,256]{2,1,0:T(8,128)(2,1)}, u32[]{:S(2)}, u32[]{:S(2)}) async-start(bf16[1216,8,256]{2,1,0:T(8,128)(2,1)} %convert_element_type.184), calls=%async_computation.5 | async-start | bytes 9961472 | tf_op jit(solution)/shard_map/all_to_all | solution.py:368
  2815.3 119.7 %copy-start.2 = (bf16[1,256,2304]{2,1,0:T(8,128)(2,1)S(1)}, bf16[1,256,2304]{2,1,0:T(8,128)(2,1)}, u32[]{:S(2)}) copy-start(bf16[1,256,2304]{2,1,0:T(8,128)(2,1)} %param.47) | copy-start | bytes 3538948
  2815.3 119.7 %copy-start.50 = (f32[2304]{0:T(1024)S(1)}, f32[2304]{0:T(1024)}, u32[]{:S(2)}) copy-start(f32[2304]{0:T(1024)} %copy-done.49) | copy-start | bytes 27652
  2818.4 118.7 %copy-start.7 = (f32[256,2304]{1,0:T(8,128)S(1)}, f32[256,2304]{1,0:T(8,128)}, u32[]{:S(2)}) copy-start(f32[256,2304]{1,0:T(8,128)} %copy-done.6) | copy-start | bytes 7077892
  2937.1 3.8 copy-start.37
  (23 other events, 32.7 us)
Sparse Core Ops, SparseCore 0:
  11.6 126.3 all-gather.11
  150.2 33.6 all-gather.15
  186.3 35.1 all-gather.13
  225.0 81.5 all-gather.17
  310.2 439.6 all-gather.19
  752.9 235.1 all-gather.21
  990.6 55.0 all-gather.27
  1048.1 175.7 all-gather.23
  1225.8 56.9 all-gather.25
  1285.1 332.8 all-gather.29
  1621.0 35.1 reduce-scatter.8
  1659.0 35.1 reduce-scatter.6
  1711.6 310.4 reduce-scatter.14
  2028.4 203.5 reduce-scatter.12
  2234.6 403.8 reduce-scatter.10
where the time goes:
time: 3060 us; the launch traced here: 3040 us
  waiting for transfers between devices  2020 us (66%)
  local copies, waits for them, and re-layouts  357 us (12%)
  matrix products  337 us (11%)
  blocking collectives  157 us (5%)
  other arithmetic  147 us (5%)
    all_gather x1, waiting for transfers between devices, body(): lax.all_gather(geglu_low, ('seq', 'dp'), axis=0, tiled=True)  430 us
    reduce_scatter x1, waiting for transfers between devices, body(): lax.psum_scatter(qkv_term, ('seq', 'dp'), scatter_dimension=0, tiled=True)  407 us
    all_gather x1, waiting for transfers between devices, body(): lax.all_gather(gate_up_low, 'seq', axis=0, tiled=True)  299 us
    reduce_scatter x1, waiting for transfers between devices, body(): lax.psum_scatter(jnp.concatenate([down_part, geglu_part], axis=1).astype(...  256 us
    reduce_scatter x1, waiting for transfers between devices, body(): lax.psum_scatter(out_term, ('seq', 'dp'), scatter_dimension=0, tiled=True)  206 us
    all_gather x1, waiting for transfers between devices, body(): lax.all_gather(down_low, ('seq', 'dp'), axis=0, tiled=True)  182 us
    scatter x1, local copies, waits for them, and re-layouts, body(): jnp.zeros((devices * capacity, share, BLK), jnp.float32).at[slots]  140 us
    unnamed x1, blocking collectives  113 us
  transfers between devices with their start and end apart: 16, of which 12 were waited for; matrix products, arithmetic and copies ran while one was open for 18% of the time, Pallas kernels for 0%

commit v1 on v0

v1 whole, which is shorter than its diff:
```python
import functools

import jax
import jax.numpy as jnp
from jax import lax
from jax.experimental import pallas as pl
from jax.experimental.pallas import tpu as pltpu
from jax.sharding import PartitionSpec as P

D = 2304
QUERY_HEADS = 8
KV_HEAD_COUNT = 4
HEAD_SIZE = 256
FF = 9216
BLK = 256
QUERY_FEATURES = 2048
KEY_FEATURES = 1024


EPSILON = 1e-06
SOFT_CAP = 50.0
NEGATIVE = -1e30
BETA_ONE = 0.9
BETA_TWO = 0.95
STEP_RATE = 0.05
TINY_ADD = 1e-08
CLIP_NORM = 1.0

F32 = jnp.float32
BF16 = jnp.bfloat16
ALL = ("seq", "dp")


def norm_forward(value_rows, gain):
    inverse = lax.rsqrt(jnp.mean(value_rows * value_rows, axis=-1, keepdims=True) + EPSILON)
    return (value_rows * inverse * gain, inverse)


def norm_backward(value_rows, inverse, gain, upstream):
    weighted = upstream * gain
    cubed = inverse * inverse * inverse
    grad_in = inverse * weighted - value_rows * cubed * jnp.mean(
        value_rows * weighted, axis=-1, keepdims=True
    )
    return (grad_in, jnp.sum(upstream * value_rows * inverse, axis=0))


def dot(left, right):
    return jnp.dot(left, right, preferred_element_type=F32)


def dot_nt(left, right):
    return lax.dot_general(left, right, (((1,), (1,)), ((), ())), preferred_element_type=F32)


def dot_tn(left, right):
    return lax.dot_general(left, right, (((0,), (0,)), ((), ())), preferred_element_type=F32)


def block_probs(query, keys, row_start, length, prefix):
    raw = dot_nt(query, keys)
    bent = jnp.tanh(raw * (HEAD_SIZE ** (-0.5) / SOFT_CAP))
    key_pos = lax.broadcasted_iota(jnp.int32, raw.shape, 1)
    query_pos = row_start + lax.broadcasted_iota(jnp.int32, raw.shape, 0)
    visible = (key_pos < length) & ((key_pos <= query_pos) | (key_pos < prefix))
    capped = jnp.where(visible, SOFT_CAP * bent, NEGATIVE)
    exponent = jnp.exp(capped - jnp.max(capped, axis=-1, keepdims=True))
    prob = exponent / jnp.sum(exponent, axis=-1, keepdims=True)
    return (prob, bent)


def attention_forward_kernel(heads, length_ref, prefix_ref, merged_ref, mixed_ref):
    length, prefix = length_ref[0], prefix_ref[0]
    key_col, value_col = heads * HEAD_SIZE, (heads + 1) * HEAD_SIZE
    tokens = merged_ref.shape[0]
    for head in range(heads):
        for start in range(0, tokens, BLK):
            rows, width = slice(start, start + BLK), start + BLK
            head_cols = slice(head * HEAD_SIZE, (head + 1) * HEAD_SIZE)
            keys = merged_ref[:width, key_col : key_col + HEAD_SIZE]
            values = merged_ref[:width, value_col : value_col + HEAD_SIZE]
            prob, _ = block_probs(merged_ref[rows, head_cols], keys, start, length, prefix)
            mixed_ref[rows, head_cols] = dot(prob.astype(BF16), values).astype(BF16)


def attention_backward_kernel(
    heads, length_ref, prefix_ref, merged_ref, upstream_ref, grad_ref, keys_acc, values_acc
):
    length, prefix = length_ref[0], prefix_ref[0]
    key_col, value_col = heads * HEAD_SIZE, (heads + 1) * HEAD_SIZE
    tokens = merged_ref.shape[0]
    keys_acc[...] = jnp.zeros_like(keys_acc)
    values_acc[...] = jnp.zeros_like(values_acc)
    for head in range(heads):
        for start in range(0, tokens, BLK):
            rows, width = slice(start, start + BLK), start + BLK
            head_cols = slice(head * HEAD_SIZE, (head + 1) * HEAD_SIZE)
            query = merged_ref[rows, head_cols]
            keys = merged_ref[:width, key_col : key_col + HEAD_SIZE]
            values = merged_ref[:width, value_col : value_col + HEAD_SIZE]
            upstream = upstream_ref[rows, head_cols]
            prob, bent = block_probs(query, keys, start, length, prefix)
            grad_prob = dot_nt(upstream, values)
            balance = jnp.sum(prob * grad_prob, axis=-1, keepdims=True)
            grad_raw = (
                prob * (grad_prob - balance) * (1.0 - bent * bent) * HEAD_SIZE ** (-0.5)
            ).astype(BF16)
            grad_ref[rows, head_cols] = dot(grad_raw, keys).astype(BF16)
            keys_acc[:width, :] += dot_tn(grad_raw, query)
            values_acc[:width, :] += dot_tn(prob.astype(BF16), upstream)
    grad_ref[:, key_col : key_col + HEAD_SIZE] = keys_acc[...].astype(BF16)
    grad_ref[:, value_col : value_col + HEAD_SIZE] = values_acc[...].astype(BF16)


SMEM_SPEC = pl.BlockSpec(memory_space=pltpu.SMEM)
VMEM_SPEC = pl.BlockSpec(memory_space=pltpu.VMEM)


def attention_forward(merged, length, prefix, heads):
    tokens = merged.shape[0]
    flops = 4 * heads * tokens * tokens * HEAD_SIZE
    return pl.pallas_call(
        functools.partial(attention_forward_kernel, heads),
        out_shape=jax.ShapeDtypeStruct((tokens, heads * HEAD_SIZE), BF16),
        in_specs=[SMEM_SPEC, SMEM_SPEC, VMEM_SPEC],
        out_specs=VMEM_SPEC,
        compiler_params=pltpu.CompilerParams(vmem_limit_bytes=40 << 20),
        cost_estimate=pl.CostEstimate(
            flops=flops, bytes_accessed=4 << 20, transcendentals=2 * heads * tokens * tokens
        ),
    )(length, prefix, merged)


def attention_backward(merged, upstream, length, prefix, heads):
    tokens = merged.shape[0]
    flops = 10 * heads * tokens * tokens * HEAD_SIZE
    return pl.pallas_call(
        functools.partial(attention_backward_kernel, heads),
        out_shape=jax.ShapeDtypeStruct(merged.shape, BF16),
        in_specs=[SMEM_SPEC, SMEM_SPEC, VMEM_SPEC, VMEM_SPEC],
        out_specs=VMEM_SPEC,
        scratch_shapes=[pltpu.VMEM((tokens, HEAD_SIZE), F32), pltpu.VMEM((tokens, HEAD_SIZE), F32)],
        compiler_params=pltpu.CompilerParams(vmem_limit_bytes=48 << 20),
        cost_estimate=pl.CostEstimate(
            flops=flops, bytes_accessed=6 << 20, transcendentals=2 * heads * tokens * tokens
        ),
    )(length, prefix, merged, upstream)


def place_kernel(layout, devices, stride, slots_ref, *refs):
    pieces, extra, out = refs[: len(layout)], refs[len(layout)], refs[len(layout) + 1]
    out[...] = jnp.zeros_like(out)

    @pl.loop(0, devices)
    def _(at):
        out[at * stride + stride - 1] = extra[at]

    seq_index = slots_ref[slots_ref.shape[0] - 1]
    for piece, (turn, base, per_row, columns) in zip(pieces, layout):
        source = jnp.bitwise_xor(seq_index, turn)

        @pl.loop(0, piece.shape[0])
        def _(a, piece=piece, base=base, per_row=per_row, columns=columns, source=source):
            for local, (fixed, factor, row_factor) in enumerate(columns):
                block = base + (a + source * row_factor) * per_row + fixed + source * factor
                out[slots_ref[block]] = piece[a, :, local * BLK : (local + 1) * BLK]


def place_pieces(pieces, extra, slots, seq_index, layout, devices, stride):
    share = extra.shape[1]
    table = jnp.concatenate([slots, seq_index[None]]).astype(jnp.int32)
    return pl.pallas_call(
        functools.partial(place_kernel, layout, devices, stride),
        out_shape=jax.ShapeDtypeStruct((devices * stride, share, BLK), BF16),
        in_specs=[SMEM_SPEC] + [VMEM_SPEC] * (len(pieces) + 1),
        out_specs=VMEM_SPEC,
        compiler_params=pltpu.CompilerParams(vmem_limit_bytes=48 << 20),
        cost_estimate=pl.CostEstimate(flops=0, bytes_accessed=12 << 20, transcendentals=0),
    )(table, *pieces, extra)


def soap_kernel(
    group, incoming, first, second, left, right, master, first_out, second_out, weight_out
):
    for at in range(group):
        if len(incoming.shape) == 4:
            grad = incoming[:, at].astype(F32).reshape(BLK, BLK)
        else:
            grad = incoming[at].astype(F32)
        size = jnp.sqrt(jnp.sum(grad * grad))
        scale = CLIP_NORM / jnp.maximum(size, CLIP_NORM)
        left_low = left[at].astype(BF16)
        right_low = right[at].astype(BF16)
        turned = dot_tn(left_low, grad.astype(BF16)).astype(BF16)
        rotated = dot(turned, right_low) * scale
        first_new = BETA_ONE * first[at] + (1.0 - BETA_ONE) * rotated
        second_new = BETA_TWO * second[at] + (1.0 - BETA_TWO) * rotated * rotated
        first_out[at] = first_new
        second_out[at] = second_new
        direction = (first_new / (jnp.sqrt(second_new) + TINY_ADD)).astype(BF16)
        back_left = dot(left_low, direction).astype(BF16)
        weight_out[at] = master[at] - STEP_RATE * dot_nt(back_left, right_low)


def soap(incoming, first, second, left, right, master):
    capacity = first.shape[0]
    group = 2 if capacity % 2 == 0 else 1
    spec = pl.BlockSpec((group, BLK, BLK), lambda at: (at, 0, 0))
    if incoming.ndim == 4:
        grad_spec = pl.BlockSpec(
            (incoming.shape[0], group) + incoming.shape[2:], lambda at: (0, at, 0, 0)
        )
    else:
        grad_spec = spec
    shape = jax.ShapeDtypeStruct(first.shape, F32)
    return pl.pallas_call(
        functools.partial(soap_kernel, group),
        grid=(capacity // group,),
        out_shape=(shape, shape, shape),
        in_specs=[grad_spec] + [spec] * 5,
        out_specs=(spec, spec, spec),
        compiler_params=pltpu.CompilerParams(vmem_limit_bytes=48 << 20),
        cost_estimate=pl.CostEstimate(
            flops=8 * capacity * BLK**3,
            bytes_accessed=34 * capacity * BLK * BLK,
            transcendentals=2 * capacity * BLK * BLK,
        ),
    )(incoming, first, second, left, right, master)


def body(
    tokens,
    cotangent,
    qkv_weight,
    out_weight,
    geglu_weight,
    down_weight,
    norm_gains,
    seq_lengths,
    prefix_lengths,
    block_owners,
    first_moment,
    second_moment,
    left_basis,
    right_basis,
    slot_weight,
):
    inputs = tokens[0].astype(F32)
    upstream = cotangent[0].astype(F32)
    rows = inputs.shape[0]
    seq_count = lax.axis_size("seq")
    dp_count = lax.axis_size("dp")
    seq_index = lax.axis_index("seq")
    share = qkv_weight.shape[0]
    total_rows = rows * seq_count
    heads = QUERY_HEADS // seq_count
    query_slice = heads * HEAD_SIZE
    key_slice = KEY_FEATURES // seq_count
    ff_slice = FF // seq_count
    d_groups = D // BLK
    half = ff_slice // 2

    def swap(value, turn):
        return lax.ppermute(value, "seq", [(at, at ^ turn) for at in range(seq_count)])

    def owner_of(turn):
        return jnp.bitwise_xor(seq_index, turn)

    def pick(value, index, size, axis):
        return lax.dynamic_slice_in_dim(value, index * size, size, axis)

    def assemble(items):
        size = items[0].shape[0]
        buffer = jnp.zeros((size * seq_count,) + items[0].shape[1:], items[0].dtype)
        for turn, item in enumerate(items):
            start = (owner_of(turn) * size,) + (0,) * (item.ndim - 1)
            buffer = lax.dynamic_update_slice(buffer, item, start)
        return buffer

    def gather_rows(value):
        received = {turn: swap(value, turn) for turn in range(seq_count - 1, 0, -1)}
        return assemble([value] + [received[turn] for turn in range(1, seq_count)])

    def scatter_rows(part_of):
        received = []
        for turn in range(seq_count - 1, 0, -1):
            received.append(swap(part_of(owner_of(turn)).astype(BF16), turn))
        result = part_of(seq_index)
        for value in received:
            result = result + value.astype(F32)
        return result

    def spread(piece_for):
        received = [piece_for(seq_index)]
        for turn in range(1, seq_count):
            received.append(swap(piece_for(owner_of(turn)), turn))
        return lax.all_gather(assemble(received), "dp", axis=0, tiled=True)

    def collect(gradient):
        summed = lax.psum_scatter(gradient.astype(BF16), "dp", scatter_dimension=0, tiled=True)
        size = summed.shape[0] // seq_count
        result = [pick(summed, seq_index, size, 0)]
        for turn in range(1, seq_count):
            result.append(swap(pick(summed, owner_of(turn), size, 0), turn))
        return result

    def row_order(groups):
        at = jnp.arange(groups * BLK, dtype=jnp.int32)
        inner = at % share
        group = (at // share) % groups
        device = at // (share * groups)
        natural = share * (dp_count * (device % seq_count) + device // seq_count) + inner
        return group * BLK + natural

    def order_matrix(groups):
        return (jnp.arange(groups * BLK, dtype=jnp.int32)[:, None] == row_order(groups)[None, :]).astype(BF16)

    wide_order = order_matrix(d_groups)
    head_order = order_matrix(heads)

    def local_rows(weight):
        return jnp.transpose(weight.astype(BF16), (1, 0, 2))

    qkv_low = local_rows(qkv_weight).reshape(d_groups * share, -1)
    out_low = local_rows(out_weight)
    down_low = local_rows(down_weight)
    gain_full = lax.all_gather(norm_gains.astype(BF16), ALL, axis=0, tiled=True)

    def qkv_piece(target):
        return jnp.concatenate(
            [
                pick(qkv_low[:, :QUERY_FEATURES], target, query_slice, 1),
                pick(qkv_low[:, QUERY_FEATURES : QUERY_FEATURES + KEY_FEATURES], target, key_slice, 1),
                pick(qkv_low[:, QUERY_FEATURES + KEY_FEATURES :], target, key_slice, 1),
            ],
            axis=1,
        )

    def out_piece(target):
        return pick(out_low, target, heads, 0).reshape(heads * share, D)

    def down_piece(target):
        return pick(down_low, target, d_groups, 0).reshape(d_groups * share, D)

    qkv_slice_full = spread(qkv_piece)
    out_slice_full = spread(out_piece)

    geglu_rows = jnp.transpose(
        geglu_weight.astype(BF16).reshape(share, d_groups, 2 * seq_count, ff_slice), (2, 1, 0, 3)
    ).reshape(2 * seq_count * d_groups * share, ff_slice)
    geglu_turned = dot(geglu_rows, wide_order).astype(BF16).reshape(
        2 * seq_count, d_groups * share, ff_slice
    )

    def geglu_piece(part):
        cols = slice(part * half, (part + 1) * half)

        def piece(target):
            return jnp.concatenate(
                [
                    lax.dynamic_index_in_dim(geglu_turned, target, 0, False)[:, cols],
                    lax.dynamic_index_in_dim(geglu_turned, target + seq_count, 0, False)[:, cols],
                ],
                axis=1,
            )

        return piece

    geglu_zero = spread(geglu_piece(0))
    down_full = spread(down_piece)
    geglu_one = spread(geglu_piece(1))
    geglu_parts = (geglu_zero, geglu_one)

    gains = gain_full.astype(F32)
    normed, inverse_one = norm_forward(inputs, gains[:, 0])
    normed_turned = dot(normed.astype(BF16), wide_order).astype(BF16)
    normed_all = gather_rows(normed_turned)
    merged = dot(normed_all, qkv_slice_full).astype(BF16)
    mixed = attention_forward(merged, seq_lengths, prefix_lengths, heads)
    mixed_turned = dot(mixed, head_order).astype(BF16)
    attended = scatter_rows(lambda owner: dot(pick(mixed_turned, owner, rows, 0), out_slice_full))
    attn_normed, inverse_two = norm_forward(attended, gains[:, 1])
    hidden = inputs + attn_normed
    ffn_normed, inverse_three = norm_forward(hidden, gains[:, 2])
    ffn_turned = dot(ffn_normed.astype(BF16), wide_order).astype(BF16)
    ffn_all = gather_rows(ffn_turned)

    gates, uppers, products = [], [], []
    for part in range(2):
        gate_up = dot(ffn_all, geglu_parts[part])
        gate, upper = gate_up[:, :half], gate_up[:, half:]
        gates.append(gate)
        uppers.append(upper)
        products.append((jax.nn.gelu(gate, approximate=True) * upper).astype(BF16))

    branch_zero = dot(products[0], down_full[:half])

    def branch_part(owner):
        return pick(branch_zero, owner, rows, 0) + dot(
            pick(products[1], owner, rows, 0), down_full[half:]
        )

    branch = scatter_rows(branch_part)
    branch_normed, inverse_four = norm_forward(branch, gains[:, 3])
    query_pos = seq_index * rows + jnp.arange(rows, dtype=jnp.int32)
    live_rows = (query_pos < seq_lengths[0]).astype(F32)[:, None]
    layer_out = ((hidden + branch_normed) * live_rows).astype(BF16)
    row_rms = jnp.sqrt(jnp.mean(inputs * inputs, axis=-1) + EPSILON)

    upstream = upstream * live_rows
    grad_branch, gain_four = norm_backward(branch, inverse_four, gains[:, 3], upstream)
    branch_all = gather_rows(grad_branch.astype(BF16))
    down_sums = collect(
        jnp.concatenate([dot_tn(products[0], branch_all), dot_tn(products[1], branch_all)], axis=0)
    )
    gate_up_grads = []
    geglu_sums = []
    for part in range(2):
        grad_product = dot_nt(branch_all, down_full[part * half : (part + 1) * half])
        activated, gelu_pull = jax.vjp(lambda value: jax.nn.gelu(value, approximate=True), gates[part])
        grad_gate = gelu_pull(grad_product * uppers[part])[0]
        grad_upper = grad_product * activated
        gate_up_grad = jnp.concatenate([grad_gate, grad_upper], axis=1).astype(BF16)
        gate_up_grads.append(gate_up_grad)
        geglu_sums.append(collect(dot_tn(ffn_all, gate_up_grad)))

    def ffn_part(owner):
        return dot_nt(pick(gate_up_grads[0], owner, rows, 0), geglu_zero) + dot_nt(
            pick(gate_up_grads[1], owner, rows, 0), geglu_one
        )

    grad_ffn = dot_nt(scatter_rows(ffn_part).astype(BF16), wide_order)
    grad_hidden_norm, gain_three = norm_backward(hidden, inverse_three, gains[:, 2], grad_ffn)
    grad_hidden = upstream + grad_hidden_norm
    grad_attended, gain_two = norm_backward(attended, inverse_two, gains[:, 1], grad_hidden)
    attended_all = gather_rows(grad_attended.astype(BF16))
    grad_mixed_turned = dot_nt(attended_all, out_slice_full).astype(BF16)
    grad_mixed = dot_nt(grad_mixed_turned, head_order).astype(BF16)
    out_sums = collect(dot_tn(mixed_turned, attended_all))
    grad_merged = attention_backward(merged, grad_mixed, seq_lengths, prefix_lengths, heads)
    qkv_sums = collect(dot_tn(normed_all, grad_merged))
    grad_normed = dot_nt(
        scatter_rows(lambda owner: dot_nt(pick(grad_merged, owner, rows, 0), qkv_slice_full)).astype(BF16),
        wide_order,
    )
    grad_input_norm, gain_one = norm_backward(inputs, inverse_one, gains[:, 0], grad_normed)
    token_grad = grad_hidden + grad_input_norm

    turned = jnp.concatenate(
        [
            jnp.concatenate(
                [geglu_sums[0][turn][:, side * half : (side + 1) * half],
                 geglu_sums[1][turn][:, side * half : (side + 1) * half]],
                axis=1,
            )
            for turn in range(seq_count)
            for side in range(2)
        ],
        axis=0,
    )
    geglu_natural = dot_nt(turned, wide_order).astype(BF16).reshape(
        seq_count, 2, d_groups, share, ff_slice
    )
    qkv_local = [value.reshape(d_groups, share, -1) for value in qkv_sums]
    out_local = [value.reshape(heads, share, D) for value in out_sums]
    down_local = [value.reshape(d_groups, share, D) for value in down_sums]

    def in_order(items):
        return assemble([item[None] for item in items])

    qkv_slices = in_order(qkv_local)
    out_grad = jnp.transpose(
        in_order(out_local).reshape(QUERY_FEATURES // BLK, share, D), (1, 0, 2)
    ).astype(F32)
    down_grad = jnp.transpose(in_order(down_local).reshape(FF // BLK, share, D), (1, 0, 2)).astype(F32)

    def columns(value):
        return jnp.transpose(value, (2, 1, 0, 3)).reshape(share, d_groups, -1)

    qkv_grad = jnp.concatenate(
        [
            columns(qkv_slices[..., :query_slice]),
            columns(qkv_slices[..., query_slice : query_slice + key_slice]),
            columns(qkv_slices[..., query_slice + key_slice :]),
        ],
        axis=-1,
    ).astype(F32)
    geglu_slices = in_order([geglu_natural[turn] for turn in range(seq_count)])
    geglu_grad = jnp.transpose(geglu_slices, (3, 2, 1, 0, 4)).reshape(share, d_groups, 2 * FF).astype(F32)

    devices = lax.axis_size(ALL)
    capacity = first_moment.shape[0]
    stride = capacity + 1
    number = jnp.arange(block_owners.shape[0], dtype=jnp.int32)
    same = (block_owners[:, None] == block_owners[None, :]) & (number[None, :] < number[:, None])
    slots = block_owners * stride + jnp.sum(same.astype(jnp.int32), axis=1)

    gain_term = jnp.stack([gain_one, gain_two, gain_three, gain_four], axis=1)
    gain_share = D // devices
    gain_flat = gain_term.reshape(devices, gain_share * 4)
    gain_high = gain_flat.astype(BF16)
    gain_low = (gain_flat - gain_high.astype(F32)).astype(BF16)
    room = share * BLK
    gain_pair = jnp.concatenate([gain_high, gain_low], axis=1)
    extra = jnp.pad(gain_pair, ((0, 0), (0, room - gain_pair.shape[1]))).reshape(devices, share, BLK)

    ff_blocks = ff_slice // BLK
    out_base = d_groups * (QUERY_FEATURES + 2 * KEY_FEATURES) // BLK
    geglu_base = out_base + (QUERY_FEATURES // BLK) * (D // BLK)
    down_base = geglu_base + d_groups * 2 * FF // BLK
    if share % 8 == 0:
        pieces, layout = [], []
        query_blocks, key_blocks = query_slice // BLK, key_slice // BLK
        for turn in range(seq_count):
            qkv_columns = [(at, query_blocks, 0) for at in range(query_blocks)]
            for begin in (QUERY_FEATURES, QUERY_FEATURES + KEY_FEATURES):
                qkv_columns += [(begin // BLK + at, key_blocks, 0) for at in range(key_blocks)]
            pieces.append(qkv_local[turn])
            layout.append((turn, 0, (QUERY_FEATURES + 2 * KEY_FEATURES) // BLK, qkv_columns))
            pieces.append(out_local[turn])
            layout.append((turn, out_base, D // BLK, [(at, 0, heads) for at in range(D // BLK)]))
            for side in range(2):
                pieces.append(geglu_natural[turn, side])
                layout.append(
                    (
                        turn,
                        geglu_base,
                        2 * FF // BLK,
                        [(side * FF // BLK + at, ff_blocks, 0) for at in range(ff_blocks)],
                    )
                )
            pieces.append(down_local[turn])
            layout.append((turn, down_base, D // BLK, [(at, 0, d_groups) for at in range(D // BLK)]))
        outgoing = place_pieces(pieces, extra, slots, seq_index, layout, devices, stride)
    else:

        def to_pieces(gradient):
            count_of_rows, groups, col_count = gradient.shape
            shaped = gradient.astype(BF16).reshape(count_of_rows, groups, col_count // BLK, BLK)
            return jnp.transpose(shaped, (1, 2, 0, 3)).reshape(-1, count_of_rows, BLK)

        every = jnp.concatenate(
            [to_pieces(qkv_grad), to_pieces(out_grad), to_pieces(geglu_grad), to_pieces(down_grad)],
            axis=0,
        )
        outgoing = jnp.zeros((devices * stride, share, BLK), BF16).at[slots].set(every)
        outgoing = outgoing.at[jnp.arange(devices) * stride + capacity].set(extra)

    incoming = lax.all_to_all(outgoing, ALL, split_axis=0, concat_axis=0, tiled=True).reshape(
        devices, stride, share, BLK
    )
    gain_parts = incoming[:, capacity].reshape(devices, room)[:, : 2 * gain_share * 4].astype(F32)
    gain_sums = jnp.sum(gain_parts, axis=0)
    gains_grad = (gain_sums[: gain_share * 4] + gain_sums[gain_share * 4 :]).reshape(gain_share, 4)
    if share % 8 == 0:
        grads = incoming
    else:
        grads = jnp.transpose(incoming[:, :capacity], (1, 0, 2, 3)).reshape(capacity, BLK, BLK)
    first_new, second_new, weight_new = soap(
        grads, first_moment, second_moment, left_basis, right_basis, slot_weight
    )
    return (
        layer_out[None],
        row_rms[None],
        token_grad[None],
        qkv_grad,
        out_grad,
        geglu_grad,
        down_grad,
        gains_grad,
        first_new,
        second_new,
        weight_new,
    )


def solution(mesh):
    in_specs = (
        P("dp", "seq", None),
        P("dp", "seq", None),
        P(ALL, None, None),
        P(ALL, None, None),
        P(ALL, None, None),
        P(ALL, None, None),
        P(ALL, None),
        P("dp"),
        P("dp"),
        P(),
        P(ALL, None, None),
        P(ALL, None, None),
        P(ALL, None, None),
        P(ALL, None, None),
        P(ALL, None, None),
    )
    out_specs = (
        P("dp", "seq", None),
        P("dp", "seq"),
        P("dp", "seq", None),
        P(ALL, None, None),
        P(ALL, None, None),
        P(ALL, None, None),
        P(ALL, None, None),
        P(ALL, None),
        P(ALL, None, None),
        P(ALL, None, None),
        P(ALL, None, None),
    )
    return jax.shard_map(body, mesh=mesh, in_specs=in_specs, out_specs=out_specs, check_vma=False)
```

time: 3060 us -> 1400 us (0.46)
  waiting for transfers between devices: 2020 us -> 812 us
  local copies, waits for them, and re-layouts: 357 us -> 58.3 us
  blocking collectives: 157 us -> 41.9 us
  other arithmetic: 147 us -> 50.5 us
  starting transfers between devices: 5.74 us -> 77.3 us
  matrix products: 337 us -> 283 us
  Pallas kernels: 0 us -> 50.6 us
    all_gather x10 -> x5, waiting for transfers between devices: 1150 us -> 39.6 us  [spread(): return lax.all_gather(assemble(received), 'dp', axis=0, tiled=True)]
    reduce_scatter x5, waiting for transfers between devices: 868 us -> 242 us  [collect(): lax.psum_scatter(gradient.astype(BF16), 'dp', scatter_dimension=0, tiled=...]
    ppermute x0 -> x54, waiting for transfers between devices: none -> 426 us  [swap(): lax.ppermute(value, 'seq', [(at, at ^ turn) for at in range(seq_count)])]
    scatter x1 -> x0, local copies, waits for them, and re-layouts: 140 us -> none  [body(): jnp.zeros((devices * capacity, share, BLK), jnp.float32).at[slots]]
    unnamed x1 -> x0, blocking collectives: 113 us -> none
    all_to_all x1, waiting for transfers between devices: 0.01 us -> 104 us  [body(): lax.all_to_all(outgoing, ALL, split_axis=0, concat_axis=0, tiled=True)]
    another operation x18 -> x7, local copies, waits for them, and re-layouts: 74.9 us -> 5.87 us  [the longest x1 34 us: body(): weight_term(ffn_rows, gate_rows, group_base, count)]
    ppermute x0 -> x54, starting transfers between devices: none -> 68.4 us  [swap(): lax.ppermute(value, 'seq', [(at, at ^ turn) for at in range(seq_count)])]
  transfers between devices with their start and end apart: 16 -> 65, of which waited for: 12 -> 37; matrix products, arithmetic and copies ran while one was open for 18% -> 20% of each run, Pallas kernels for 0% -> 1%
where the time goes in v1:
time: 1400 us; the launch traced here: 1390 us
  waiting for transfers between devices  812 us (58%)
  matrix products  283 us (20%)
  starting transfers between devices  77.3 us (6%)
  local copies, waits for them, and re-layouts  58.3 us (4%)
  Pallas kernels  50.6 us (4%)
  other arithmetic  50.5 us (4%)
  blocking collectives  41.9 us (3%)
  between operations  17.5 us (1%)
    ppermute x54, waiting for transfers between devices, swap(): lax.ppermute(value, 'seq', [(at, at ^ turn) for at in range(seq_count)])  426 us
    reduce_scatter x5, waiting for transfers between devices, collect(): lax.psum_scatter(gradient.astype(BF16), 'dp', scatter_dimension=0, tiled=...  242 us
    dot_general x16, matrix products, dot_nt(): lax.dot_general(left, right, (((1,), (1,)), ((), ())), preferred_element_...  138 us
    all_to_all x1, waiting for transfers between devices, body(): lax.all_to_all(outgoing, ALL, split_axis=0, concat_axis=0, tiled=True)  104 us
    dot_general x16, matrix products, dot(): return jnp.dot(left, right, preferred_element_type=F32)  80.8 us
    ppermute x54, starting transfers between devices, swap(): lax.ppermute(value, 'seq', [(at, at ^ turn) for at in range(seq_count)])  68.4 us
    dot_general x6, matrix products, dot_tn(): lax.dot_general(left, right, (((0,), (0,)), ((), ())), preferred_element_...  64.6 us
    all_gather x1, blocking collectives, body(): gain_full = lax.all_gather(norm_gains.astype(BF16), ALL, axis=0, tiled=True)  41.9 us
  transfers between devices with their start and end apart: 65, of which 37 were waited for; matrix products, arithmetic and copies ran while one was open for 20% of the time, Pallas kernels for 1%

profile of v1, /device:TPU:0, one launch (start us, length us, event | category | flops | bytes accessed | tf_op | source)
XLA Modules:
  0.0 1391.8 jit_solution(13344279579472586295)
XLA Ops:
  16.1 4.3 collective-permute-done.4
  29.6 8.7 fusion.31
  43.6 6.7 collective-permute-done.15
  50.3 5.3 collective-permute-done.16
  60.6 6.4 collective-permute-done.21
  77.5 41.9 %all-gather = bf16[32,72,4]{1,2,0:T(4,128)(2,1)S(1)} all-gather(bf16[1,72,4]{1,2,0:T(4,128)(2,1)S(1)} %convert_bitcast_fusion.2), channel_id=1, replica_groups=mesh['seq'=4,'dp'=8] {'seq','dp'}, dimensions={0}, use_global_device_ids=true | all-gather | bytes 19008 | tf_op jit(solution)/shard_map/all_gather | solution.py:327
  129.4 5.5 constant_dynamic-update-slice_fusion.30
  139.8 24.0 %collective-permute-done = bf16[256,2304]{1,0:T(8,128)(2,1)S(1)} collective-permute-done((bf16[256,2304]{1,0:T(8,128)(2,1)S(1)}, bf16[256,2304]{1,0:T(8,128)(2,1)S(1)}, u32[]{:S(2)}, u32[]{:S(2)}) %collective-permute-start) | collective-permute-done | bytes 1179680 | tf_op jit(solution)/shard_map/ppermute | solution.py:264
  166.0 23.3 %collective-permute-done.2 = bf16[256,2304]{1,0:T(8,128)(2,1)S(1)} collective-permute-done((bf16[256,2304]{1,0:T(8,128)(2,1)S(1)}, bf16[256,2304]{1,0:T(8,128)(2,1)S(1)}, u32[]{:S(2)}, u32[]{:S(2)}) %collective-permute-start.2) | collective-permute-done | bytes 1179680 | tf_op jit(solution)/shard_map/ppermute | solution.py:264
  190.3 8.4 convolution_convert_fusion.12.merged_ref
  211.6 23.6 %collective-permute-done.11 = bf16[256,2304]{1,0:T(8,128)(2,1)S(1)} collective-permute-done((bf16[256,2304]{1,0:T(8,128)(2,1)S(1)}, bf16[256,2304]{1,0:T(8,128)(2,1)S(1)}, u32[]{:S(2)}, u32[]{:S(2)}) %collective-permute-start.11) | collective-permute-done | bytes 1179680 | tf_op jit(solution)/shard_map/ppermute | solution.py:264
  235.2 25.9 %collective-permute-done.10 = bf16[256,2304]{1,0:T(8,128)(2,1)S(1)} collective-permute-done((bf16[256,2304]{1,0:T(8,128)(2,1)S(1)}, bf16[256,2304]{1,0:T(8,128)(2,1)S(1)}, u32[]{:S(2)}, u32[]{:S(2)}) %collective-permute-start.10) | collective-permute-done | bytes 1179680 | tf_op jit(solution)/shard_map/ppermute | solution.py:264
  266.7 5.6 constant_dynamic-update-slice_fusion.20
  275.9 25.3 %collective-permute-done.12 = bf16[256,2304]{1,0:T(8,128)(2,1)S(1)} collective-permute-done((bf16[256,2304]{1,0:T(8,128)(2,1)S(1)}, bf16[256,2304]{1,0:T(8,128)(2,1)S(1)}, u32[]{:S(2)}, u32[]{:S(2)}) %collective-permute-start.12) | collective-permute-done | bytes 1179680 | tf_op jit(solution)/shard_map/ppermute | solution.py:264
  302.3 21.1 %collective-permute-done.13 = bf16[256,2304]{1,0:T(8,128)(2,1)S(1)} collective-permute-done((bf16[256,2304]{1,0:T(8,128)(2,1)S(1)}, bf16[256,2304]{1,0:T(8,128)(2,1)S(1)}, u32[]{:S(2)}, u32[]{:S(2)}) %collective-permute-start.13) | collective-permute-done | bytes 1179680 | tf_op jit(solution)/shard_map/ppermute | solution.py:264
  326.1 14.9 %fusion.239 = f32[1024,2304]{1,0:T(8,128)S(1)} fusion(bf16[1024,2304]{1,0:T(8,128)(2,1)} %constant_dynamic-update-slice_fusion.17, bf16[2304,2304]{1,0:T(8,128)(2,1)} %all-gather.11.cloned.1.call-done), kind=kOutput, calls=%fused_computation.466 | convolution fusion | flops 10871635968 | bytes 24772608 | tf_op jit(solution)/shard_map/dot_general | solution.py:49
  347.4 14.9 %fusion.240 = f32[1024,2304]{1,0:T(8,128)S(1)} fusion(bf16[1024,2304]{1,0:T(8,128)(2,1)} %constant_dynamic-update-slice_fusion.17, bf16[2304,2304]{1,0:T(8,128)(2,1)} %all-gather.15.cloned.1.call-done), kind=kOutput, calls=%fused_computation.467 | convolution fusion | flops 10871635968 | bytes 24772608 | tf_op jit(solution)/shard_map/dot_general | solution.py:49
  369.3 39.5 %all-gather.13.cloned.1.call-done = bf16[2304,2304]{1,0:T(8,128)(2,1)} async-done(((bf16[288,2304]{1,0:T(8,128)(2,1)}), bf16[2304,2304]{1,0:T(8,128)(2,1)}) %all-gather.13.cloned.1.call-update) | async-done | bytes 10616848 | tf_op jit(solution)/shard_map/all_gather | solution.py:297
  408.8 9.6 fusion.29
  428.9 20.1 %collective-permute-done.26 = bf16[256,2304]{1,0:T(8,128)(2,1)S(1)} collective-permute-done((bf16[256,2304]{1,0:T(8,128)(2,1)S(1)}, bf16[256,2304]{1,0:T(8,128)(2,1)S(1)}, u32[]{:S(2)}, u32[]{:S(2)}) %collective-permute-start.26) | collective-permute-done | bytes 1179680 | tf_op jit(solution)/shard_map/ppermute | solution.py:264
  449.0 27.5 %collective-permute-done.25 = bf16[256,2304]{1,0:T(8,128)(2,1)S(1)} collective-permute-done((bf16[256,2304]{1,0:T(8,128)(2,1)S(1)}, bf16[256,2304]{1,0:T(8,128)(2,1)S(1)}, u32[]{:S(2)}, u32[]{:S(2)}) %collective-permute-start.25) | collective-permute-done | bytes 1179680 | tf_op jit(solution)/shard_map/ppermute | solution.py:264
  485.4 25.3 %collective-permute-done.27 = bf16[256,2304]{1,0:T(8,128)(2,1)S(1)} collective-permute-done((bf16[256,2304]{1,0:T(8,128)(2,1)S(1)}, bf16[256,2304]{1,0:T(8,128)(2,1)S(1)}, u32[]{:S(2)}, u32[]{:S(2)}) %collective-permute-start.27) | collective-permute-done | bytes 1179680 | tf_op jit(solution)/shard_map/ppermute | solution.py:264
  510.8 22.6 %collective-permute-done.28 = bf16[256,2304]{1,0:T(8,128)(2,1)S(1)} collective-permute-done((bf16[256,2304]{1,0:T(8,128)(2,1)S(1)}, bf16[256,2304]{1,0:T(8,128)(2,1)S(1)}, u32[]{:S(2)}, u32[]{:S(2)}) %collective-permute-start.28) | collective-permute-done | bytes 1179680 | tf_op jit(solution)/shard_map/ppermute | solution.py:264
  535.2 16.3 %multiply_convert_fusion = (bf16[1024,1152]{1,0:T(8,128)(2,1)}, bf16[1024,1152]{1,0:T(8,128)(2,1)}) fusion(f32[1024,2304]{1,0:T(8,128)} %copy-done.14, bf16[1024,2304]{1,0:T(8,128)(2,1)S(1)} %constant_dynamic-update-slice_fusion.4, bf16[2304,2304]{1,0:T(8,128)(2,1)} %all-gather.13.cloned.1.call-done), kind=kOutput, calls=%fused_computation.64 | convolution fusion | flops 5464129536 | bytes 24182784 | tf_op jit(solution)/shard_map/dot_general | solution.py:53
  551.5 12.8 multiply_convert_fusion.1
  564.3 9.6 fusion.89
  573.9 7.9 fusion.46
  582.9 9.0 fusion.86
  591.9 5.9 fusion.45
  599.2 8.7 fusion.83
  608.0 5.9 fusion.44
  614.9 8.7 fusion.80
  623.7 25.3 %collective-permute-done.31 = bf16[256,2304]{1,0:T(8,128)(2,1)} collective-permute-done((bf16[256,2304]{1,0:T(8,128)(2,1)}, bf16[256,2304]{1,0:T(8,128)(2,1)}, u32[]{:S(2)}, u32[]{:S(2)}) %collective-permute-start.31) | collective-permute-done | bytes 1179680 | tf_op jit(solution)/shard_map/ppermute | solution.py:264
  649.0 15.5 %multiply_reduce_fusion = (f32[2304]{0:T(1024)}, f32[256]{0:T(256)}, f32[256,2304]{1,0:T(8,128)}) fusion(f32[256,2304]{1,0:T(8,128)} %copy-done.5, f32[256]{0:T(256)} %copy-done.48, f32[2304]{0:T(1024)} %get-tuple-element.81, s32[2304]{0:T(1024)} %copy-done.41, f32[256,2304]{1,0:T(8,128)} %fusion.80, bf16[2304,2304]{1,0:T(8,128)(2,1)} %all-gather.11.cloned.1.call-done, ...), kind=kOutput, calls=%fused_computation.136 | convolution fusion | flops 5451741184 | bytes 25981956 | tf_op jit(solution)/shard_map/dot_general | solution.py:53
  665.2 4.4 multiply_reduce_fusion.1
  675.1 25.3 %collective-permute-done.33 = bf16[256,2304]{1,0:T(8,128)(2,1)S(1)} collective-permute-done((bf16[256,2304]{1,0:T(8,128)(2,1)S(1)}, bf16[256,2304]{1,0:T(8,128)(2,1)S(1)}, u32[]{:S(2)}, u32[]{:S(2)}) %collective-permute-start.33) | collective-permute-done | bytes 1179680 | tf_op jit(solution)/shard_map/ppermute | solution.py:264
  700.6 22.3 %collective-permute-done.34 = bf16[256,2304]{1,0:T(8,128)(2,1)S(1)} collective-permute-done((bf16[256,2304]{1,0:T(8,128)(2,1)S(1)}, bf16[256,2304]{1,0:T(8,128)(2,1)S(1)}, u32[]{:S(2)}, u32[]{:S(2)}) %collective-permute-start.34) | collective-permute-done | bytes 1179680 | tf_op jit(solution)/shard_map/ppermute | solution.py:264
  729.9 6.5 convolution_convert_fusion.13.upstream_ref
  737.9 7.3 shard_map.231
  745.3 9.1 convolution_convert_fusion.4
  754.7 17.0 %convolution_convert_fusion = bf16[2304,2304]{1,0:T(8,128)(2,1)} fusion(bf16[1024,2304]{1,0:T(8,128)(2,1)} %constant_dynamic-update-slice_fusion.17, bf16[1024,1152]{1,0:T(8,128)(2,1)} %get-tuple-element.97, bf16[1024,1152]{1,0:T(8,128)(2,1)} %get-tuple-element.98), kind=kOutput, calls=%fused_computation.7 | convolution fusion | flops 10886381568 | bytes 20054016 | tf_op jit(solution)/shard_map/dot_general | solution.py:57
  771.7 17.0 %convolution_convert_fusion.1 = bf16[2304,2304]{1,0:T(8,128)(2,1)} fusion(bf16[1024,2304]{1,0:T(8,128)(2,1)} %constant_dynamic-update-slice_fusion.17, bf16[1024,1152]{1,0:T(8,128)(2,1)} %copy-done.56, bf16[1024,1152]{1,0:T(8,128)(2,1)} %get-tuple-element.96), kind=kOutput, calls=%fused_computation.8 | convolution fusion | flops 10886381568 | bytes 20054016 | tf_op jit(solution)/shard_map/dot_general | solution.py:57
  789.2 9.2 convolution_convert_fusion.2
  798.3 8.6 convolution_convert_fusion.3
  806.9 12.3 pad_maximum_fusion
  819.3 5.0 convolution_convert_fusion.6
  825.0 5.5 convolution_convert_fusion.7
  836.0 17.4 %collective-permute-done.38 = bf16[256,2304]{1,0:T(8,128)(2,1)} collective-permute-done((bf16[256,2304]{1,0:T(8,128)(2,1)}, bf16[256,2304]{1,0:T(8,128)(2,1)}, u32[]{:S(2)}, u32[]{:S(2)}) %collective-permute-start.38) | collective-permute-done | bytes 1179680 | tf_op jit(solution)/shard_map/ppermute | solution.py:264
  853.4 24.9 %collective-permute-done.37 = bf16[256,2304]{1,0:T(8,128)(2,1)} collective-permute-done((bf16[256,2304]{1,0:T(8,128)(2,1)}, bf16[256,2304]{1,0:T(8,128)(2,1)}, u32[]{:S(2)}, u32[]{:S(2)}) %collective-permute-start.37) | collective-permute-done | bytes 1179680 | tf_op jit(solution)/shard_map/ppermute | solution.py:264
  878.3 10.7 fusion.66
  892.4 4.3 fusion.63
  904.5 26.8 %reduce-scatter.12.cloned.1.call-done = bf16[288,2304]{1,0:T(8,128)(2,1)} async-done(((bf16[2304,2304]{1,0:T(8,128)(2,1)}), bf16[288,2304]{1,0:T(8,128)(2,1)}) %reduce-scatter.12.cloned.1.call-update) | async-done | bytes 1327120 | tf_op jit(solution)/shard_map/reduce_scatter | solution.py:300
  935.8 106.9 %reduce-scatter.10.cloned.1.call-done = bf16[288,2304]{1,0:T(8,128)(2,1)} async-done(((bf16[2304,2304]{1,0:T(8,128)(2,1)}), bf16[288,2304]{1,0:T(8,128)(2,1)}) %reduce-scatter.10.cloned.1.call-update) | async-done | bytes 1327120 | tf_op jit(solution)/shard_map/reduce_scatter | solution.py:300
  1045.4 108.5 %reduce-scatter.14.cloned.1.call-done = bf16[288,2304]{1,0:T(8,128)(2,1)} async-done(((bf16[2304,2304]{1,0:T(8,128)(2,1)}), bf16[288,2304]{1,0:T(8,128)(2,1)}) %reduce-scatter.14.cloned.1.call-update) | async-done | bytes 1327120 | tf_op jit(solution)/shard_map/reduce_scatter | solution.py:300
  1158.0 5.2 collective-permute-done.45
  1164.7 7.0 collective-permute-done.48
  1173.3 9.1 collective-permute-done.47
  1184.9 6.4 collective-permute-done.50
  1193.7 5.6 collective-permute-done.49
  1200.8 7.5 fusion.32
  1221.6 5.7 shard_map.232
  1227.2 7.3 all-to-all-start
  1244.6 104.5 %all-to-all-done = bf16[1248,8,256]{2,1,0:T(8,128)(2,1)} async-done(((bf16[1248,8,256]{2,1,0:T(8,128)(2,1)}), bf16[1248,8,256]{2,1,0:T(8,128)(2,1)}, u32[]{:S(2)}, u32[]{:S(2)}) %all-to-all-start) | async-done | bytes 5111840 | tf_op jit(solution)/shard_map/all_to_all | solution.py:549
  1350.9 33.9 %shard_map.233 = (f32[38,256,256]{2,1,0:T(8,128)}, f32[38,256,256]{2,1,0:T(8,128)}, f32[38,256,256]{2,1,0:T(8,128)}) custom-call(bf16[32,39,8,256]{3,2,1,0:T(8,128)(2,1)} %bitcast.92.incoming, f32[38,256,256]{2,1,0:T(8,128)} %first.1, f32[38,256,256]{2,1,0:T(8,128)} %second.1, f32[38,256,256]{2,1,0:T(8,128)} %left.1, f32[38,256,256]{2,1,0:T(8,128)} %right.1, ...), custom_call_target="tpu_custom_call" | custom-call | flops 5100273664 | bytes 84672512 | tf_op jit(solution)/shard_map/pallas_call | solution.py:216
  (413 shorter events, 197.2 us)
Async XLA Ops:
  7.2 183.2 %all-gather.7.cloned.1.call-start = ((), (), s32[]{:S(2)}) async-start(), calls=%async_computation.6 | async-start | bytes 5308416 | tf_op jit(solution)/shard_map/all_gather | solution.py:297
  8.8 7.3 collective-permute-start.3
  11.9 8.5 collective-permute-start.4
  13.5 7.0 collective-permute-start.5
  21.3 182.1 %all-gather.9.cloned.1.call-start = ((), (), s32[]{:S(2)}) async-start(), calls=%async_computation.7 | async-start | bytes 2654208 | tf_op jit(solution)/shard_map/all_gather | solution.py:297
  22.2 16.3 %collective-permute-start.6 = (bf16[16,2304]{1,0:T(8,128)(2,1)}, bf16[16,2304]{1,0:T(8,128)(2,1)S(1)}, u32[]{:S(2)}, u32[]{:S(2)}) collective-permute-start(bf16[16,2304]{1,0:T(8,128)(2,1)} %get-tuple-element.184), channel_id=1, source_target_pairs={{0,8},{8,0},{16,24},{24,16},{1,9},{9,1},{17,25},{25,17},{2,10},{10... | collective-permute-start | bytes 221192 | tf_op jit(solution)/shard_map/ppermute | solution.py:264
  23.4 15.2 %collective-permute-start.7 = (bf16[16,2304]{1,0:T(8,128)(2,1)}, bf16[16,2304]{1,0:T(8,128)(2,1)S(1)}, u32[]{:S(2)}, u32[]{:S(2)}) collective-permute-start(bf16[16,2304]{1,0:T(8,128)(2,1)} %get-tuple-element.183), channel_id=1, source_target_pairs={{0,16},{8,24},{16,0},{24,8},{1,17},{9,25},{17,1},{25,9},{2,18},{10... | collective-permute-start | bytes 221192 | tf_op jit(solution)/shard_map/ppermute | solution.py:264
  24.3 14.3 %collective-permute-start.8 = (bf16[16,2304]{1,0:T(8,128)(2,1)S(1)}, bf16[16,2304]{1,0:T(8,128)(2,1)S(1)}, u32[]{:S(2)}, u32[]{:S(2)}) collective-permute-start(bf16[16,2304]{1,0:T(8,128)(2,1)S(1)} %get-tuple-element.182), channel_id=1, source_target_pairs={{0,24},{8,16},{16,8},{24,0},{1,25},{9,17},{17,9},{25,1},{2,26},{10... | collective-permute-start | bytes 221192 | tf_op jit(solution)/shard_map/ppermute | solution.py:264
  39.4 286.7 %all-gather.11.cloned.1.call-start = ((), (), s32[]{:S(2)}) async-start(), calls=%async_computation.8 | async-start | bytes 11943936 | tf_op jit(solution)/shard_map/all_gather | solution.py:297
  39.5 10.7 collective-permute-start.15
  40.8 14.7 %collective-permute-start.16 = (bf16[72,2304]{1,0:T(8,128)(2,1)S(1)}, bf16[72,2304]{1,0:T(8,128)(2,1)S(1)}, u32[]{:S(2)}, u32[]{:S(2)}) collective-permute-start(bf16[72,2304]{1,0:T(8,128)(2,1)S(1)} %pad_maximum_fusion.6), channel_id=1, source_target_pairs={{0,16},{8,24},{16,0},{24,8},{1,17},{9,25},{17,1},{25,9},{2,18},{10... | collective-permute-start | bytes 995336 | tf_op jit(solution)/shard_map/ppermute | solution.py:264
  41.9 13.7 collective-permute-start.17
  56.7 290.8 %all-gather.15.cloned.1.call-start = ((), (), s32[]{:S(2)}) async-start(), calls=%async_computation.10 | async-start | bytes 11943936 | tf_op jit(solution)/shard_map/all_gather | solution.py:297
  56.8 10.3 collective-permute-start.21
  57.4 13.3 collective-permute-start.22
  59.2 11.6 collective-permute-start.23
  71.9 336.9 %all-gather.13.cloned.1.call-start = ((), (), s32[]{:S(2)}) async-start(), calls=%async_computation.9 | async-start | bytes 11943936 | tf_op jit(solution)/shard_map/all_gather | solution.py:297
  74.0 46.6 %collective-permute-start.18 = (bf16[72,2304]{1,0:T(8,128)(2,1)S(1)}, bf16[72,2304]{1,0:T(8,128)(2,1)}, u32[]{:S(2)}, u32[]{:S(2)}) collective-permute-start(bf16[72,2304]{1,0:T(8,128)(2,1)S(1)} %get-tuple-element.136), channel_id=1, source_target_pairs={{0,8},{8,0},{16,24},{24,16},{1,9},{9,1},{17,25},{25,17},{2,10},{10... | collective-permute-start | bytes 995336 | tf_op jit(solution)/shard_map/ppermute | solution.py:264
  75.8 45.8 %collective-permute-start.19 = (bf16[72,2304]{1,0:T(8,128)(2,1)S(1)}, bf16[72,2304]{1,0:T(8,128)(2,1)}, u32[]{:S(2)}, u32[]{:S(2)}) collective-permute-start(bf16[72,2304]{1,0:T(8,128)(2,1)S(1)} %get-tuple-element.135), channel_id=1, source_target_pairs={{0,16},{8,24},{16,0},{24,8},{1,17},{9,25},{17,1},{25,9},{2,18},{10... | collective-permute-start | bytes 995336 | tf_op jit(solution)/shard_map/ppermute | solution.py:264
  76.1 46.5 %collective-permute-start.20 = (bf16[72,2304]{1,0:T(8,128)(2,1)S(1)}, bf16[72,2304]{1,0:T(8,128)(2,1)}, u32[]{:S(2)}, u32[]{:S(2)}) collective-permute-start(bf16[72,2304]{1,0:T(8,128)(2,1)S(1)} %get-tuple-element.134), channel_id=1, source_target_pairs={{0,24},{8,16},{16,8},{24,0},{1,25},{9,17},{17,9},{25,1},{2,26},{10... | collective-permute-start | bytes 995336 | tf_op jit(solution)/shard_map/ppermute | solution.py:264
  124.7 771.9 %reduce-scatter.8.cloned.1.call-start = ((), (), s32[]{:S(2)}) async-start(), calls=%async_computation.12 | async-start | bytes 2654208 | tf_op jit(solution)/shard_map/reduce_scatter | solution.py:300
  134.9 28.8 %collective-permute-start = (bf16[256,2304]{1,0:T(8,128)(2,1)S(1)}, bf16[256,2304]{1,0:T(8,128)(2,1)S(1)}, u32[]{:S(2)}, u32[]{:S(2)}) collective-permute-start(bf16[256,2304]{1,0:T(8,128)(2,1)S(1)} %get-tuple-element.203), channel_id=1, source_target_pairs={{0,8},{8,0},{16,24},{24,16},{1,9},{9,1},{17,25},{25,17},{2,10},{10... | collective-permute-start | bytes 3538952 | tf_op jit(solution)/shard_map/ppermute | solution.py:264
  134.9 29.9 %collective-permute-start.1 = (bf16[256,2304]{1,0:T(8,128)(2,1)S(1)}, bf16[256,2304]{1,0:T(8,128)(2,1)S(1)}, u32[]{:S(2)}, u32[]{:S(2)}) collective-permute-start(bf16[256,2304]{1,0:T(8,128)(2,1)S(1)} %get-tuple-element.203), channel_id=1, source_target_pairs={{0,16},{8,24},{16,0},{24,8},{1,17},{9,25},{17,1},{25,9},{2,18},{10... | collective-permute-start | bytes 3538952 | tf_op jit(solution)/shard_map/ppermute | solution.py:264
  136.3 52.9 %collective-permute-start.2 = (bf16[256,2304]{1,0:T(8,128)(2,1)S(1)}, bf16[256,2304]{1,0:T(8,128)(2,1)S(1)}, u32[]{:S(2)}, u32[]{:S(2)}) collective-permute-start(bf16[256,2304]{1,0:T(8,128)(2,1)S(1)} %get-tuple-element.203), channel_id=1, source_target_pairs={{0,24},{8,16},{16,8},{24,0},{1,25},{9,17},{17,9},{25,1},{2,26},{10... | collective-permute-start | bytes 3538952 | tf_op jit(solution)/shard_map/ppermute | solution.py:264
  206.2 29.0 %collective-permute-start.11 = (bf16[256,2304]{1,0:T(8,128)(2,1)S(1)}, bf16[256,2304]{1,0:T(8,128)(2,1)S(1)}, u32[]{:S(2)}, u32[]{:S(2)}) collective-permute-start(bf16[256,2304]{1,0:T(8,128)(2,1)S(1)} %convolution_convert_fusion.9), channel_id=1, source_target_pairs={{0,8},{8,0},{16,24},{24,16},{1,9},{9,1},{17,25},{25,17},{2,10},{10... | collective-permute-start | bytes 3538952 | tf_op jit(solution)/shard_map/ppermute | solution.py:264
  209.2 51.9 %collective-permute-start.10 = (bf16[256,2304]{1,0:T(8,128)(2,1)S(1)}, bf16[256,2304]{1,0:T(8,128)(2,1)S(1)}, u32[]{:S(2)}, u32[]{:S(2)}) collective-permute-start(bf16[256,2304]{1,0:T(8,128)(2,1)S(1)} %convolution_convert_fusion.10), channel_id=1, source_target_pairs={{0,16},{8,24},{16,0},{24,8},{1,17},{9,25},{17,1},{25,9},{2,18},{10... | collective-permute-start | bytes 3538952 | tf_op jit(solution)/shard_map/ppermute | solution.py:264
  211.4 49.7 %collective-permute-start.9 = (bf16[256,2304]{1,0:T(8,128)(2,1)S(1)}, bf16[256,2304]{1,0:T(8,128)(2,1)S(1)}, u32[]{:S(2)}, u32[]{:S(2)}) collective-permute-start(bf16[256,2304]{1,0:T(8,128)(2,1)S(1)} %convolution_convert_fusion.11), channel_id=1, source_target_pairs={{0,24},{8,16},{16,8},{24,0},{1,25},{9,17},{17,9},{25,1},{2,26},{10... | collective-permute-start | bytes 3538952 | tf_op jit(solution)/shard_map/ppermute | solution.py:264
  272.4 28.8 %collective-permute-start.12 = (bf16[256,2304]{1,0:T(8,128)(2,1)S(1)}, bf16[256,2304]{1,0:T(8,128)(2,1)S(1)}, u32[]{:S(2)}, u32[]{:S(2)}) collective-permute-start(bf16[256,2304]{1,0:T(8,128)(2,1)S(1)} %get-tuple-element.207), channel_id=1, source_target_pairs={{0,8},{8,0},{16,24},{24,16},{1,9},{9,1},{17,25},{25,17},{2,10},{10... | collective-permute-start | bytes 3538952 | tf_op jit(solution)/shard_map/ppermute | solution.py:264
  273.0 50.4 %collective-permute-start.13 = (bf16[256,2304]{1,0:T(8,128)(2,1)S(1)}, bf16[256,2304]{1,0:T(8,128)(2,1)S(1)}, u32[]{:S(2)}, u32[]{:S(2)}) collective-permute-start(bf16[256,2304]{1,0:T(8,128)(2,1)S(1)} %get-tuple-element.207), channel_id=1, source_target_pairs={{0,16},{8,24},{16,0},{24,8},{1,17},{9,25},{17,1},{25,9},{2,18},{10... | collective-permute-start | bytes 3538952 | tf_op jit(solution)/shard_map/ppermute | solution.py:264
  274.4 50.6 %collective-permute-start.14 = (bf16[256,2304]{1,0:T(8,128)(2,1)S(1)}, bf16[256,2304]{1,0:T(8,128)(2,1)S(1)}, u32[]{:S(2)}, u32[]{:S(2)}) collective-permute-start(bf16[256,2304]{1,0:T(8,128)(2,1)S(1)} %get-tuple-element.207), channel_id=1, source_target_pairs={{0,24},{8,16},{16,8},{24,0},{1,25},{9,17},{17,9},{25,1},{2,26},{10... | collective-permute-start | bytes 3538952 | tf_op jit(solution)/shard_map/ppermute | solution.py:264
  420.1 28.9 %collective-permute-start.26 = (bf16[256,2304]{1,0:T(8,128)(2,1)S(1)}, bf16[256,2304]{1,0:T(8,128)(2,1)S(1)}, u32[]{:S(2)}, u32[]{:S(2)}) collective-permute-start(bf16[256,2304]{1,0:T(8,128)(2,1)S(1)} %add_convert_fusion), channel_id=1, source_target_pairs={{0,8},{8,0},{16,24},{24,16},{1,9},{9,1},{17,25},{25,17},{2,10},{10... | collective-permute-start | bytes 3538952 | tf_op jit(solution)/shard_map/ppermute | solution.py:264
  423.4 53.2 %collective-permute-start.25 = (bf16[256,2304]{1,0:T(8,128)(2,1)S(1)}, bf16[256,2304]{1,0:T(8,128)(2,1)S(1)}, u32[]{:S(2)}, u32[]{:S(2)}) collective-permute-start(bf16[256,2304]{1,0:T(8,128)(2,1)S(1)} %add_convert_fusion.1), channel_id=1, source_target_pairs={{0,16},{8,24},{16,0},{24,8},{1,17},{9,25},{17,1},{25,9},{2,18},{10... | collective-permute-start | bytes 3538952 | tf_op jit(solution)/shard_map/ppermute | solution.py:264
  426.6 49.9 %collective-permute-start.24 = (bf16[256,2304]{1,0:T(8,128)(2,1)S(1)}, bf16[256,2304]{1,0:T(8,128)(2,1)S(1)}, u32[]{:S(2)}, u32[]{:S(2)}) collective-permute-start(bf16[256,2304]{1,0:T(8,128)(2,1)S(1)} %add_convert_fusion.2), channel_id=1, source_target_pairs={{0,24},{8,16},{16,8},{24,0},{1,25},{9,17},{17,9},{25,1},{2,26},{10... | collective-permute-start | bytes 3538952 | tf_op jit(solution)/shard_map/ppermute | solution.py:264
  481.8 28.9 %collective-permute-start.27 = (bf16[256,2304]{1,0:T(8,128)(2,1)S(1)}, bf16[256,2304]{1,0:T(8,128)(2,1)S(1)}, u32[]{:S(2)}, u32[]{:S(2)}) collective-permute-start(bf16[256,2304]{1,0:T(8,128)(2,1)S(1)} %get-tuple-element.90), channel_id=1, source_target_pairs={{0,8},{8,0},{16,24},{24,16},{1,9},{9,1},{17,25},{25,17},{2,10},{10... | collective-permute-start | bytes 3538952 | tf_op jit(solution)/shard_map/ppermute | solution.py:264
  482.4 51.0 %collective-permute-start.28 = (bf16[256,2304]{1,0:T(8,128)(2,1)S(1)}, bf16[256,2304]{1,0:T(8,128)(2,1)S(1)}, u32[]{:S(2)}, u32[]{:S(2)}) collective-permute-start(bf16[256,2304]{1,0:T(8,128)(2,1)S(1)} %get-tuple-element.90), channel_id=1, source_target_pairs={{0,16},{8,24},{16,0},{24,8},{1,17},{9,25},{17,1},{25,9},{2,18},{10... | collective-permute-start | bytes 3538952 | tf_op jit(solution)/shard_map/ppermute | solution.py:264
  483.9 51.1 %collective-permute-start.29 = (bf16[256,2304]{1,0:T(8,128)(2,1)S(1)}, bf16[256,2304]{1,0:T(8,128)(2,1)S(1)}, u32[]{:S(2)}, u32[]{:S(2)}) collective-permute-start(bf16[256,2304]{1,0:T(8,128)(2,1)S(1)} %get-tuple-element.90), channel_id=1, source_target_pairs={{0,24},{8,16},{16,8},{24,0},{1,25},{9,17},{17,9},{25,1},{2,26},{10... | collective-permute-start | bytes 3538952 | tf_op jit(solution)/shard_map/ppermute | solution.py:264
  581.9 41.8 %collective-permute-start.32 = (bf16[256,2304]{1,0:T(8,128)(2,1)S(1)}, bf16[256,2304]{1,0:T(8,128)(2,1)}, u32[]{:S(2)}, u32[]{:S(2)}) collective-permute-start(bf16[256,2304]{1,0:T(8,128)(2,1)S(1)} %fusion.46), channel_id=1, source_target_pairs={{0,8},{8,0},{16,24},{24,16},{1,9},{9,1},{17,25},{25,17},{2,10},{10... | collective-permute-start | bytes 3538952 | tf_op jit(solution)/shard_map/ppermute | solution.py:264
  597.8 51.2 %collective-permute-start.31 = (bf16[256,2304]{1,0:T(8,128)(2,1)}, bf16[256,2304]{1,0:T(8,128)(2,1)}, u32[]{:S(2)}, u32[]{:S(2)}) collective-permute-start(bf16[256,2304]{1,0:T(8,128)(2,1)} %fusion.45), channel_id=1, source_target_pairs={{0,16},{8,24},{16,0},{24,8},{1,17},{9,25},{17,1},{25,9},{2,18},{10... | collective-permute-start | bytes 3538952 | tf_op jit(solution)/shard_map/ppermute | solution.py:264
  613.9 35.1 %collective-permute-start.30 = (bf16[256,2304]{1,0:T(8,128)(2,1)}, bf16[256,2304]{1,0:T(8,128)(2,1)}, u32[]{:S(2)}, u32[]{:S(2)}) collective-permute-start(bf16[256,2304]{1,0:T(8,128)(2,1)} %fusion.44), channel_id=1, source_target_pairs={{0,24},{8,16},{16,8},{24,0},{1,25},{9,17},{17,9},{25,1},{2,26},{10... | collective-permute-start | bytes 3538952 | tf_op jit(solution)/shard_map/ppermute | solution.py:264
  671.6 28.9 %collective-permute-start.33 = (bf16[256,2304]{1,0:T(8,128)(2,1)S(1)}, bf16[256,2304]{1,0:T(8,128)(2,1)S(1)}, u32[]{:S(2)}, u32[]{:S(2)}) collective-permute-start(bf16[256,2304]{1,0:T(8,128)(2,1)S(1)} %get-tuple-element.87), channel_id=1, source_target_pairs={{0,8},{8,0},{16,24},{24,16},{1,9},{9,1},{17,25},{25,17},{2,10},{10... | collective-permute-start | bytes 3538952 | tf_op jit(solution)/shard_map/ppermute | solution.py:264
  672.9 50.0 %collective-permute-start.34 = (bf16[256,2304]{1,0:T(8,128)(2,1)S(1)}, bf16[256,2304]{1,0:T(8,128)(2,1)S(1)}, u32[]{:S(2)}, u32[]{:S(2)}) collective-permute-start(bf16[256,2304]{1,0:T(8,128)(2,1)S(1)} %get-tuple-element.87), channel_id=1, source_target_pairs={{0,16},{8,24},{16,0},{24,8},{1,17},{9,25},{17,1},{25,9},{2,18},{10... | collective-permute-start | bytes 3538952 | tf_op jit(solution)/shard_map/ppermute | solution.py:264
  673.5 49.5 %collective-permute-start.35 = (bf16[256,2304]{1,0:T(8,128)(2,1)S(1)}, bf16[256,2304]{1,0:T(8,128)(2,1)S(1)}, u32[]{:S(2)}, u32[]{:S(2)}) collective-permute-start(bf16[256,2304]{1,0:T(8,128)(2,1)S(1)} %get-tuple-element.87), channel_id=1, source_target_pairs={{0,24},{8,16},{16,8},{24,0},{1,25},{9,17},{17,9},{25,1},{2,26},{10... | collective-permute-start | bytes 3538952 | tf_op jit(solution)/shard_map/ppermute | solution.py:264
  729.2 172.8 %reduce-scatter.6.cloned.1.call-start = ((), (), s32[]{:S(2)}) async-start(), calls=%async_computation.11 | async-start | bytes 5308416 | tf_op jit(solution)/shard_map/reduce_scatter | solution.py:300
  754.4 176.9 %reduce-scatter.12.cloned.1.call-start = ((), (), s32[]{:S(2)}) async-start(), calls=%async_computation.14 | async-start | bytes 11943936 | tf_op jit(solution)/shard_map/reduce_scatter | solution.py:300
  771.7 271.1 %reduce-scatter.10.cloned.1.call-start = ((), (), s32[]{:S(2)}) async-start(), calls=%async_computation.13 | async-start | bytes 11943936 | tf_op jit(solution)/shard_map/reduce_scatter | solution.py:300
  788.7 365.2 %reduce-scatter.14.cloned.1.call-start = ((), (), s32[]{:S(2)}) async-start(), calls=%async_computation.15 | async-start | bytes 11943936 | tf_op jit(solution)/shard_map/reduce_scatter | solution.py:300
  824.3 29.2 %collective-permute-start.38 = (bf16[256,2304]{1,0:T(8,128)(2,1)}, bf16[256,2304]{1,0:T(8,128)(2,1)}, u32[]{:S(2)}, u32[]{:S(2)}) collective-permute-start(bf16[256,2304]{1,0:T(8,128)(2,1)} %convolution_convert_fusion.6), channel_id=1, source_target_pairs={{0,8},{8,0},{16,24},{24,16},{1,9},{9,1},{17,25},{25,17},{2,10},{10... | collective-permute-start | bytes 3538952 | tf_op jit(solution)/shard_map/ppermute | solution.py:264
  830.5 47.8 %collective-permute-start.37 = (bf16[256,2304]{1,0:T(8,128)(2,1)}, bf16[256,2304]{1,0:T(8,128)(2,1)}, u32[]{:S(2)}, u32[]{:S(2)}) collective-permute-start(bf16[256,2304]{1,0:T(8,128)(2,1)} %convolution_convert_fusion.7), channel_id=1, source_target_pairs={{0,16},{8,24},{16,0},{24,8},{1,17},{9,25},{17,1},{25,9},{2,18},{10... | collective-permute-start | bytes 3538952 | tf_op jit(solution)/shard_map/ppermute | solution.py:264
  833.5 44.8 %collective-permute-start.36 = (bf16[256,2304]{1,0:T(8,128)(2,1)}, bf16[256,2304]{1,0:T(8,128)(2,1)}, u32[]{:S(2)}, u32[]{:S(2)}) collective-permute-start(bf16[256,2304]{1,0:T(8,128)(2,1)} %convolution_convert_fusion.8), channel_id=1, source_target_pairs={{0,24},{8,16},{16,8},{24,0},{1,25},{9,17},{17,9},{25,1},{2,26},{10... | collective-permute-start | bytes 3538952 | tf_op jit(solution)/shard_map/ppermute | solution.py:264
  898.3 310.0 %collective-permute-start.42 = (bf16[16,2304]{1,0:T(8,128)(2,1)S(1)}, bf16[16,2304]{1,0:T(8,128)(2,1)S(1)}, u32[]{:S(2)}, u32[]{:S(2)}) collective-permute-start(bf16[16,2304]{1,0:T(8,128)(2,1)S(1)} %get-tuple-element.176), channel_id=1, source_target_pairs={{0,8},{8,0},{16,24},{24,16},{1,9},{9,1},{17,25},{25,17},{2,10},{10... | collective-permute-start | bytes 221192 | tf_op jit(solution)/shard_map/ppermute | solution.py:264
  898.9 311.0 %collective-permute-start.43 = (bf16[16,2304]{1,0:T(8,128)(2,1)}, bf16[16,2304]{1,0:T(8,128)(2,1)S(1)}, u32[]{:S(2)}, u32[]{:S(2)}) collective-permute-start(bf16[16,2304]{1,0:T(8,128)(2,1)} %get-tuple-element.175), channel_id=1, source_target_pairs={{0,16},{8,24},{16,0},{24,8},{1,17},{9,25},{17,1},{25,9},{2,18},{10... | collective-permute-start | bytes 221192 | tf_op jit(solution)/shard_map/ppermute | solution.py:264
  900.6 309.9 %collective-permute-start.44 = (bf16[16,2304]{1,0:T(8,128)(2,1)S(1)}, bf16[16,2304]{1,0:T(8,128)(2,1)S(1)}, u32[]{:S(2)}, u32[]{:S(2)}) collective-permute-start(bf16[16,2304]{1,0:T(8,128)(2,1)S(1)} %get-tuple-element.174), channel_id=1, source_target_pairs={{0,24},{8,16},{16,8},{24,0},{1,25},{9,17},{17,9},{25,1},{2,26},{10... | collective-permute-start | bytes 221192 | tf_op jit(solution)/shard_map/ppermute | solution.py:264
  904.0 307.9 %collective-permute-start.39 = (bf16[72,1024]{1,0:T(8,128)(2,1)}, bf16[72,1024]{1,0:T(8,128)(2,1)S(1)}, u32[]{:S(2)}, u32[]{:S(2)}) collective-permute-start(bf16[72,1024]{1,0:T(8,128)(2,1)} %get-tuple-element.140), channel_id=1, source_target_pairs={{0,8},{8,0},{16,24},{24,16},{1,9},{9,1},{17,25},{25,17},{2,10},{10... | collective-permute-start | bytes 442376 | tf_op jit(solution)/shard_map/ppermute | solution.py:264
  933.3 222.2 %collective-permute-start.46 = (bf16[72,2304]{1,0:T(8,128)(2,1)}, bf16[72,2304]{1,0:T(8,128)(2,1)}, u32[]{:S(2)}, u32[]{:S(2)}) collective-permute-start(bf16[72,2304]{1,0:T(8,128)(2,1)} %get-tuple-element.129), channel_id=1, source_target_pairs={{0,8},{8,0},{16,24},{24,16},{1,9},{9,1},{17,25},{25,17},{2,10},{10... | collective-permute-start | bytes 995336 | tf_op jit(solution)/shard_map/ppermute | solution.py:264
  1155.5 7.7 collective-permute-start.45
  1163.2 8.6 collective-permute-start.48
  1171.8 10.7 collective-permute-start.47
  1182.4 8.8 collective-permute-start.50
  1191.2 8.0 collective-permute-start.49
  1199.3 14.3 %collective-permute-start.40 = (bf16[72,1024]{1,0:T(8,128)(2,1)}, bf16[72,1024]{1,0:T(8,128)(2,1)S(1)}, u32[]{:S(2)}, u32[]{:S(2)}) collective-permute-start(bf16[72,1024]{1,0:T(8,128)(2,1)} %get-tuple-element.139), channel_id=1, source_target_pairs={{0,16},{8,24},{16,0},{24,8},{1,17},{9,25},{17,1},{25,9},{2,18},{10... | collective-permute-start | bytes 442376 | tf_op jit(solution)/shard_map/ppermute | solution.py:264
  1209.9 7.2 collective-permute-start.51
  1210.4 9.7 collective-permute-start.52
  1211.9 9.7 collective-permute-start.53
  1227.2 121.9 %all-to-all-start = ((bf16[1248,8,256]{2,1,0:T(8,128)(2,1)}), bf16[1248,8,256]{2,1,0:T(8,128)(2,1)}, u32[]{:S(2)}, u32[]{:S(2)}) async-start(bf16[1248,8,256]{2,1,0:T(8,128)(2,1)} %shard_map.232), calls=%async_computation.5 | async-start | bytes 10223616 | tf_op jit(solution)/shard_map/all_to_all | solution.py:549
  (66 other events, 1303.2 us)
Sparse Core Ops, SparseCore 0:
  21.4 51.5 all-gather.6
  75.2 30.4 all-gather.8
  107.9 99.6 all-gather.10
  209.7 98.7 all-gather.14
  310.0 98.7 all-gather.12
  729.3 34.1 reduce-scatter.7
  766.4 53.5 reduce-scatter.5
  822.3 109.0 reduce-scatter.11
  933.6 109.0 reduce-scatter.9
  1044.9 109.0 reduce-scatter.13

commit v2 on v1

--- a/solution.py
+++ b/solution.py
@@ -7,9 +7,9 @@
 from jax.experimental.pallas import tpu as pltpu
 from jax.sharding import PartitionSpec as P
 
+
 D = 2304
 QUERY_HEADS = 8
-KV_HEAD_COUNT = 4
 HEAD_SIZE = 256
 FF = 9216
 BLK = 256
@@ -252,16 +252,28 @@
     dp_count = lax.axis_size("dp")
     seq_index = lax.axis_index("seq")
     share = qkv_weight.shape[0]
-    total_rows = rows * seq_count
     heads = QUERY_HEADS // seq_count
     query_slice = heads * HEAD_SIZE
     key_slice = KEY_FEATURES // seq_count
     ff_slice = FF // seq_count
     d_groups = D // BLK
     half = ff_slice // 2
+    parts = (slice(0, D // 3), slice(D // 3, D))
 
     def swap(value, turn):
         return lax.ppermute(value, "seq", [(at, at ^ turn) for at in range(seq_count)])
+
+    def double_gather(value):
+        for axis, size in (("dp", dp_count), ("seq", seq_count)):
+            step = 1
+            while step < size:
+                other = lax.ppermute(value, axis, [(at, at ^ step) for at in range(size)])
+                upper = (lax.axis_index(axis) & step) != 0
+                value = jnp.concatenate(
+                    [jnp.where(upper, other, value), jnp.where(upper, value, other)], axis=0
+                )
+                step *= 2
+        return value
 
     def owner_of(turn):
         return jnp.bitwise_xor(seq_index, turn)
@@ -294,15 +306,19 @@
         received = [piece_for(seq_index)]
         for turn in range(1, seq_count):
             received.append(swap(piece_for(owner_of(turn)), turn))
-        return lax.all_gather(assemble(received), "dp", axis=0, tiled=True)
+        operand = assemble(received)
+        return lax.all_gather(operand, "dp", axis=0, tiled=True)
 
     def collect(gradient):
-        summed = lax.psum_scatter(gradient.astype(BF16), "dp", scatter_dimension=0, tiled=True)
+        summed = lax.psum_scatter(gradient, "dp", scatter_dimension=0, tiled=True)
         size = summed.shape[0] // seq_count
         result = [pick(summed, seq_index, size, 0)]
         for turn in range(1, seq_count):
             result.append(swap(pick(summed, owner_of(turn), size, 0), turn))
         return result
+
+    def after(values, others):
+        return list(lax.optimization_barrier(tuple(values) + tuple(others)))[: len(values)]
 
     def row_order(groups):
         at = jnp.arange(groups * BLK, dtype=jnp.int32)
@@ -324,7 +340,7 @@
     qkv_low = local_rows(qkv_weight).reshape(d_groups * share, -1)
     out_low = local_rows(out_weight)
     down_low = local_rows(down_weight)
-    gain_full = lax.all_gather(norm_gains.astype(BF16), ALL, axis=0, tiled=True)
+    gain_full = double_gather(norm_gains.astype(BF16).reshape(1, -1)).reshape(D, 4)
 
     def qkv_piece(target):
         return jnp.concatenate(
@@ -339,8 +355,10 @@
     def out_piece(target):
         return pick(out_low, target, heads, 0).reshape(heads * share, D)
 
-    def down_piece(target):
-        return pick(down_low, target, d_groups, 0).reshape(d_groups * share, D)
+    def down_piece(part):
+        return lambda target: pick(down_low[..., part], target, d_groups, 0).reshape(
+            d_groups * share, -1
+        )
 
     qkv_slice_full = spread(qkv_piece)
     out_slice_full = spread(out_piece)
@@ -367,9 +385,10 @@
         return piece
 
     geglu_zero = spread(geglu_piece(0))
-    down_full = spread(down_piece)
     geglu_one = spread(geglu_piece(1))
     geglu_parts = (geglu_zero, geglu_one)
+    down_late = spread(down_piece(parts[1]))
+    down_early = spread(down_piece(parts[0]))
 
     gains = gain_full.astype(F32)
     normed, inverse_one = norm_forward(inputs, gains[:, 0])
@@ -393,14 +412,16 @@
         uppers.append(upper)
         products.append((jax.nn.gelu(gate, approximate=True) * upper).astype(BF16))
 
-    branch_zero = dot(products[0], down_full[:half])
-
-    def branch_part(owner):
-        return pick(branch_zero, owner, rows, 0) + dot(
-            pick(products[1], owner, rows, 0), down_full[half:]
-        )
-
-    branch = scatter_rows(branch_part)
+    product = jnp.concatenate(products, axis=1)
+
+    def branch_columns(weight):
+        def part_of(owner):
+            return dot(pick(product, owner, rows, 0), weight)
+
+        return scatter_rows(part_of)
+
+    branch_late = branch_columns(down_late)
+    branch = jnp.concatenate([branch_columns(down_early), branch_late], axis=1)
     branch_normed, inverse_four = norm_forward(branch, gains[:, 3])
     query_pos = seq_index * rows + jnp.arange(rows, dtype=jnp.int32)
     live_rows = (query_pos < seq_lengths[0]).astype(F32)[:, None]
@@ -409,36 +430,47 @@
 
     upstream = upstream * live_rows
     grad_branch, gain_four = norm_backward(branch, inverse_four, gains[:, 3], upstream)
-    branch_all = gather_rows(grad_branch.astype(BF16))
-    down_sums = collect(
-        jnp.concatenate([dot_tn(products[0], branch_all), dot_tn(products[1], branch_all)], axis=0)
-    )
+    branch_low = grad_branch.astype(BF16)
+    branch_alls = [gather_rows(branch_low[:, part]) for part in parts]
+    down_terms = []
+    for value in branch_alls:
+        down_terms.append(dot_tn(product, value).astype(BF16))
+    down_sums = [collect(term) for term in down_terms]
+    branch_alls = after(branch_alls, down_terms)
     gate_up_grads = []
-    geglu_sums = []
+    geglu_terms = []
     for part in range(2):
-        grad_product = dot_nt(branch_all, down_full[part * half : (part + 1) * half])
+        ff_rows = slice(part * half, (part + 1) * half)
+        grad_product = dot_nt(branch_alls[0], down_early[ff_rows]) + dot_nt(
+            branch_alls[1], down_late[ff_rows]
+        )
         activated, gelu_pull = jax.vjp(lambda value: jax.nn.gelu(value, approximate=True), gates[part])
         grad_gate = gelu_pull(grad_product * uppers[part])[0]
         grad_upper = grad_product * activated
         gate_up_grad = jnp.concatenate([grad_gate, grad_upper], axis=1).astype(BF16)
+        geglu_terms.append(dot_tn(ffn_all, gate_up_grad).astype(BF16))
+        if part == 0:
+            branch_alls = after(branch_alls, [geglu_terms[0]])
         gate_up_grads.append(gate_up_grad)
-        geglu_sums.append(collect(dot_tn(ffn_all, gate_up_grad)))
+    geglu_sums = [collect(term) for term in geglu_terms]
+    ffn_total = dot_nt(gate_up_grads[0], geglu_zero) + dot_nt(gate_up_grads[1], geglu_one)
 
     def ffn_part(owner):
-        return dot_nt(pick(gate_up_grads[0], owner, rows, 0), geglu_zero) + dot_nt(
-            pick(gate_up_grads[1], owner, rows, 0), geglu_one
-        )
+        return pick(ffn_total, owner, rows, 0)
 
     grad_ffn = dot_nt(scatter_rows(ffn_part).astype(BF16), wide_order)
     grad_hidden_norm, gain_three = norm_backward(hidden, inverse_three, gains[:, 2], grad_ffn)
     grad_hidden = upstream + grad_hidden_norm
     grad_attended, gain_two = norm_backward(attended, inverse_two, gains[:, 1], grad_hidden)
     attended_all = gather_rows(grad_attended.astype(BF16))
+    (attended_all,) = after([attended_all], [geglu_terms[1]])
     grad_mixed_turned = dot_nt(attended_all, out_slice_full).astype(BF16)
     grad_mixed = dot_nt(grad_mixed_turned, head_order).astype(BF16)
-    out_sums = collect(dot_tn(mixed_turned, attended_all))
+    out_term = dot_tn(mixed_turned, attended_all).astype(BF16)
+    out_sums = collect(out_term)
+    (grad_mixed,) = after([grad_mixed], [out_term])
     grad_merged = attention_backward(merged, grad_mixed, seq_lengths, prefix_lengths, heads)
-    qkv_sums = collect(dot_tn(normed_all, grad_merged))
+    qkv_sums = collect(dot_tn(normed_all, grad_merged).astype(BF16))
     grad_normed = dot_nt(
         scatter_rows(lambda owner: dot_nt(pick(grad_merged, owner, rows, 0), qkv_slice_full)).astype(BF16),
         wide_order,
@@ -458,12 +490,16 @@
         ],
         axis=0,
     )
-    geglu_natural = dot_nt(turned, wide_order).astype(BF16).reshape(
+    geglu_natural = dot_nt(turned, wide_order).astype(BF16)
+    geglu_natural = geglu_natural.reshape(
         seq_count, 2, d_groups, share, ff_slice
     )
     qkv_local = [value.reshape(d_groups, share, -1) for value in qkv_sums]
     out_local = [value.reshape(heads, share, D) for value in out_sums]
-    down_local = [value.reshape(d_groups, share, D) for value in down_sums]
+    down_local = [
+        jnp.concatenate([early, late], axis=1).reshape(d_groups, share, D)
+        for early, late in zip(*down_sums)
+    ]
 
     def in_order(items):
         return assemble([item[None] for item in items])
@@ -605,4 +641,5 @@
         P(ALL, None, None),
         P(ALL, None, None),
     )
+
     return jax.shard_map(body, mesh=mesh, in_specs=in_specs, out_specs=out_specs, check_vma=False)

time: 1400 us -> 1380 us (0.986)
  blocking collectives: 41.9 us -> 0 us
  local copies, waits for them, and re-layouts: 58.3 us -> 91.6 us
  matrix products: 283 us -> 258 us
  starting transfers between devices: 77.3 us -> 102 us
  other arithmetic: 50.5 us -> 35.8 us
    all_gather x1 -> x0, blocking collectives: 41.9 us -> none  [body(): gain_full = lax.all_gather(norm_gains.astype(BF16), ALL, axis=0, tiled=True)]
    dot_general x16 -> x13, matrix products: 138 us -> 109 us  [dot_nt(): lax.dot_general(left, right, (((1,), (1,)), ((), ())), preferred_element_...]
    ppermute x54 -> x66, starting transfers between devices: 68.4 us -> 91 us  [swap(): lax.ppermute(value, 'seq', [(at, at ^ turn) for at in range(seq_count)])]
    ppermute x54 -> x66, waiting for transfers between devices: 426 us -> 404 us  [swap(): lax.ppermute(value, 'seq', [(at, at ^ turn) for at in range(seq_count)])]
    all_gather x5 -> x6, waiting for transfers between devices: 39.6 us -> 60.9 us  [spread(): return lax.all_gather(operand, 'dp', axis=0, tiled=True)]
    unnamed x135 -> x182, local copies, waits for them, and re-layouts: 19.2 us -> 31.7 us
    dot_general x16 -> x19, matrix products: 80.8 us -> 86.2 us  [dot(): return jnp.dot(left, right, preferred_element_type=F32)]
    reduce_scatter x5 -> x6, waiting for transfers between devices: 242 us -> 237 us  [collect(): summed = lax.psum_scatter(gradient, 'dp', scatter_dimension=0, tiled=True)]
  transfers between devices with their start and end apart: 65 -> 84, of which waited for: 37 -> 50; matrix products, arithmetic and copies ran while one was open for 20% -> 18% of each run, Pallas kernels for 1% -> 1%
where the time goes in v2:
time: 1380 us
  waiting for transfers between devices  820 us (59%)
  matrix products  258 us (19%)
  starting transfers between devices  102 us (7%)
  local copies, waits for them, and re-layouts  91.6 us (7%)
  Pallas kernels  50.6 us (4%)
  other arithmetic  35.8 us (3%)
  between operations  18.1 us (1%)
    ppermute x66, waiting for transfers between devices, swap(): lax.ppermute(value, 'seq', [(at, at ^ turn) for at in range(seq_count)])  404 us
    reduce_scatter x6, waiting for transfers between devices, collect(): summed = lax.psum_scatter(gradient, 'dp', scatter_dimension=0, tiled=True)  237 us
    dot_general x13, matrix products, dot_nt(): lax.dot_general(left, right, (((1,), (1,)), ((), ())), preferred_element_...  109 us
    all_to_all x1, waiting for transfers between devices, body(): lax.all_to_all(outgoing, ALL, split_axis=0, concat_axis=0, tiled=True)  105 us
    ppermute x66, starting transfers between devices, swap(): lax.ppermute(value, 'seq', [(at, at ^ turn) for at in range(seq_count)])  91 us
    dot_general x19, matrix products, dot(): return jnp.dot(left, right, preferred_element_type=F32)  86.2 us
    dot_general x6, matrix products, dot_tn(): lax.dot_general(left, right, (((0,), (0,)), ((), ())), preferred_element_...  62.2 us
    all_gather x6, waiting for transfers between devices, spread(): return lax.all_gather(operand, 'dp', axis=0, tiled=True)  60.9 us
  transfers between devices with their start and end apart: 84, of which 50 were waited for; matrix products, arithmetic and copies ran while one was open for 18% of the time, Pallas kernels for 1%

profile of v2, /device:TPU:0, one launch (start us, length us, event | category | flops | bytes accessed | tf_op | source)
XLA Modules:
  0.0 1375.9 jit_solution(6604135246224377695)
XLA Ops:
  29.6 8.7 fusion.27
  43.6 6.7 collective-permute-done.20
  50.3 5.3 collective-permute-done.21
  60.6 6.4 collective-permute-done.23
  92.8 4.5 collective-permute-start.2
  112.1 5.5 constant_dynamic-update-slice_fusion.37
  122.4 24.0 %collective-permute-done.5 = bf16[256,2304]{1,0:T(8,128)(2,1)S(1)} collective-permute-done((bf16[256,2304]{1,0:T(8,128)(2,1)S(1)}, bf16[256,2304]{1,0:T(8,128)(2,1)S(1)}, u32[]{:S(2)}, u32[]{:S(2)}) %collective-permute-start.5) | collective-permute-done | bytes 1179680 | tf_op jit(solution)/shard_map/ppermute | solution.py:264
  147.5 20.6 %collective-permute-done.6 = bf16[256,2304]{1,0:T(8,128)(2,1)S(1)} collective-permute-done((bf16[256,2304]{1,0:T(8,128)(2,1)S(1)}, bf16[256,2304]{1,0:T(8,128)(2,1)S(1)}, u32[]{:S(2)}, u32[]{:S(2)}) %collective-permute-start.6) | collective-permute-done | bytes 1179680 | tf_op jit(solution)/shard_map/ppermute | solution.py:264
  170.3 8.8 convolution_convert_fusion.15.merged_ref
  191.8 23.6 %collective-permute-done.16 = bf16[256,2304]{1,0:T(8,128)(2,1)S(1)} collective-permute-done((bf16[256,2304]{1,0:T(8,128)(2,1)S(1)}, bf16[256,2304]{1,0:T(8,128)(2,1)S(1)}, u32[]{:S(2)}, u32[]{:S(2)}) %collective-permute-start.16) | collective-permute-done | bytes 1179680 | tf_op jit(solution)/shard_map/ppermute | solution.py:264
  215.4 21.1 %collective-permute-done.15 = bf16[256,2304]{1,0:T(8,128)(2,1)S(1)} collective-permute-done((bf16[256,2304]{1,0:T(8,128)(2,1)S(1)}, bf16[256,2304]{1,0:T(8,128)(2,1)S(1)}, u32[]{:S(2)}, u32[]{:S(2)}) %collective-permute-start.15) | collective-permute-done | bytes 1179680 | tf_op jit(solution)/shard_map/ppermute | solution.py:264
  240.5 5.6 constant_dynamic-update-slice_fusion.27
  255.5 24.1 %collective-permute-done.26 = bf16[72,768]{1,0:T(8,128)(2,1)S(1)} collective-permute-done((bf16[72,768]{1,0:T(8,128)(2,1)S(1)}, bf16[72,768]{1,0:T(8,128)(2,1)S(1)}, u32[]{:S(2)}, u32[]{:S(2)}) %collective-permute-start.26) | collective-permute-done | bytes 110624 | tf_op jit(solution)/shard_map/ppermute | solution.py:264
  281.7 19.9 %collective-permute-done.27 = bf16[72,768]{1,0:T(8,128)(2,1)S(1)} collective-permute-done((bf16[72,768]{1,0:T(8,128)(2,1)S(1)}, bf16[72,768]{1,0:T(8,128)(2,1)S(1)}, u32[]{:S(2)}, u32[]{:S(2)}) %collective-permute-start.27) | collective-permute-done | bytes 110624 | tf_op jit(solution)/shard_map/ppermute | solution.py:264
  307.1 15.0 %fusion.186 = f32[1024,2304]{1,0:T(8,128)S(1)} fusion(bf16[1024,2304]{1,0:T(8,128)(2,1)} %constant_dynamic-update-slice_fusion.24, bf16[2304,2304]{1,0:T(8,128)(2,1)} %all-gather.11.cloned.1.call-done), kind=kOutput, calls=%fused_computation.468 | convolution fusion | flops 10871635968 | bytes 24772608 | tf_op jit(solution)/shard_map/dot_general | solution.py:49
  327.5 15.0 %fusion.187 = f32[1024,2304]{1,0:T(8,128)S(1)} fusion(bf16[1024,2304]{1,0:T(8,128)(2,1)} %constant_dynamic-update-slice_fusion.24, bf16[2304,2304]{1,0:T(8,128)(2,1)} %all-gather.13.cloned.1.call-done), kind=kOutput, calls=%fused_computation.469 | convolution fusion | flops 10871635968 | bytes 24772608 | tf_op jit(solution)/shard_map/dot_general | solution.py:49
  349.2 30.8 %all-gather.17.cloned.1.call-done = bf16[2304,1536]{1,0:T(8,128)(2,1)} async-done(((bf16[288,1536]{1,0:T(8,128)(2,1)}), bf16[2304,1536]{1,0:T(8,128)(2,1)}) %all-gather.17.cloned.1.call-update) | async-done | bytes 7077904 | tf_op jit(solution)/shard_map/all_gather | solution.py:310
  380.0 6.2 convolution_convert_fusion.12
  392.1 30.1 %all-gather.15.cloned.1.call-done = bf16[2304,768]{1,0:T(8,128)(2,1)} async-done(((bf16[288,768]{1,0:T(8,128)(2,1)}), bf16[2304,768]{1,0:T(8,128)(2,1)}) %all-gather.15.cloned.1.call-update) | async-done | bytes 3538960 | tf_op jit(solution)/shard_map/all_gather | solution.py:310
  440.0 24.5 %collective-permute-done.30 = bf16[256,768]{1,0:T(8,128)(2,1)S(1)} collective-permute-done((bf16[256,768]{1,0:T(8,128)(2,1)S(1)}, bf16[256,768]{1,0:T(8,128)(2,1)S(1)}, u32[]{:S(2)}, u32[]{:S(2)}) %collective-permute-start.30) | collective-permute-done | bytes 393248 | tf_op jit(solution)/shard_map/ppermute | solution.py:264
  488.0 7.3 collective-permute-done.39
  496.9 5.9 convolution_convert_fusion.4
  502.8 9.0 collective-permute-done.41
  514.0 12.3 collective-permute-done.42
  530.4 11.4 convolution_convert_fusion.2
  541.9 7.3 fusion.38
  549.3 8.5 fusion.19
  559.2 15.6 %convolution_convert_fusion.1 = bf16[2304,2304]{1,0:T(8,128)(2,1)} fusion(bf16[1024,2304]{1,0:T(8,128)(2,1)S(1)} %bitcast.246, bf16[1024,1152]{1,0:T(8,128)(2,1)} %get-tuple-element.84, bf16[1024,1152]{1,0:T(8,128)(2,1)S(1)} %get-tuple-element.83), kind=kOutput, calls=%fused_computation.8 | convolution fusion | flops 10886381568 | bytes 20054016 | tf_op jit(solution)/shard_map/dot_general | solution.py:57
  574.7 7.3 fusion.36
  582.1 8.2 fusion.26
  592.4 13.6 fusion.40
  606.0 17.5 %convolution_add_fusion = f32[1024,2304]{1,0:T(8,128)} fusion(f32[1024,2304]{1,0:T(8,128)} %fusion.40, bf16[2304,2304]{1,0:T(8,128)(2,1)} %all-gather.11.cloned.1.call-done, bf16[1024,1152]{1,0:T(8,128)(2,1)} %get-tuple-element.84, bf16[1024,1152]{1,0:T(8,128)(2,1)S(1)} %copy-done.75), kind=kOutput, calls=%fused_computation.29 | convolution fusion | flops 10883432448 | bytes 34209792 | tf_op jit(solution)/shard_map/dot_general | solution.py:53
  623.5 5.0 dynamic-slice_convert_fusion.2
  632.6 25.0 %collective-permute-done.46 = bf16[256,2304]{1,0:T(8,128)(2,1)} collective-permute-done((bf16[256,2304]{1,0:T(8,128)(2,1)}, bf16[256,2304]{1,0:T(8,128)(2,1)}, u32[]{:S(2)}, u32[]{:S(2)}) %collective-permute-start.46) | collective-permute-done | bytes 1179680 | tf_op jit(solution)/shard_map/ppermute | solution.py:264
  657.7 22.7 %collective-permute-done.45 = bf16[256,2304]{1,0:T(8,128)(2,1)} collective-permute-done((bf16[256,2304]{1,0:T(8,128)(2,1)}, bf16[256,2304]{1,0:T(8,128)(2,1)}, u32[]{:S(2)}, u32[]{:S(2)}) %collective-permute-start.45) | collective-permute-done | bytes 1179680 | tf_op jit(solution)/shard_map/ppermute | solution.py:264
  680.3 9.3 multiply_reduce_fusion
  699.8 14.0 %convolution_convert_fusion = bf16[2304,2304]{1,0:T(8,128)(2,1)} fusion(bf16[1024,2304]{1,0:T(8,128)(2,1)S(1)} %bitcast.248, bf16[1024,1152]{1,0:T(8,128)(2,1)S(1)} %copy-done.73, bf16[1024,1152]{1,0:T(8,128)(2,1)S(1)} %copy-done.71), kind=kOutput, calls=%fused_computation.7 | convolution fusion | flops 10886381568 | bytes 20054016 | tf_op jit(solution)/shard_map/dot_general | solution.py:57
  713.8 11.4 collective-permute-done.47
  727.6 17.5 %collective-permute-done.48 = bf16[256,2304]{1,0:T(8,128)(2,1)S(1)} collective-permute-done((bf16[256,2304]{1,0:T(8,128)(2,1)S(1)}, bf16[256,2304]{1,0:T(8,128)(2,1)S(1)}, u32[]{:S(2)}, u32[]{:S(2)}) %collective-permute-start.48) | collective-permute-done | bytes 1179680 | tf_op jit(solution)/shard_map/ppermute | solution.py:264
  747.3 6.2 convolution_convert_fusion.5
  754.2 6.3 convolution_convert_fusion.16.upstream_ref
  762.0 7.3 shard_map.231
  769.4 9.1 convolution_convert_fusion.3
  780.4 5.0 convolution_convert_fusion.6
  786.5 4.8 convolution_convert_fusion.7
  799.3 15.2 %collective-permute-done.52 = bf16[256,2304]{1,0:T(8,128)(2,1)} collective-permute-done((bf16[256,2304]{1,0:T(8,128)(2,1)}, bf16[256,2304]{1,0:T(8,128)(2,1)}, u32[]{:S(2)}, u32[]{:S(2)}) %collective-permute-start.52) | collective-permute-done | bytes 1179680 | tf_op jit(solution)/shard_map/ppermute | solution.py:264
  814.5 26.0 %collective-permute-done.51 = bf16[256,2304]{1,0:T(8,128)(2,1)} collective-permute-done((bf16[256,2304]{1,0:T(8,128)(2,1)}, bf16[256,2304]{1,0:T(8,128)(2,1)}, u32[]{:S(2)}, u32[]{:S(2)}) %collective-permute-start.51) | collective-permute-done | bytes 1179680 | tf_op jit(solution)/shard_map/ppermute | solution.py:264
  840.5 11.4 fusion.52
  883.5 41.4 %reduce-scatter.17.cloned.1.call-done = bf16[288,1536]{1,0:T(8,128)(2,1)} async-done(((bf16[2304,1536]{1,0:T(8,128)(2,1)}), bf16[288,1536]{1,0:T(8,128)(2,1)}) %reduce-scatter.17.cloned.1.call-update) | async-done | bytes 884752 | tf_op jit(solution)/shard_map/reduce_scatter | solution.py:313
  927.9 4.4 collective-permute-done.66
  933.8 6.8 collective-permute-done.68
  943.0 4.4 collective-permute-done.70
  947.5 88.9 %reduce-scatter.13.cloned.1.call-done = bf16[288,2304]{1,0:T(8,128)(2,1)} async-done(((bf16[2304,2304]{1,0:T(8,128)(2,1)}), bf16[288,2304]{1,0:T(8,128)(2,1)}) %reduce-scatter.13.cloned.1.call-update) | async-done | bytes 1327120 | tf_op jit(solution)/shard_map/reduce_scatter | solution.py:313
  1040.9 106.7 %reduce-scatter.11.cloned.1.call-done = bf16[288,2304]{1,0:T(8,128)(2,1)} async-done(((bf16[2304,2304]{1,0:T(8,128)(2,1)}), bf16[288,2304]{1,0:T(8,128)(2,1)}) %reduce-scatter.11.cloned.1.call-update) | async-done | bytes 1327120 | tf_op jit(solution)/shard_map/reduce_scatter | solution.py:313
  1152.6 5.2 collective-permute-done.59
  1159.3 7.0 collective-permute-done.62
  1167.8 9.1 collective-permute-done.61
  1179.4 6.4 collective-permute-done.64
  1188.3 5.6 collective-permute-done.63
  1195.4 7.5 fusion.28
  1204.7 4.4 collective-permute-done.55
  1209.0 5.7 shard_map.232
  1228.3 104.6 %all-to-all-done = bf16[1248,8,256]{2,1,0:T(8,128)(2,1)} async-done(((bf16[1248,8,256]{2,1,0:T(8,128)(2,1)}), bf16[1248,8,256]{2,1,0:T(8,128)(2,1)}, u32[]{:S(2)}, u32[]{:S(2)}) %all-to-all-start) | async-done | bytes 5111840 | tf_op jit(solution)/shard_map/all_to_all | solution.py:585
  1334.7 33.9 %shard_map.233 = (f32[38,256,256]{2,1,0:T(8,128)}, f32[38,256,256]{2,1,0:T(8,128)}, f32[38,256,256]{2,1,0:T(8,128)}) custom-call(bf16[32,39,8,256]{3,2,1,0:T(8,128)(2,1)} %bitcast.92.incoming, f32[38,256,256]{2,1,0:T(8,128)} %first.1, f32[38,256,256]{2,1,0:T(8,128)} %second.1, f32[38,256,256]{2,1,0:T(8,128)} %left.1, f32[38,256,256]{2,1,0:T(8,128)} %right.1, ...), custom_call_target="tpu_custom_call" | custom-call | flops 5100273664 | bytes 84672512 | tf_op jit(solution)/shard_map/pallas_call | solution.py:216
  (531 shorter events, 289.4 us)
Async XLA Ops:
  7.2 163.1 %all-gather.7.cloned.1.call-start = ((), (), s32[]{:S(2)}) async-start(), calls=%async_computation.7 | async-start | bytes 5308416 | tf_op jit(solution)/shard_map/all_gather | solution.py:310
  21.3 162.4 %all-gather.9.cloned.1.call-start = ((), (), s32[]{:S(2)}) async-start(), calls=%async_computation.8 | async-start | bytes 2654208 | tf_op jit(solution)/shard_map/all_gather | solution.py:310
  22.2 16.3 %collective-permute-start.11 = (bf16[16,2304]{1,0:T(8,128)(2,1)}, bf16[16,2304]{1,0:T(8,128)(2,1)S(1)}, u32[]{:S(2)}, u32[]{:S(2)}) collective-permute-start(bf16[16,2304]{1,0:T(8,128)(2,1)} %get-tuple-element.185), channel_id=1, source_target_pairs={{0,8},{8,0},{16,24},{24,16},{1,9},{9,1},{17,25},{25,17},{2,10},{10... | collective-permute-start | bytes 221192 | tf_op jit(solution)/shard_map/ppermute | solution.py:264
  23.4 15.2 %collective-permute-start.12 = (bf16[16,2304]{1,0:T(8,128)(2,1)}, bf16[16,2304]{1,0:T(8,128)(2,1)S(1)}, u32[]{:S(2)}, u32[]{:S(2)}) collective-permute-start(bf16[16,2304]{1,0:T(8,128)(2,1)} %get-tuple-element.184), channel_id=1, source_target_pairs={{0,16},{8,24},{16,0},{24,8},{1,17},{9,25},{17,1},{25,9},{2,18},{10... | collective-permute-start | bytes 221192 | tf_op jit(solution)/shard_map/ppermute | solution.py:264
  24.3 14.3 %collective-permute-start.13 = (bf16[16,2304]{1,0:T(8,128)(2,1)S(1)}, bf16[16,2304]{1,0:T(8,128)(2,1)S(1)}, u32[]{:S(2)}, u32[]{:S(2)}) collective-permute-start(bf16[16,2304]{1,0:T(8,128)(2,1)S(1)} %get-tuple-element.183), channel_id=1, source_target_pairs={{0,24},{8,16},{16,8},{24,0},{1,25},{9,17},{17,9},{25,1},{2,26},{10... | collective-permute-start | bytes 221192 | tf_op jit(solution)/shard_map/ppermute | solution.py:264
  39.3 267.7 %all-gather.11.cloned.1.call-start = ((), (), s32[]{:S(2)}) async-start(), calls=%async_computation.9 | async-start | bytes 11943936 | tf_op jit(solution)/shard_map/all_gather | solution.py:310
  39.5 10.7 collective-permute-start.20
  40.8 14.7 %collective-permute-start.21 = (bf16[72,2304]{1,0:T(8,128)(2,1)S(1)}, bf16[72,2304]{1,0:T(8,128)(2,1)S(1)}, u32[]{:S(2)}, u32[]{:S(2)}) collective-permute-start(bf16[72,2304]{1,0:T(8,128)(2,1)S(1)} %pad_maximum_fusion.11), channel_id=1, source_target_pairs={{0,16},{8,24},{16,0},{24,8},{1,17},{9,25},{17,1},{25,9},{2,18},{10... | collective-permute-start | bytes 995336 | tf_op jit(solution)/shard_map/ppermute | solution.py:264
  41.9 13.7 collective-permute-start.22
  56.7 270.8 %all-gather.13.cloned.1.call-start = ((), (), s32[]{:S(2)}) async-start(), calls=%async_computation.10 | async-start | bytes 11943936 | tf_op jit(solution)/shard_map/all_gather | solution.py:310
  56.8 10.3 collective-permute-start.23
  57.4 13.3 collective-permute-start.24
  59.2 11.6 collective-permute-start.25
  71.9 308.1 %all-gather.17.cloned.1.call-start = ((), (), s32[]{:S(2)}) async-start(), calls=%async_computation.12 | async-start | bytes 7962624 | tf_op jit(solution)/shard_map/all_gather | solution.py:310
  87.1 335.0 %all-gather.15.cloned.1.call-start = ((), (), s32[]{:S(2)}) async-start(), calls=%async_computation.11 | async-start | bytes 3981312 | tf_op jit(solution)/shard_map/all_gather | solution.py:310
  117.6 28.8 %collective-permute-start.5 = (bf16[256,2304]{1,0:T(8,128)(2,1)S(1)}, bf16[256,2304]{1,0:T(8,128)(2,1)S(1)}, u32[]{:S(2)}, u32[]{:S(2)}) collective-permute-start(bf16[256,2304]{1,0:T(8,128)(2,1)S(1)} %get-tuple-element.214), channel_id=1, source_target_pairs={{0,8},{8,0},{16,24},{24,16},{1,9},{9,1},{17,25},{25,17},{2,10},{10... | collective-permute-start | bytes 3538952 | tf_op jit(solution)/shard_map/ppermute | solution.py:264
  117.9 50.1 %collective-permute-start.6 = (bf16[256,2304]{1,0:T(8,128)(2,1)S(1)}, bf16[256,2304]{1,0:T(8,128)(2,1)S(1)}, u32[]{:S(2)}, u32[]{:S(2)}) collective-permute-start(bf16[256,2304]{1,0:T(8,128)(2,1)S(1)} %get-tuple-element.214), channel_id=1, source_target_pairs={{0,16},{8,24},{16,0},{24,8},{1,17},{9,25},{17,1},{25,9},{2,18},{10... | collective-permute-start | bytes 3538952 | tf_op jit(solution)/shard_map/ppermute | solution.py:264
  119.4 49.8 %collective-permute-start.7 = (bf16[256,2304]{1,0:T(8,128)(2,1)S(1)}, bf16[256,2304]{1,0:T(8,128)(2,1)S(1)}, u32[]{:S(2)}, u32[]{:S(2)}) collective-permute-start(bf16[256,2304]{1,0:T(8,128)(2,1)S(1)} %get-tuple-element.214), channel_id=1, source_target_pairs={{0,24},{8,16},{16,8},{24,0},{1,25},{9,17},{17,9},{25,1},{2,26},{10... | collective-permute-start | bytes 3538952 | tf_op jit(solution)/shard_map/ppermute | solution.py:264
  186.5 28.9 %collective-permute-start.16 = (bf16[256,2304]{1,0:T(8,128)(2,1)S(1)}, bf16[256,2304]{1,0:T(8,128)(2,1)S(1)}, u32[]{:S(2)}, u32[]{:S(2)}) collective-permute-start(bf16[256,2304]{1,0:T(8,128)(2,1)S(1)} %convolution_convert_fusion.9), channel_id=1, source_target_pairs={{0,8},{8,0},{16,24},{24,16},{1,9},{9,1},{17,25},{25,17},{2,10},{10... | collective-permute-start | bytes 3538952 | tf_op jit(solution)/shard_map/ppermute | solution.py:264
  189.2 47.4 %collective-permute-start.15 = (bf16[256,2304]{1,0:T(8,128)(2,1)S(1)}, bf16[256,2304]{1,0:T(8,128)(2,1)S(1)}, u32[]{:S(2)}, u32[]{:S(2)}) collective-permute-start(bf16[256,2304]{1,0:T(8,128)(2,1)S(1)} %convolution_convert_fusion.10), channel_id=1, source_target_pairs={{0,16},{8,24},{16,0},{24,8},{1,17},{9,25},{17,1},{25,9},{2,18},{10... | collective-permute-start | bytes 3538952 | tf_op jit(solution)/shard_map/ppermute | solution.py:264
  190.2 46.3 %collective-permute-start.14 = (bf16[256,2304]{1,0:T(8,128)(2,1)S(1)}, bf16[256,2304]{1,0:T(8,128)(2,1)S(1)}, u32[]{:S(2)}, u32[]{:S(2)}) collective-permute-start(bf16[256,2304]{1,0:T(8,128)(2,1)S(1)} %convolution_convert_fusion.11), channel_id=1, source_target_pairs={{0,24},{8,16},{16,8},{24,0},{1,25},{9,17},{17,9},{25,1},{2,26},{10... | collective-permute-start | bytes 3538952 | tf_op jit(solution)/shard_map/ppermute | solution.py:264
  248.2 54.3 %collective-permute-start.17 = (bf16[256,2304]{1,0:T(8,128)(2,1)}, bf16[256,2304]{1,0:T(8,128)(2,1)S(1)}, u32[]{:S(2)}, u32[]{:S(2)}) collective-permute-start(bf16[256,2304]{1,0:T(8,128)(2,1)} %get-tuple-element.218), channel_id=1, source_target_pairs={{0,8},{8,0},{16,24},{24,16},{1,9},{9,1},{17,25},{25,17},{2,10},{10... | collective-permute-start | bytes 3538952 | tf_op jit(solution)/shard_map/ppermute | solution.py:264
  249.3 54.3 %collective-permute-start.18 = (bf16[256,2304]{1,0:T(8,128)(2,1)}, bf16[256,2304]{1,0:T(8,128)(2,1)S(1)}, u32[]{:S(2)}, u32[]{:S(2)}) collective-permute-start(bf16[256,2304]{1,0:T(8,128)(2,1)} %get-tuple-element.218), channel_id=1, source_target_pairs={{0,16},{8,24},{16,0},{24,8},{1,17},{9,25},{17,1},{25,9},{2,18},{10... | collective-permute-start | bytes 3538952 | tf_op jit(solution)/shard_map/ppermute | solution.py:264
  251.9 27.7 %collective-permute-start.26 = (bf16[72,768]{1,0:T(8,128)(2,1)S(1)}, bf16[72,768]{1,0:T(8,128)(2,1)S(1)}, u32[]{:S(2)}, u32[]{:S(2)}) collective-permute-start(bf16[72,768]{1,0:T(8,128)(2,1)S(1)} %get-tuple-element.145), channel_id=1, source_target_pairs={{0,8},{8,0},{16,24},{24,16},{1,9},{9,1},{17,25},{25,17},{2,10},{10... | collective-permute-start | bytes 331784 | tf_op jit(solution)/shard_map/ppermute | solution.py:264
  252.4 49.2 %collective-permute-start.27 = (bf16[72,768]{1,0:T(8,128)(2,1)S(1)}, bf16[72,768]{1,0:T(8,128)(2,1)S(1)}, u32[]{:S(2)}, u32[]{:S(2)}) collective-permute-start(bf16[72,768]{1,0:T(8,128)(2,1)S(1)} %get-tuple-element.144), channel_id=1, source_target_pairs={{0,16},{8,24},{16,0},{24,8},{1,17},{9,25},{17,1},{25,9},{2,18},{10... | collective-permute-start | bytes 331784 | tf_op jit(solution)/shard_map/ppermute | solution.py:264
  253.4 51.3 %collective-permute-start.19 = (bf16[256,2304]{1,0:T(8,128)(2,1)}, bf16[256,2304]{1,0:T(8,128)(2,1)}, u32[]{:S(2)}, u32[]{:S(2)}) collective-permute-start(bf16[256,2304]{1,0:T(8,128)(2,1)} %get-tuple-element.218), channel_id=1, source_target_pairs={{0,24},{8,16},{16,8},{24,0},{1,25},{9,17},{17,9},{25,1},{2,26},{10... | collective-permute-start | bytes 3538952 | tf_op jit(solution)/shard_map/ppermute | solution.py:264
  279.6 22.0 %collective-permute-start.28 = (bf16[72,768]{1,0:T(8,128)(2,1)S(1)}, bf16[72,768]{1,0:T(8,128)(2,1)S(1)}, u32[]{:S(2)}, u32[]{:S(2)}) collective-permute-start(bf16[72,768]{1,0:T(8,128)(2,1)S(1)} %get-tuple-element.143), channel_id=1, source_target_pairs={{0,24},{8,16},{16,8},{24,0},{1,25},{9,17},{17,9},{25,1},{2,26},{10... | collective-permute-start | bytes 331784 | tf_op jit(solution)/shard_map/ppermute | solution.py:264
  302.5 562.4 %reduce-scatter.15.cloned.1.call-start = ((), (), s32[]{:S(2)}) async-start(), calls=%async_computation.17 | async-start | bytes 3981312 | tf_op jit(solution)/shard_map/reduce_scatter | solution.py:313
  386.2 79.5 %collective-permute-start.37 = (bf16[256,1536]{1,0:T(8,128)(2,1)}, bf16[256,1536]{1,0:T(8,128)(2,1)}, u32[]{:S(2)}, u32[]{:S(2)}) collective-permute-start(bf16[256,1536]{1,0:T(8,128)(2,1)} %convolution_convert_fusion.12), channel_id=1, source_target_pairs={{0,8},{8,0},{16,24},{24,16},{1,9},{9,1},{17,25},{25,17},{2,10},{10... | collective-permute-start | bytes 2359304 | tf_op jit(solution)/shard_map/ppermute | solution.py:264
  390.6 75.1 %collective-permute-start.36 = (bf16[256,1536]{1,0:T(8,128)(2,1)}, bf16[256,1536]{1,0:T(8,128)(2,1)}, u32[]{:S(2)}, u32[]{:S(2)}) collective-permute-start(bf16[256,1536]{1,0:T(8,128)(2,1)} %convolution_convert_fusion.13), channel_id=1, source_target_pairs={{0,16},{8,24},{16,0},{24,8},{1,17},{9,25},{17,1},{25,9},{2,18},{10... | collective-permute-start | bytes 2359304 | tf_op jit(solution)/shard_map/ppermute | solution.py:264
  425.6 12.1 collective-permute-start.31
  428.2 36.3 %collective-permute-start.30 = (bf16[256,768]{1,0:T(8,128)(2,1)S(1)}, bf16[256,768]{1,0:T(8,128)(2,1)S(1)}, u32[]{:S(2)}, u32[]{:S(2)}) collective-permute-start(bf16[256,768]{1,0:T(8,128)(2,1)S(1)} %convolution_convert_fusion.20), channel_id=1, source_target_pairs={{0,16},{8,24},{16,0},{24,8},{1,17},{9,25},{17,1},{25,9},{2,18},{10... | collective-permute-start | bytes 1179656 | tf_op jit(solution)/shard_map/ppermute | solution.py:264
  430.9 33.7 %collective-permute-start.29 = (bf16[256,768]{1,0:T(8,128)(2,1)S(1)}, bf16[256,768]{1,0:T(8,128)(2,1)S(1)}, u32[]{:S(2)}, u32[]{:S(2)}) collective-permute-start(bf16[256,768]{1,0:T(8,128)(2,1)S(1)} %convolution_convert_fusion.21), channel_id=1, source_target_pairs={{0,24},{8,16},{16,8},{24,0},{1,25},{9,17},{17,9},{25,1},{2,26},{10... | collective-permute-start | bytes 1179656 | tf_op jit(solution)/shard_map/ppermute | solution.py:264
  437.6 28.1 %collective-permute-start.35 = (bf16[256,1536]{1,0:T(8,128)(2,1)S(1)}, bf16[256,1536]{1,0:T(8,128)(2,1)S(1)}, u32[]{:S(2)}, u32[]{:S(2)}) collective-permute-start(bf16[256,1536]{1,0:T(8,128)(2,1)S(1)} %convolution_convert_fusion.14), channel_id=1, source_target_pairs={{0,24},{8,16},{16,8},{24,0},{1,25},{9,17},{17,9},{25,1},{2,26},{10... | collective-permute-start | bytes 2359304 | tf_op jit(solution)/shard_map/ppermute | solution.py:264
  474.3 12.1 collective-permute-start.38
  475.1 20.2 %collective-permute-start.39 = (bf16[256,768]{1,0:T(8,128)(2,1)S(1)}, bf16[256,768]{1,0:T(8,128)(2,1)S(1)}, u32[]{:S(2)}, u32[]{:S(2)}) collective-permute-start(bf16[256,768]{1,0:T(8,128)(2,1)S(1)} %get-tuple-element.122), channel_id=1, source_target_pairs={{0,16},{8,24},{16,0},{24,8},{1,17},{9,25},{17,1},{25,9},{2,18},{10... | collective-permute-start | bytes 1179656 | tf_op jit(solution)/shard_map/ppermute | solution.py:264
  476.6 19.2 %collective-permute-start.40 = (bf16[256,768]{1,0:T(8,128)(2,1)S(1)}, bf16[256,768]{1,0:T(8,128)(2,1)S(1)}, u32[]{:S(2)}, u32[]{:S(2)}) collective-permute-start(bf16[256,768]{1,0:T(8,128)(2,1)S(1)} %get-tuple-element.122), channel_id=1, source_target_pairs={{0,24},{8,16},{16,8},{24,0},{1,25},{9,17},{17,9},{25,1},{2,26},{10... | collective-permute-start | bytes 1179656 | tf_op jit(solution)/shard_map/ppermute | solution.py:264
  479.8 32.0 %collective-permute-start.41 = (bf16[256,1536]{1,0:T(8,128)(2,1)S(1)}, bf16[256,1536]{1,0:T(8,128)(2,1)}, u32[]{:S(2)}, u32[]{:S(2)}) collective-permute-start(bf16[256,1536]{1,0:T(8,128)(2,1)S(1)} %get-tuple-element.120), channel_id=1, source_target_pairs={{0,8},{8,0},{16,24},{24,16},{1,9},{9,1},{17,25},{25,17},{2,10},{10... | collective-permute-start | bytes 2359304 | tf_op jit(solution)/shard_map/ppermute | solution.py:264
  480.9 45.3 %collective-permute-start.42 = (bf16[256,1536]{1,0:T(8,128)(2,1)S(1)}, bf16[256,1536]{1,0:T(8,128)(2,1)}, u32[]{:S(2)}, u32[]{:S(2)}) collective-permute-start(bf16[256,1536]{1,0:T(8,128)(2,1)S(1)} %get-tuple-element.120), channel_id=1, source_target_pairs={{0,16},{8,24},{16,0},{24,8},{1,17},{9,25},{17,1},{25,9},{2,18},{10... | collective-permute-start | bytes 2359304 | tf_op jit(solution)/shard_map/ppermute | solution.py:264
  486.3 42.0 %collective-permute-start.43 = (bf16[256,1536]{1,0:T(8,128)(2,1)S(1)}, bf16[256,1536]{1,0:T(8,128)(2,1)}, u32[]{:S(2)}, u32[]{:S(2)}) collective-permute-start(bf16[256,1536]{1,0:T(8,128)(2,1)S(1)} %get-tuple-element.120), channel_id=1, source_target_pairs={{0,24},{8,16},{16,8},{24,0},{1,25},{9,17},{17,9},{25,1},{2,26},{10... | collective-permute-start | bytes 2359304 | tf_op jit(solution)/shard_map/ppermute | solution.py:264
  628.5 29.2 %collective-permute-start.46 = (bf16[256,2304]{1,0:T(8,128)(2,1)}, bf16[256,2304]{1,0:T(8,128)(2,1)}, u32[]{:S(2)}, u32[]{:S(2)}) collective-permute-start(bf16[256,2304]{1,0:T(8,128)(2,1)} %get-tuple-element.86), channel_id=1, source_target_pairs={{0,8},{8,0},{16,24},{24,16},{1,9},{9,1},{17,25},{25,17},{2,10},{10... | collective-permute-start | bytes 3538952 | tf_op jit(solution)/shard_map/ppermute | solution.py:264
  629.6 50.8 %collective-permute-start.45 = (bf16[256,2304]{1,0:T(8,128)(2,1)}, bf16[256,2304]{1,0:T(8,128)(2,1)}, u32[]{:S(2)}, u32[]{:S(2)}) collective-permute-start(bf16[256,2304]{1,0:T(8,128)(2,1)} %get-tuple-element.87), channel_id=1, source_target_pairs={{0,16},{8,24},{16,0},{24,8},{1,17},{9,25},{17,1},{25,9},{2,18},{10... | collective-permute-start | bytes 3538952 | tf_op jit(solution)/shard_map/ppermute | solution.py:264
  632.1 48.2 %collective-permute-start.44 = (bf16[256,2304]{1,0:T(8,128)(2,1)}, bf16[256,2304]{1,0:T(8,128)(2,1)}, u32[]{:S(2)}, u32[]{:S(2)}) collective-permute-start(bf16[256,2304]{1,0:T(8,128)(2,1)} %get-tuple-element.85), channel_id=1, source_target_pairs={{0,24},{8,16},{16,8},{24,0},{1,25},{9,17},{17,9},{25,1},{2,26},{10... | collective-permute-start | bytes 3538952 | tf_op jit(solution)/shard_map/ppermute | solution.py:264
  632.5 241.7 %reduce-scatter.9.cloned.1.call-start = ((), (), s32[]{:S(2)}) async-start(), calls=%async_computation.14 | async-start | bytes 2654208 | tf_op jit(solution)/shard_map/reduce_scatter | solution.py:313
  696.3 28.9 %collective-permute-start.47 = (bf16[256,2304]{1,0:T(8,128)(2,1)S(1)}, bf16[256,2304]{1,0:T(8,128)(2,1)}, u32[]{:S(2)}, u32[]{:S(2)}) collective-permute-start(bf16[256,2304]{1,0:T(8,128)(2,1)S(1)} %get-tuple-element.77), channel_id=1, source_target_pairs={{0,8},{8,0},{16,24},{24,16},{1,9},{9,1},{17,25},{25,17},{2,10},{10... | collective-permute-start | bytes 3538952 | tf_op jit(solution)/shard_map/ppermute | solution.py:264
  697.1 48.0 %collective-permute-start.48 = (bf16[256,2304]{1,0:T(8,128)(2,1)S(1)}, bf16[256,2304]{1,0:T(8,128)(2,1)S(1)}, u32[]{:S(2)}, u32[]{:S(2)}) collective-permute-start(bf16[256,2304]{1,0:T(8,128)(2,1)S(1)} %get-tuple-element.77), channel_id=1, source_target_pairs={{0,16},{8,24},{16,0},{24,8},{1,17},{9,25},{17,1},{25,9},{2,18},{10... | collective-permute-start | bytes 3538952 | tf_op jit(solution)/shard_map/ppermute | solution.py:264
  698.0 48.2 %collective-permute-start.49 = (bf16[256,2304]{1,0:T(8,128)(2,1)S(1)}, bf16[256,2304]{1,0:T(8,128)(2,1)S(1)}, u32[]{:S(2)}, u32[]{:S(2)}) collective-permute-start(bf16[256,2304]{1,0:T(8,128)(2,1)S(1)} %get-tuple-element.77), channel_id=1, source_target_pairs={{0,24},{8,16},{16,8},{24,0},{1,25},{9,17},{17,9},{25,1},{2,26},{10... | collective-permute-start | bytes 3538952 | tf_op jit(solution)/shard_map/ppermute | solution.py:264
  753.5 126.1 %reduce-scatter.7.cloned.1.call-start = ((), (), s32[]{:S(2)}) async-start(), calls=%async_computation.13 | async-start | bytes 5308416 | tf_op jit(solution)/shard_map/reduce_scatter | solution.py:313
  778.5 146.5 %reduce-scatter.17.cloned.1.call-start = ((), (), s32[]{:S(2)}) async-start(), calls=%async_computation.18 | async-start | bytes 7962624 | tf_op jit(solution)/shard_map/reduce_scatter | solution.py:313
  779.1 257.3 %reduce-scatter.13.cloned.1.call-start = ((), (), s32[]{:S(2)}) async-start(), calls=%async_computation.16 | async-start | bytes 11943936 | tf_op jit(solution)/shard_map/reduce_scatter | solution.py:313
  779.8 367.8 %reduce-scatter.11.cloned.1.call-start = ((), (), s32[]{:S(2)}) async-start(), calls=%async_computation.15 | async-start | bytes 11943936 | tf_op jit(solution)/shard_map/reduce_scatter | solution.py:313
  785.4 29.2 %collective-permute-start.52 = (bf16[256,2304]{1,0:T(8,128)(2,1)}, bf16[256,2304]{1,0:T(8,128)(2,1)}, u32[]{:S(2)}, u32[]{:S(2)}) collective-permute-start(bf16[256,2304]{1,0:T(8,128)(2,1)} %convolution_convert_fusion.6), channel_id=1, source_target_pairs={{0,8},{8,0},{16,24},{24,16},{1,9},{9,1},{17,25},{25,17},{2,10},{10... | collective-permute-start | bytes 3538952 | tf_op jit(solution)/shard_map/ppermute | solution.py:264
  791.4 49.1 %collective-permute-start.51 = (bf16[256,2304]{1,0:T(8,128)(2,1)}, bf16[256,2304]{1,0:T(8,128)(2,1)}, u32[]{:S(2)}, u32[]{:S(2)}) collective-permute-start(bf16[256,2304]{1,0:T(8,128)(2,1)} %convolution_convert_fusion.7), channel_id=1, source_target_pairs={{0,16},{8,24},{16,0},{24,8},{1,17},{9,25},{17,1},{25,9},{2,18},{10... | collective-permute-start | bytes 3538952 | tf_op jit(solution)/shard_map/ppermute | solution.py:264
  796.1 44.5 %collective-permute-start.50 = (bf16[256,2304]{1,0:T(8,128)(2,1)}, bf16[256,2304]{1,0:T(8,128)(2,1)}, u32[]{:S(2)}, u32[]{:S(2)}) collective-permute-start(bf16[256,2304]{1,0:T(8,128)(2,1)} %convolution_convert_fusion.8), channel_id=1, source_target_pairs={{0,24},{8,16},{16,8},{24,0},{1,25},{9,17},{17,9},{25,1},{2,26},{10... | collective-permute-start | bytes 3538952 | tf_op jit(solution)/shard_map/ppermute | solution.py:264
  875.9 327.0 %collective-permute-start.56 = (bf16[16,2304]{1,0:T(8,128)(2,1)S(1)}, bf16[16,2304]{1,0:T(8,128)(2,1)S(1)}, u32[]{:S(2)}, u32[]{:S(2)}) collective-permute-start(bf16[16,2304]{1,0:T(8,128)(2,1)S(1)} %get-tuple-element.177), channel_id=1, source_target_pairs={{0,8},{8,0},{16,24},{24,16},{1,9},{9,1},{17,25},{25,17},{2,10},{10... | collective-permute-start | bytes 221192 | tf_op jit(solution)/shard_map/ppermute | solution.py:264
  877.9 326.7 %collective-permute-start.57 = (bf16[16,2304]{1,0:T(8,128)(2,1)}, bf16[16,2304]{1,0:T(8,128)(2,1)S(1)}, u32[]{:S(2)}, u32[]{:S(2)}) collective-permute-start(bf16[16,2304]{1,0:T(8,128)(2,1)} %get-tuple-element.176), channel_id=1, source_target_pairs={{0,16},{8,24},{16,0},{24,8},{1,17},{9,25},{17,1},{25,9},{2,18},{10... | collective-permute-start | bytes 221192 | tf_op jit(solution)/shard_map/ppermute | solution.py:264
  879.2 325.4 %collective-permute-start.58 = (bf16[16,2304]{1,0:T(8,128)(2,1)S(1)}, bf16[16,2304]{1,0:T(8,128)(2,1)S(1)}, u32[]{:S(2)}, u32[]{:S(2)}) collective-permute-start(bf16[16,2304]{1,0:T(8,128)(2,1)S(1)} %get-tuple-element.175), channel_id=1, source_target_pairs={{0,24},{8,16},{16,8},{24,0},{1,25},{9,17},{17,9},{25,1},{2,26},{10... | collective-permute-start | bytes 221192 | tf_op jit(solution)/shard_map/ppermute | solution.py:264
  881.6 323.1 %collective-permute-start.53 = (bf16[72,1024]{1,0:T(8,128)(2,1)}, bf16[72,1024]{1,0:T(8,128)(2,1)S(1)}, u32[]{:S(2)}, u32[]{:S(2)}) collective-permute-start(bf16[72,1024]{1,0:T(8,128)(2,1)} %get-tuple-element.134), channel_id=1, source_target_pairs={{0,8},{8,0},{16,24},{24,16},{1,9},{9,1},{17,25},{25,17},{2,10},{10... | collective-permute-start | bytes 442376 | tf_op jit(solution)/shard_map/ppermute | solution.py:264
  1038.4 111.6 %collective-permute-start.60 = (bf16[72,2304]{1,0:T(8,128)(2,1)}, bf16[72,2304]{1,0:T(8,128)(2,1)}, u32[]{:S(2)}, u32[]{:S(2)}) collective-permute-start(bf16[72,2304]{1,0:T(8,128)(2,1)} %get-tuple-element.115), channel_id=1, source_target_pairs={{0,8},{8,0},{16,24},{24,16},{1,9},{9,1},{17,25},{25,17},{2,10},{10... | collective-permute-start | bytes 995336 | tf_op jit(solution)/shard_map/ppermute | solution.py:264
  1157.7 8.5 collective-permute-start.62
  1166.3 10.7 collective-permute-start.61
  1177.0 8.8 collective-permute-start.64
  1193.8 10.8 collective-permute-start.54
  1214.7 118.2 %all-to-all-start = ((bf16[1248,8,256]{2,1,0:T(8,128)(2,1)}), bf16[1248,8,256]{2,1,0:T(8,128)(2,1)}, u32[]{:S(2)}, u32[]{:S(2)}) async-start(bf16[1248,8,256]{2,1,0:T(8,128)(2,1)} %shard_map.232), calls=%async_computation.6 | async-start | bytes 10223616 | tf_op jit(solution)/shard_map/all_to_all | solution.py:585
  (107 other events, 1918.0 us)
Sparse Core Ops, SparseCore 0:
  21.4 51.5 all-gather.6
  75.2 30.3 all-gather.8
  107.8 99.6 all-gather.10
  209.6 98.7 all-gather.12
  310.4 69.5 all-gather.16
  382.1 40.0 all-gather.14
  632.6 42.7 reduce-scatter.14
  753.6 36.2 reduce-scatter.8
  792.9 53.6 reduce-scatter.6
  849.3 75.6 reduce-scatter.16
  927.3 109.0 reduce-scatter.12
  1038.5 109.0 reduce-scatter.10

commit v3 on v2

--- a/solution.py
+++ b/solution.py
@@ -147,41 +147,47 @@
     )(length, prefix, merged, upstream)
 
 
-def place_kernel(layout, devices, stride, slots_ref, *refs):
-    pieces, extra, out = refs[: len(layout)], refs[len(layout)], refs[len(layout) + 1]
-    out[...] = jnp.zeros_like(out)
+def place_kernel(layout, devices, sizes, slots_ref, *refs):
+    count = len(refs) - 4
+    pieces, extra, out_one, out_two, flat = refs[:count], refs[count], *refs[count + 1 :]
+    flat[...] = jnp.zeros_like(flat)
+    split = devices * sizes[0]
 
     @pl.loop(0, devices)
     def _(at):
-        out[at * stride + stride - 1] = extra[at]
+        flat[split + (at + 1) * sizes[1] - 1] = extra[at]
 
     seq_index = slots_ref[slots_ref.shape[0] - 1]
-    for piece, (turn, base, per_row, columns) in zip(pieces, layout):
+    for index, turn, base, per_row, columns in layout:
+        piece = pieces[index]
         source = jnp.bitwise_xor(seq_index, turn)
 
         @pl.loop(0, piece.shape[0])
         def _(a, piece=piece, base=base, per_row=per_row, columns=columns, source=source):
-            for local, (fixed, factor, row_factor) in enumerate(columns):
+            for local, fixed, factor, row_factor in columns:
                 block = base + (a + source * row_factor) * per_row + fixed + source * factor
-                out[slots_ref[block]] = piece[a, :, local * BLK : (local + 1) * BLK]
-
-
-def place_pieces(pieces, extra, slots, seq_index, layout, devices, stride):
+                flat[slots_ref[block]] = piece[a, :, local * BLK : (local + 1) * BLK]
+
+    out_one[...] = flat[:split]
+    out_two[...] = flat[split:]
+
+
+def place_pieces(pieces, extra, slots, seq_index, layout, devices, sizes):
     share = extra.shape[1]
     table = jnp.concatenate([slots, seq_index[None]]).astype(jnp.int32)
     return pl.pallas_call(
-        functools.partial(place_kernel, layout, devices, stride),
-        out_shape=jax.ShapeDtypeStruct((devices * stride, share, BLK), BF16),
+        functools.partial(place_kernel, layout, devices, sizes),
+        out_shape=tuple(jax.ShapeDtypeStruct((devices * size, share, BLK), BF16) for size in sizes),
         in_specs=[SMEM_SPEC] + [VMEM_SPEC] * (len(pieces) + 1),
-        out_specs=VMEM_SPEC,
+        out_specs=(VMEM_SPEC, VMEM_SPEC),
+        scratch_shapes=[pltpu.VMEM((devices * sum(sizes), share, BLK), BF16)],
         compiler_params=pltpu.CompilerParams(vmem_limit_bytes=48 << 20),
         cost_estimate=pl.CostEstimate(flops=0, bytes_accessed=12 << 20, transcendentals=0),
     )(table, *pieces, extra)
 
 
-def soap_kernel(
-    group, incoming, first, second, left, right, master, first_out, second_out, weight_out
-):
+def soap_kernel(group, incoming, first, second, left, right, master, *outs):
+    first_out, second_out, weight_out = outs[-3:]
     for at in range(group):
         if len(incoming.shape) == 4:
             grad = incoming[:, at].astype(F32).reshape(BLK, BLK)
@@ -202,30 +208,31 @@
         weight_out[at] = master[at] - STEP_RATE * dot_nt(back_left, right_low)
 
 
-def soap(incoming, first, second, left, right, master):
-    capacity = first.shape[0]
-    group = 2 if capacity % 2 == 0 else 1
-    spec = pl.BlockSpec((group, BLK, BLK), lambda at: (at, 0, 0))
+def soap(incoming, state, begin, count, earlier):
+    capacity = state[0].shape[0]
+    group = 2 if begin % 2 == 0 and count % 2 == 0 else 1
+    spec = pl.BlockSpec((group, BLK, BLK), lambda at: (at + begin // group, 0, 0))
     if incoming.ndim == 4:
         grad_spec = pl.BlockSpec(
             (incoming.shape[0], group) + incoming.shape[2:], lambda at: (0, at, 0, 0)
         )
     else:
-        grad_spec = spec
-    shape = jax.ShapeDtypeStruct(first.shape, F32)
+        grad_spec = pl.BlockSpec((group, BLK, BLK), lambda at: (at, 0, 0))
+    shape = jax.ShapeDtypeStruct((capacity, BLK, BLK), F32)
     return pl.pallas_call(
         functools.partial(soap_kernel, group),
-        grid=(capacity // group,),
+        grid=(count // group,),
         out_shape=(shape, shape, shape),
-        in_specs=[grad_spec] + [spec] * 5,
+        in_specs=[grad_spec] + [spec] * 5 + [pl.BlockSpec(memory_space=pl.ANY)] * len(earlier),
         out_specs=(spec, spec, spec),
+        input_output_aliases={6 + at: at for at in range(len(earlier))},
         compiler_params=pltpu.CompilerParams(vmem_limit_bytes=48 << 20),
         cost_estimate=pl.CostEstimate(
-            flops=8 * capacity * BLK**3,
-            bytes_accessed=34 * capacity * BLK * BLK,
-            transcendentals=2 * capacity * BLK * BLK,
+            flops=8 * count * BLK**3,
+            bytes_accessed=34 * count * BLK * BLK,
+            transcendentals=2 * count * BLK * BLK,
         ),
-    )(incoming, first, second, left, right, master)
+    )(incoming, *state, *earlier)
 
 
 def body(
@@ -257,8 +264,9 @@
     key_slice = KEY_FEATURES // seq_count
     ff_slice = FF // seq_count
     d_groups = D // BLK
-    half = ff_slice // 2
-    parts = (slice(0, D // 3), slice(D // 3, D))
+    cut = D * 5 // 18
+    parts = (slice(0, cut), slice(cut, D))
+    qkv_slice = query_slice + 2 * key_slice
 
     def swap(value, turn):
         return lax.ppermute(value, "seq", [(at, at ^ turn) for at in range(seq_count)])
@@ -342,26 +350,31 @@
     down_low = local_rows(down_weight)
     gain_full = double_gather(norm_gains.astype(BF16).reshape(1, -1)).reshape(D, 4)
 
+    def out_piece(target):
+        piece = pick(out_low, target, heads, 0).reshape(heads, share, d_groups, BLK)
+        return jnp.transpose(piece, (2, 1, 0, 3)).reshape(d_groups * share, query_slice)
+
     def qkv_piece(target):
         return jnp.concatenate(
             [
                 pick(qkv_low[:, :QUERY_FEATURES], target, query_slice, 1),
                 pick(qkv_low[:, QUERY_FEATURES : QUERY_FEATURES + KEY_FEATURES], target, key_slice, 1),
                 pick(qkv_low[:, QUERY_FEATURES + KEY_FEATURES :], target, key_slice, 1),
+                out_piece(target),
             ],
             axis=1,
         )
-
-    def out_piece(target):
-        return pick(out_low, target, heads, 0).reshape(heads * share, D)
 
     def down_piece(part):
         return lambda target: pick(down_low[..., part], target, d_groups, 0).reshape(
             d_groups * share, -1
         )
 
-    qkv_slice_full = spread(qkv_piece)
-    out_slice_full = spread(out_piece)
+    heads_full = spread(qkv_piece)
+    qkv_slice_full = heads_full[:, :qkv_slice]
+    out_slice_full = jnp.transpose(
+        heads_full[:, qkv_slice:].reshape(-1, d_groups, share, heads, BLK), (0, 3, 2, 1, 4)
+    ).reshape(query_slice, D)
 
     geglu_rows = jnp.transpose(
         geglu_weight.astype(BF16).reshape(share, d_groups, 2 * seq_count, ff_slice), (2, 1, 0, 3)
@@ -370,23 +383,16 @@
         2 * seq_count, d_groups * share, ff_slice
     )
 
-    def geglu_piece(part):
-        cols = slice(part * half, (part + 1) * half)
-
-        def piece(target):
-            return jnp.concatenate(
-                [
-                    lax.dynamic_index_in_dim(geglu_turned, target, 0, False)[:, cols],
-                    lax.dynamic_index_in_dim(geglu_turned, target + seq_count, 0, False)[:, cols],
-                ],
-                axis=1,
-            )
-
-        return piece
-
-    geglu_zero = spread(geglu_piece(0))
-    geglu_one = spread(geglu_piece(1))
-    geglu_parts = (geglu_zero, geglu_one)
+    def geglu_piece(target):
+        return jnp.concatenate(
+            [
+                lax.dynamic_index_in_dim(geglu_turned, target, 0, False),
+                lax.dynamic_index_in_dim(geglu_turned, target + seq_count, 0, False),
+            ],
+            axis=1,
+        )
+
+    geglu_full = spread(geglu_piece)
     down_late = spread(down_piece(parts[1]))
     down_early = spread(down_piece(parts[0]))
 
@@ -404,15 +410,9 @@
     ffn_turned = dot(ffn_normed.astype(BF16), wide_order).astype(BF16)
     ffn_all = gather_rows(ffn_turned)
 
-    gates, uppers, products = [], [], []
-    for part in range(2):
-        gate_up = dot(ffn_all, geglu_parts[part])
-        gate, upper = gate_up[:, :half], gate_up[:, half:]
-        gates.append(gate)
-        uppers.append(upper)
-        products.append((jax.nn.gelu(gate, approximate=True) * upper).astype(BF16))
-
-    product = jnp.concatenate(products, axis=1)
+    gate_up = dot(ffn_all, geglu_full)
+    gate, upper = gate_up[:, :ff_slice], gate_up[:, ff_slice:]
+    product = (jax.nn.gelu(gate, approximate=True) * upper).astype(BF16)
 
     def branch_columns(weight):
         def part_of(owner):
@@ -437,23 +437,15 @@
         down_terms.append(dot_tn(product, value).astype(BF16))
     down_sums = [collect(term) for term in down_terms]
     branch_alls = after(branch_alls, down_terms)
-    gate_up_grads = []
-    geglu_terms = []
-    for part in range(2):
-        ff_rows = slice(part * half, (part + 1) * half)
-        grad_product = dot_nt(branch_alls[0], down_early[ff_rows]) + dot_nt(
-            branch_alls[1], down_late[ff_rows]
-        )
-        activated, gelu_pull = jax.vjp(lambda value: jax.nn.gelu(value, approximate=True), gates[part])
-        grad_gate = gelu_pull(grad_product * uppers[part])[0]
-        grad_upper = grad_product * activated
-        gate_up_grad = jnp.concatenate([grad_gate, grad_upper], axis=1).astype(BF16)
-        geglu_terms.append(dot_tn(ffn_all, gate_up_grad).astype(BF16))
-        if part == 0:
-            branch_alls = after(branch_alls, [geglu_terms[0]])
-        gate_up_grads.append(gate_up_grad)
-    geglu_sums = [collect(term) for term in geglu_terms]
-    ffn_total = dot_nt(gate_up_grads[0], geglu_zero) + dot_nt(gate_up_grads[1], geglu_one)
+    grad_product = dot_nt(branch_alls[0], down_early) + dot_nt(branch_alls[1], down_late)
+    activated, gelu_pull = jax.vjp(lambda value: jax.nn.gelu(value, approximate=True), gate)
+    grad_gate = gelu_pull(grad_product * upper)[0]
+    grad_upper = grad_product * activated
+    gate_up_grad = jnp.concatenate([grad_gate, grad_upper], axis=1).astype(BF16)
+    geglu_term = dot_tn(ffn_all, gate_up_grad).astype(BF16)
+    geglu_sums = collect(geglu_term)
+    (gate_up_grad,) = after([gate_up_grad], [geglu_term])
+    ffn_total = dot_nt(gate_up_grad, geglu_full)
 
     def ffn_part(owner):
         return pick(ffn_total, owner, rows, 0)
@@ -463,14 +455,16 @@
     grad_hidden = upstream + grad_hidden_norm
     grad_attended, gain_two = norm_backward(attended, inverse_two, gains[:, 1], grad_hidden)
     attended_all = gather_rows(grad_attended.astype(BF16))
-    (attended_all,) = after([attended_all], [geglu_terms[1]])
     grad_mixed_turned = dot_nt(attended_all, out_slice_full).astype(BF16)
     grad_mixed = dot_nt(grad_mixed_turned, head_order).astype(BF16)
     out_term = dot_tn(mixed_turned, attended_all).astype(BF16)
-    out_sums = collect(out_term)
-    (grad_mixed,) = after([grad_mixed], [out_term])
+    out_blocks = jnp.transpose(
+        out_term.reshape(-1, heads, share, d_groups, BLK), (0, 3, 2, 1, 4)
+    ).reshape(D, query_slice)
+    (grad_mixed, out_blocks) = after([grad_mixed, out_blocks], [])
     grad_merged = attention_backward(merged, grad_mixed, seq_lengths, prefix_lengths, heads)
-    qkv_sums = collect(dot_tn(normed_all, grad_merged).astype(BF16))
+    qkv_term = dot_tn(normed_all, grad_merged).astype(BF16)
+    heads_sums = collect(jnp.concatenate([qkv_term, out_blocks], axis=1))
     grad_normed = dot_nt(
         scatter_rows(lambda owner: dot_nt(pick(grad_merged, owner, rows, 0), qkv_slice_full)).astype(BF16),
         wide_order,
@@ -480,11 +474,7 @@
 
     turned = jnp.concatenate(
         [
-            jnp.concatenate(
-                [geglu_sums[0][turn][:, side * half : (side + 1) * half],
-                 geglu_sums[1][turn][:, side * half : (side + 1) * half]],
-                axis=1,
-            )
+            geglu_sums[turn][:, side * ff_slice : (side + 1) * ff_slice]
             for turn in range(seq_count)
             for side in range(2)
         ],
@@ -494,8 +484,7 @@
     geglu_natural = geglu_natural.reshape(
         seq_count, 2, d_groups, share, ff_slice
     )
-    qkv_local = [value.reshape(d_groups, share, -1) for value in qkv_sums]
-    out_local = [value.reshape(heads, share, D) for value in out_sums]
+    heads_local = [value.reshape(d_groups, share, -1) for value in heads_sums]
     down_local = [
         jnp.concatenate([early, late], axis=1).reshape(d_groups, share, D)
         for early, late in zip(*down_sums)
@@ -504,10 +493,15 @@
     def in_order(items):
         return assemble([item[None] for item in items])
 
-    qkv_slices = in_order(qkv_local)
-    out_grad = jnp.transpose(
-        in_order(out_local).reshape(QUERY_FEATURES // BLK, share, D), (1, 0, 2)
-    ).astype(F32)
+    qkv_slices = in_order(heads_local)
+    out_grad = (
+        jnp.transpose(
+            qkv_slices[..., qkv_slice:].reshape(seq_count, d_groups, share, heads, BLK),
+            (2, 0, 3, 1, 4),
+        )
+        .reshape(share, QUERY_FEATURES // BLK, D)
+        .astype(F32)
+    )
     down_grad = jnp.transpose(in_order(down_local).reshape(FF // BLK, share, D), (1, 0, 2)).astype(F32)
 
     def columns(value):
@@ -517,7 +511,7 @@
         [
             columns(qkv_slices[..., :query_slice]),
             columns(qkv_slices[..., query_slice : query_slice + key_slice]),
-            columns(qkv_slices[..., query_slice + key_slice :]),
+            columns(qkv_slices[..., query_slice + key_slice : qkv_slice]),
         ],
         axis=-1,
     ).astype(F32)
@@ -526,10 +520,16 @@
 
     devices = lax.axis_size(ALL)
     capacity = first_moment.shape[0]
-    stride = capacity + 1
+    early = capacity * 3 // 8 * 2
+    sizes = (early, capacity - early + 1)
     number = jnp.arange(block_owners.shape[0], dtype=jnp.int32)
     same = (block_owners[:, None] == block_owners[None, :]) & (number[None, :] < number[:, None])
-    slots = block_owners * stride + jnp.sum(same.astype(jnp.int32), axis=1)
+    rank = jnp.sum(same.astype(jnp.int32), axis=1)
+    slots = jnp.where(
+        rank < early,
+        block_owners * early + rank,
+        devices * early + block_owners * sizes[1] + rank - early,
+    )
 
     gain_term = jnp.stack([gain_one, gain_two, gain_three, gain_four], axis=1)
     gain_share = D // devices
@@ -547,27 +547,31 @@
     if share % 8 == 0:
         pieces, layout = [], []
         query_blocks, key_blocks = query_slice // BLK, key_slice // BLK
+        wide = (QUERY_FEATURES + 2 * KEY_FEATURES) // BLK
+        d_blocks = D // BLK
         for turn in range(seq_count):
-            qkv_columns = [(at, query_blocks, 0) for at in range(query_blocks)]
-            for begin in (QUERY_FEATURES, QUERY_FEATURES + KEY_FEATURES):
-                qkv_columns += [(begin // BLK + at, key_blocks, 0) for at in range(key_blocks)]
-            pieces.append(qkv_local[turn])
-            layout.append((turn, 0, (QUERY_FEATURES + 2 * KEY_FEATURES) // BLK, qkv_columns))
-            pieces.append(out_local[turn])
-            layout.append((turn, out_base, D // BLK, [(at, 0, heads) for at in range(D // BLK)]))
+            qkv_columns = [(at, at, query_blocks, 0) for at in range(query_blocks)]
+            for kind, begin in enumerate((QUERY_FEATURES, QUERY_FEATURES + KEY_FEATURES)):
+                qkv_columns += [
+                    (query_blocks + kind * key_blocks + at, begin // BLK + at, key_blocks, 0)
+                    for at in range(key_blocks)
+                ]
+            out_columns = [
+                (qkv_slice // BLK + at, at * d_blocks, heads * d_blocks, 0) for at in range(heads)
+            ]
+            layout.append((len(pieces), turn, 0, wide, qkv_columns))
+            layout.append((len(pieces), turn, out_base, 1, out_columns))
+            pieces.append(heads_local[turn])
             for side in range(2):
+                side_columns = [
+                    (at, side * FF // BLK + at, ff_blocks, 0) for at in range(ff_blocks)
+                ]
+                layout.append((len(pieces), turn, geglu_base, 2 * FF // BLK, side_columns))
                 pieces.append(geglu_natural[turn, side])
-                layout.append(
-                    (
-                        turn,
-                        geglu_base,
-                        2 * FF // BLK,
-                        [(side * FF // BLK + at, ff_blocks, 0) for at in range(ff_blocks)],
-                    )
-                )
+            down_columns = [(at, at, 0, d_groups) for at in range(d_blocks)]
+            layout.append((len(pieces), turn, down_base, d_blocks, down_columns))
             pieces.append(down_local[turn])
-            layout.append((turn, down_base, D // BLK, [(at, 0, d_groups) for at in range(D // BLK)]))
-        outgoing = place_pieces(pieces, extra, slots, seq_index, layout, devices, stride)
+        outgoing = place_pieces(pieces, extra, slots, seq_index, layout, devices, sizes)
     else:
 
         def to_pieces(gradient):
@@ -579,21 +583,30 @@
             [to_pieces(qkv_grad), to_pieces(out_grad), to_pieces(geglu_grad), to_pieces(down_grad)],
             axis=0,
         )
-        outgoing = jnp.zeros((devices * stride, share, BLK), BF16).at[slots].set(every)
-        outgoing = outgoing.at[jnp.arange(devices) * stride + capacity].set(extra)
-
-    incoming = lax.all_to_all(outgoing, ALL, split_axis=0, concat_axis=0, tiled=True).reshape(
-        devices, stride, share, BLK
-    )
-    gain_parts = incoming[:, capacity].reshape(devices, room)[:, : 2 * gain_share * 4].astype(F32)
-    gain_sums = jnp.sum(gain_parts, axis=0)
+        split = devices * early
+        flat = jnp.zeros((devices * sum(sizes), share, BLK), BF16).at[slots].set(every)
+        flat = flat.at[split + (jnp.arange(devices) + 1) * sizes[1] - 1].set(extra)
+        outgoing = (flat[:split], flat[split:])
+
+    def exchange(value):
+        moved = lax.all_to_all(value, ALL, split_axis=0, concat_axis=0, tiled=True)
+        return moved.reshape(devices, -1, share, BLK)
+
+    def blocks_of(value, count):
+        if share % 8 == 0:
+            return value
+        return jnp.transpose(value[:, :count], (1, 0, 2, 3)).reshape(count, BLK, BLK)
+
+    incoming_one = exchange(outgoing[0])
+    later, incoming_one = lax.optimization_barrier((outgoing[1], incoming_one))
+    incoming_two = exchange(later)
+    gain_parts = incoming_two[:, sizes[1] - 1].reshape(devices, room)[:, : 2 * gain_share * 4]
+    gain_sums = jnp.sum(gain_parts.astype(F32), axis=0)
     gains_grad = (gain_sums[: gain_share * 4] + gain_sums[gain_share * 4 :]).reshape(gain_share, 4)
-    if share % 8 == 0:
-        grads = incoming
-    else:
-        grads = jnp.transpose(incoming[:, :capacity], (1, 0, 2, 3)).reshape(capacity, BLK, BLK)
+    state = (first_moment, second_moment, left_basis, right_basis, slot_weight)
+    updated = soap(blocks_of(incoming_one, early), state, 0, early, ())
     first_new, second_new, weight_new = soap(
-        grads, first_moment, second_moment, left_basis, right_basis, slot_weight
+        blocks_of(incoming_two, capacity - early), state, early, capacity - early, updated
     )
     return (
         layer_out[None],

time: 1380 us -> 1270 us (0.920)
  waiting for transfers between devices: 820 us -> 685 us
    reduce_scatter x6 -> x4, waiting for transfers between devices: 237 us -> 184 us  [collect(): summed = lax.psum_scatter(gradient, 'dp', scatter_dimension=0, tiled=True)]
    all_gather x6 -> x4, waiting for transfers between devices: 60.9 us -> 25.6 us  [spread(): return lax.all_gather(operand, 'dp', axis=0, tiled=True)]
    all_to_all x1 -> x2, waiting for transfers between devices: 105 us -> 72.9 us  [exchange(): moved = lax.all_to_all(value, ALL, split_axis=0, concat_axis=0, tiled=True)]
    ppermute x66 -> x54, starting transfers between devices: 91 us -> 70.5 us  [swap(): lax.ppermute(value, 'seq', [(at, at ^ turn) for at in range(seq_count)])]
    concatenate x7 -> x5, other arithmetic: 0.18 us -> 15.6 us  [the longest x1 8.97 us: body(): gate_up_grad = jnp.concatenate([grad_gate, grad_upper], axis=1).astype(BF16)]
    ppermute x66 -> x54, waiting for transfers between devices: 404 us -> 394 us  [swap(): lax.ppermute(value, 'seq', [(at, at ^ turn) for at in range(seq_count)])]
    dot_general x19 -> x18, matrix products: 86.2 us -> 92.2 us  [dot(): return jnp.dot(left, right, preferred_element_type=F32)]
    unnamed x182 -> x159, local copies, waits for them, and re-layouts: 31.7 us -> 35.8 us
  transfers between devices with their start and end apart: 84 -> 69, of which waited for: 50 -> 42; matrix products, arithmetic and copies ran while one was open for 18% -> 30% of each run, Pallas kernels for 1% -> 3%
where the time goes in v3:
time: 1270 us; the launch traced here: 1260 us
  waiting for transfers between devices  685 us (54%)
  matrix products  262 us (21%)
  local copies, waits for them, and re-layouts  104 us (8%)
  starting transfers between devices  89.5 us (7%)
  Pallas kernels  52.8 us (4%)
  other arithmetic  48 us (4%)
  between operations  17.6 us (1%)
    ppermute x54, waiting for transfers between devices, swap(): lax.ppermute(value, 'seq', [(at, at ^ turn) for at in range(seq_count)])  394 us
    reduce_scatter x4, waiting for transfers between devices, collect(): summed = lax.psum_scatter(gradient, 'dp', scatter_dimension=0, tiled=True)  184 us
    dot_general x10, matrix products, dot_nt(): lax.dot_general(left, right, (((1,), (1,)), ((), ())), preferred_element_...  109 us
    dot_general x18, matrix products, dot(): return jnp.dot(left, right, preferred_element_type=F32)  92.2 us
    all_to_all x2, waiting for transfers between devices, exchange(): moved = lax.all_to_all(value, ALL, split_axis=0, concat_axis=0, tiled=True)  72.9 us
    ppermute x54, starting transfers between devices, swap(): lax.ppermute(value, 'seq', [(at, at ^ turn) for at in range(seq_count)])  70.5 us
    dot_general x5, matrix products, dot_tn(): lax.dot_general(left, right, (((0,), (0,)), ((), ())), preferred_element_...  61.1 us
    unnamed x159, local copies, waits for them, and re-layouts  35.8 us
  transfers between devices with their start and end apart: 69, of which 42 were waited for; matrix products, arithmetic and copies ran while one was open for 30% of the time, Pallas kernels for 3%

profile of v3, /device:TPU:0, one launch (start us, length us, event | category | flops | bytes accessed | tf_op | source)
XLA Modules:
  0.0 1259.5 jit_solution(7124605604908808781)
XLA Ops:
  14.4 4.2 collective-permute-done.8
  18.6 5.5 collective-permute-done.9
  28.9 8.7 fusion.20
  41.9 13.8 %collective-permute-done.17 = bf16[72,4608]{1,0:T(8,128)(2,1)S(1)} collective-permute-done((bf16[72,4608]{1,0:T(8,128)(2,1)S(1)}, bf16[72,4608]{1,0:T(8,128)(2,1)S(1)}, u32[]{:S(2)}, u32[]{:S(2)}) %collective-permute-start.17) | collective-permute-done | bytes 663584 | tf_op jit(solution)/shard_map/ppermute | solution.py:272
  55.8 13.1 %collective-permute-done.18 = bf16[72,4608]{1,0:T(8,128)(2,1)S(1)} collective-permute-done((bf16[72,4608]{1,0:T(8,128)(2,1)S(1)}, bf16[72,4608]{1,0:T(8,128)(2,1)S(1)}, u32[]{:S(2)}, u32[]{:S(2)}) %collective-permute-start.18) | collective-permute-done | bytes 663584 | tf_op jit(solution)/shard_map/ppermute | solution.py:272
  78.1 4.7 collective-permute-done.26
  111.2 5.5 constant_dynamic-update-slice_fusion.37
  121.5 24.0 %collective-permute-done.5 = bf16[256,2304]{1,0:T(8,128)(2,1)S(1)} collective-permute-done((bf16[256,2304]{1,0:T(8,128)(2,1)S(1)}, bf16[256,2304]{1,0:T(8,128)(2,1)S(1)}, u32[]{:S(2)}, u32[]{:S(2)}) %collective-permute-start.5) | collective-permute-done | bytes 1179680 | tf_op jit(solution)/shard_map/ppermute | solution.py:272
  146.7 20.5 %collective-permute-done.6 = bf16[256,2304]{1,0:T(8,128)(2,1)S(1)} collective-permute-done((bf16[256,2304]{1,0:T(8,128)(2,1)S(1)}, bf16[256,2304]{1,0:T(8,128)(2,1)S(1)}, u32[]{:S(2)}, u32[]{:S(2)}) %collective-permute-start.6) | collective-permute-done | bytes 1179680 | tf_op jit(solution)/shard_map/ppermute | solution.py:272
  172.7 5.1 reshape.435
  178.2 9.1 fusion.55.merged_ref
  187.4 3.8 shard_map.230
  197.8 25.4 %collective-permute-done.13 = bf16[256,2304]{1,0:T(8,128)(2,1)S(1)} collective-permute-done((bf16[256,2304]{1,0:T(8,128)(2,1)S(1)}, bf16[256,2304]{1,0:T(8,128)(2,1)S(1)}, u32[]{:S(2)}, u32[]{:S(2)}) %collective-permute-start.13) | collective-permute-done | bytes 1179680 | tf_op jit(solution)/shard_map/ppermute | solution.py:272
  223.2 18.2 %collective-permute-done.12 = bf16[256,2304]{1,0:T(8,128)(2,1)S(1)} collective-permute-done((bf16[256,2304]{1,0:T(8,128)(2,1)S(1)}, bf16[256,2304]{1,0:T(8,128)(2,1)S(1)}, u32[]{:S(2)}, u32[]{:S(2)}) %collective-permute-start.12) | collective-permute-done | bytes 1179680 | tf_op jit(solution)/shard_map/ppermute | solution.py:272
  247.0 10.6 constant_dynamic-update-slice_fusion.30
  264.3 24.2 %collective-permute-done.20 = bf16[72,640]{1,0:T(8,128)(2,1)S(1)} collective-permute-done((bf16[72,640]{1,0:T(8,128)(2,1)S(1)}, bf16[72,640]{1,0:T(8,128)(2,1)S(1)}, u32[]{:S(2)}, u32[]{:S(2)}) %collective-permute-start.20) | collective-permute-done | bytes 92192 | tf_op jit(solution)/shard_map/ppermute | solution.py:272
  290.1 20.5 %collective-permute-done.21 = bf16[72,640]{1,0:T(8,128)(2,1)S(1)} collective-permute-done((bf16[72,640]{1,0:T(8,128)(2,1)S(1)}, bf16[72,640]{1,0:T(8,128)(2,1)S(1)}, u32[]{:S(2)}, u32[]{:S(2)}) %collective-permute-start.21) | collective-permute-done | bytes 92192 | tf_op jit(solution)/shard_map/ppermute | solution.py:272
  318.6 26.6 %fusion.167 = f32[1024,4608]{1,0:T(8,128)S(1)} fusion(bf16[1024,2304]{1,0:T(8,128)(2,1)} %constant_dynamic-update-slice_fusion.27, bf16[2304,4608]{1,0:T(8,128)(2,1)} %all-gather.7.cloned.1.call-done), kind=kOutput, calls=%fused_computation.415 | convolution fusion | flops 21743271936 | bytes 44826624 | tf_op jit(solution)/shard_map/dot_general | solution.py:49
  345.2 6.4 copy-done.6
  351.6 4.9 multiply_convert_fusion.1
  356.5 5.2 all-gather.11.cloned.1.call-done
  361.7 6.9 convolution_convert_fusion.11
  378.5 20.4 %all-gather.9.cloned.1.call-done = bf16[2304,640]{1,0:T(8,128)(2,1)} async-done(((bf16[288,640]{1,0:T(8,128)(2,1)}), bf16[2304,640]{1,0:T(8,128)(2,1)}) %all-gather.9.cloned.1.call-update) | async-done | bytes 2949136 | tf_op jit(solution)/shard_map/all_gather | solution.py:318
  411.3 3.9 collective-permute-done.25
  417.6 9.0 collective-permute-done.24
  427.9 3.9 fusion.28
  449.4 5.2 collective-permute-done.33
  456.6 5.3 convolution_convert_fusion.3
  462.0 11.0 collective-permute-done.35
  475.1 14.0 %collective-permute-done.36 = bf16[256,1664]{1,0:T(8,128)(2,1)} collective-permute-done((bf16[256,1664]{1,0:T(8,128)(2,1)}, bf16[256,1664]{1,0:T(8,128)(2,1)}, u32[]{:S(2)}, u32[]{:S(2)}) %collective-permute-start.36) | collective-permute-done | bytes 852000 | tf_op jit(solution)/shard_map/ppermute | solution.py:272
  493.4 13.6 %convolution_convert_fusion.1 = bf16[2304,1664]{1,0:T(8,128)(2,1)} fusion(bf16[1024,2304]{1,0:T(8,128)(2,1)} %multiply_convert_fusion.1, bf16[1024,1664]{1,0:T(8,128)(2,1)} %constant_dynamic-update-slice_fusion.10), kind=kOutput, calls=%fused_computation.10 | convolution fusion | flops 7855570944 | bytes 15794176 | tf_op jit(solution)/shard_map/dot_general | solution.py:57
  507.1 14.9 %fusion.168 = f32[1024,2304]{1,0:T(8,128)} fusion(bf16[1024,1664]{1,0:T(8,128)(2,1)} %constant_dynamic-update-slice_fusion.10, bf16[2304,1664]{1,0:T(8,128)(2,1)} %all-gather.11.cloned.1.call-done), kind=kOutput, calls=%fused_computation.416 | convolution fusion | flops 7851737088 | bytes 20512768 | tf_op jit(solution)/shard_map/dot_general | solution.py:53
  522.0 18.6 %fusion.18 = (bf16[1024,2304]{1,0:T(8,128)(2,1)}, bf16[1024,2304]{1,0:T(8,128)(2,1)}) fusion(f32[1024,4608]{1,0:T(8,128)} %copy-done.6, f32[1024,2304]{1,0:T(8,128)} %fusion.168, bf16[1024,640]{1,0:T(8,128)(2,1)S(1)} %copy-done.26, bf16[2304,640]{1,0:T(8,128)(2,1)} %all-gather.9.cloned.1.call-done), kind=kOutput, calls=%fused_computation.23 | convolution fusion | flops 3078881280 | bytes 42008576 | tf_op jit(solution)/shard_map/dot_general | solution.py:53
  540.6 9.0 pad_maximum_fusion
  549.6 30.0 %convolution_convert_fusion = bf16[2304,4608]{1,0:T(8,128)(2,1)} fusion(bf16[1024,2304]{1,0:T(8,128)(2,1)} %constant_dynamic-update-slice_fusion.27, bf16[1024,2304]{1,0:T(8,128)(2,1)} %get-tuple-element.105, bf16[1024,2304]{1,0:T(8,128)(2,1)} %get-tuple-element.104), kind=kOutput, calls=%fused_computation | convolution fusion | flops 21772763136 | bytes 35389440 | tf_op jit(solution)/shard_map/dot_general | solution.py:57
  579.6 31.0 %fusion.169 = f32[1024,2304]{1,0:T(8,128)} fusion(bf16[1024,4608]{1,0:T(8,128)(2,1)} %pad_maximum_fusion, bf16[2304,4608]{1,0:T(8,128)(2,1)} %all-gather.7.cloned.1.call-done), kind=kOutput, calls=%fused_computation.417 | convolution fusion | flops 21743271936 | bytes 40108032 | tf_op jit(solution)/shard_map/dot_general | solution.py:53
  618.3 24.8 %collective-permute-done.40 = bf16[256,2304]{1,0:T(8,128)(2,1)S(1)} collective-permute-done((bf16[256,2304]{1,0:T(8,128)(2,1)S(1)}, bf16[256,2304]{1,0:T(8,128)(2,1)S(1)}, u32[]{:S(2)}, u32[]{:S(2)}) %collective-permute-start.40) | collective-permute-done | bytes 1179680 | tf_op jit(solution)/shard_map/ppermute | solution.py:272
  643.1 22.0 %collective-permute-done.39 = bf16[256,2304]{1,0:T(8,128)(2,1)S(1)} collective-permute-done((bf16[256,2304]{1,0:T(8,128)(2,1)S(1)}, bf16[256,2304]{1,0:T(8,128)(2,1)S(1)}, u32[]{:S(2)}, u32[]{:S(2)}) %collective-permute-start.39) | collective-permute-done | bytes 1179680 | tf_op jit(solution)/shard_map/ppermute | solution.py:272
  665.1 7.6 multiply_reduce_fusion
  679.2 25.4 %collective-permute-done.41 = bf16[256,2304]{1,0:T(8,128)(2,1)S(1)} collective-permute-done((bf16[256,2304]{1,0:T(8,128)(2,1)S(1)}, bf16[256,2304]{1,0:T(8,128)(2,1)S(1)}, u32[]{:S(2)}, u32[]{:S(2)}) %collective-permute-start.41) | collective-permute-done | bytes 1179680 | tf_op jit(solution)/shard_map/ppermute | solution.py:272
  704.7 20.5 %collective-permute-done.42 = bf16[256,2304]{1,0:T(8,128)(2,1)S(1)} collective-permute-done((bf16[256,2304]{1,0:T(8,128)(2,1)S(1)}, bf16[256,2304]{1,0:T(8,128)(2,1)S(1)}, u32[]{:S(2)}, u32[]{:S(2)}) %collective-permute-start.42) | collective-permute-done | bytes 1179680 | tf_op jit(solution)/shard_map/ppermute | solution.py:272
  732.8 6.3 convolution_convert_fusion.14.upstream_ref
  739.1 4.3 copy.128
  745.0 7.3 shard_map.231
  752.3 9.1 convolution_convert_fusion.2
  761.4 6.5 pad_maximum_fusion.1
  767.9 10.3 copy.143
  778.9 4.9 convolution_convert_fusion.5
  785.2 4.8 convolution_convert_fusion.6
  795.6 17.4 %collective-permute-done.46 = bf16[256,2304]{1,0:T(8,128)(2,1)} collective-permute-done((bf16[256,2304]{1,0:T(8,128)(2,1)}, bf16[256,2304]{1,0:T(8,128)(2,1)}, u32[]{:S(2)}, u32[]{:S(2)}) %collective-permute-start.46) | collective-permute-done | bytes 1179680 | tf_op jit(solution)/shard_map/ppermute | solution.py:272
  813.0 26.4 %collective-permute-done.45 = bf16[256,2304]{1,0:T(8,128)(2,1)} collective-permute-done((bf16[256,2304]{1,0:T(8,128)(2,1)}, bf16[256,2304]{1,0:T(8,128)(2,1)}, u32[]{:S(2)}, u32[]{:S(2)}) %collective-permute-start.45) | collective-permute-done | bytes 1179680 | tf_op jit(solution)/shard_map/ppermute | solution.py:272
  839.5 10.8 fusion.44
  867.5 4.2 collective-permute-done.56
  880.3 184.3 %reduce-scatter.7.cloned.1.call-done = bf16[288,4608]{1,0:T(8,128)(2,1)} async-done(((bf16[2304,4608]{1,0:T(8,128)(2,1)}), bf16[288,4608]{1,0:T(8,128)(2,1)}) %reduce-scatter.7.cloned.1.call-update) | async-done | bytes 2654224 | tf_op jit(solution)/shard_map/reduce_scatter | solution.py:321
  1071.2 9.8 collective-permute-done.50
  1083.8 12.7 %collective-permute-done.51 = bf16[72,4608]{1,0:T(8,128)(2,1)S(1)} collective-permute-done((bf16[72,4608]{1,0:T(8,128)(2,1)S(1)}, bf16[72,4608]{1,0:T(8,128)(2,1)S(1)}, u32[]{:S(2)}, u32[]{:S(2)}) %collective-permute-start.51) | collective-permute-done | bytes 663584 | tf_op jit(solution)/shard_map/ppermute | solution.py:272
  1096.6 7.5 fusion.21
  1105.6 6.1 shard_map.232
  1111.7 7.2 all-to-all-start
  1118.9 4.5 fusion.41
  1135.4 67.2 %all-to-all-done = bf16[896,8,256]{2,1,0:T(8,128)(2,1)} async-done(((bf16[896,8,256]{2,1,0:T(8,128)(2,1)}), bf16[896,8,256]{2,1,0:T(8,128)(2,1)}, u32[]{:S(2)}, u32[]{:S(2)}) %all-to-all-start) | async-done | bytes 3670048 | tf_op jit(solution)/shard_map/all_to_all | solution.py:592
  1210.2 25.5 %shard_map.233 = (f32[38,256,256]{2,1,0:T(8,128)}, f32[38,256,256]{2,1,0:T(8,128)}, f32[38,256,256]{2,1,0:T(8,128)}) custom-call(bf16[32,28,8,256]{3,2,1,0:T(8,128)(2,1)} %bitcast.89.incoming, f32[38,256,256]{2,1,0:T(8,128)} %first.3, f32[38,256,256]{2,1,0:T(8,128)} %second.3, f32[38,256,256]{2,1,0:T(8,128)} %left.3, f32[38,256,256]{2,1,0:T(8,128)} %right.3, ...), custom_call_target="tpu_custom_call" | custom-call | flops 3758096384 | bytes 62390272 | tf_op jit(solution)/shard_map/pallas_call | solution.py:222
  1235.7 5.7 all-to-all-done.1
  1242.3 10.1 shard_map.234
  (444 shorter events, 231.9 us)
Async XLA Ops:
  7.2 162.2 %all-gather.5.cloned.1.call-start = ((), (), s32[]{:S(2)}) async-start(), calls=%async_computation.6 | async-start | bytes 7962624 | tf_op jit(solution)/shard_map/all_gather | solution.py:318
  9.2 9.3 collective-permute-start.8
  12.4 11.7 collective-permute-start.9
  14.0 10.0 collective-permute-start.10
  25.1 293.6 %all-gather.7.cloned.1.call-start = ((), (), s32[]{:S(2)}) async-start(), calls=%async_computation.7 | async-start | bytes 23887872 | tf_op jit(solution)/shard_map/all_gather | solution.py:318
  37.9 17.8 %collective-permute-start.17 = (bf16[72,4608]{1,0:T(8,128)(2,1)S(1)}, bf16[72,4608]{1,0:T(8,128)(2,1)S(1)}, u32[]{:S(2)}, u32[]{:S(2)}) collective-permute-start(bf16[72,4608]{1,0:T(8,128)(2,1)S(1)} %pad_maximum_fusion.3), channel_id=1, source_target_pairs={{0,8},{8,0},{16,24},{24,16},{1,9},{9,1},{17,25},{25,17},{2,10},{10... | collective-permute-start | bytes 1990664 | tf_op jit(solution)/shard_map/ppermute | solution.py:272
  39.1 29.8 %collective-permute-start.18 = (bf16[72,4608]{1,0:T(8,128)(2,1)S(1)}, bf16[72,4608]{1,0:T(8,128)(2,1)S(1)}, u32[]{:S(2)}, u32[]{:S(2)}) collective-permute-start(bf16[72,4608]{1,0:T(8,128)(2,1)S(1)} %pad_maximum_fusion.4), channel_id=1, source_target_pairs={{0,16},{8,24},{16,0},{24,8},{1,17},{9,25},{17,1},{25,9},{2,18},{10... | collective-permute-start | bytes 1990664 | tf_op jit(solution)/shard_map/ppermute | solution.py:272
  40.2 28.7 %collective-permute-start.19 = (bf16[72,4608]{1,0:T(8,128)(2,1)S(1)}, bf16[72,4608]{1,0:T(8,128)(2,1)S(1)}, u32[]{:S(2)}, u32[]{:S(2)}) collective-permute-start(bf16[72,4608]{1,0:T(8,128)(2,1)S(1)} %pad_maximum_fusion.5), channel_id=1, source_target_pairs={{0,24},{8,16},{16,8},{24,0},{1,25},{9,17},{17,9},{25,1},{2,26},{10... | collective-permute-start | bytes 1990664 | tf_op jit(solution)/shard_map/ppermute | solution.py:272
  70.5 291.2 %all-gather.11.cloned.1.call-start = ((), (), s32[]{:S(2)}) async-start(), calls=%async_computation.9 | async-start | bytes 8626176 | tf_op jit(solution)/shard_map/all_gather | solution.py:318
  74.5 8.3 collective-permute-start.26
  75.1 10.6 collective-permute-start.27
  76.7 9.9 collective-permute-start.28
  87.6 311.3 %all-gather.9.cloned.1.call-start = ((), (), s32[]{:S(2)}) async-start(), calls=%async_computation.8 | async-start | bytes 3317760 | tf_op jit(solution)/shard_map/all_gather | solution.py:318
  116.7 28.8 %collective-permute-start.5 = (bf16[256,2304]{1,0:T(8,128)(2,1)S(1)}, bf16[256,2304]{1,0:T(8,128)(2,1)S(1)}, u32[]{:S(2)}, u32[]{:S(2)}) collective-permute-start(bf16[256,2304]{1,0:T(8,128)(2,1)S(1)} %get-tuple-element.198), channel_id=1, source_target_pairs={{0,8},{8,0},{16,24},{24,16},{1,9},{9,1},{17,25},{25,17},{2,10},{10... | collective-permute-start | bytes 3538952 | tf_op jit(solution)/shard_map/ppermute | solution.py:272
  118.2 49.0 %collective-permute-start.6 = (bf16[256,2304]{1,0:T(8,128)(2,1)S(1)}, bf16[256,2304]{1,0:T(8,128)(2,1)S(1)}, u32[]{:S(2)}, u32[]{:S(2)}) collective-permute-start(bf16[256,2304]{1,0:T(8,128)(2,1)S(1)} %get-tuple-element.198), channel_id=1, source_target_pairs={{0,16},{8,24},{16,0},{24,8},{1,17},{9,25},{17,1},{25,9},{2,18},{10... | collective-permute-start | bytes 3538952 | tf_op jit(solution)/shard_map/ppermute | solution.py:272
  118.5 49.8 %collective-permute-start.7 = (bf16[256,2304]{1,0:T(8,128)(2,1)S(1)}, bf16[256,2304]{1,0:T(8,128)(2,1)S(1)}, u32[]{:S(2)}, u32[]{:S(2)}) collective-permute-start(bf16[256,2304]{1,0:T(8,128)(2,1)S(1)} %get-tuple-element.198), channel_id=1, source_target_pairs={{0,24},{8,16},{16,8},{24,0},{1,25},{9,17},{17,9},{25,1},{2,26},{10... | collective-permute-start | bytes 3538952 | tf_op jit(solution)/shard_map/ppermute | solution.py:272
  194.3 28.9 %collective-permute-start.13 = (bf16[256,2304]{1,0:T(8,128)(2,1)S(1)}, bf16[256,2304]{1,0:T(8,128)(2,1)S(1)}, u32[]{:S(2)}, u32[]{:S(2)}) collective-permute-start(bf16[256,2304]{1,0:T(8,128)(2,1)S(1)} %convolution_convert_fusion.8), channel_id=1, source_target_pairs={{0,8},{8,0},{16,24},{24,16},{1,9},{9,1},{17,25},{25,17},{2,10},{10... | collective-permute-start | bytes 3538952 | tf_op jit(solution)/shard_map/ppermute | solution.py:272
  194.7 46.7 %collective-permute-start.12 = (bf16[256,2304]{1,0:T(8,128)(2,1)S(1)}, bf16[256,2304]{1,0:T(8,128)(2,1)S(1)}, u32[]{:S(2)}, u32[]{:S(2)}) collective-permute-start(bf16[256,2304]{1,0:T(8,128)(2,1)S(1)} %convolution_convert_fusion.9), channel_id=1, source_target_pairs={{0,16},{8,24},{16,0},{24,8},{1,17},{9,25},{17,1},{25,9},{2,18},{10... | collective-permute-start | bytes 3538952 | tf_op jit(solution)/shard_map/ppermute | solution.py:272
  194.9 46.5 %collective-permute-start.11 = (bf16[256,2304]{1,0:T(8,128)(2,1)S(1)}, bf16[256,2304]{1,0:T(8,128)(2,1)S(1)}, u32[]{:S(2)}, u32[]{:S(2)}) collective-permute-start(bf16[256,2304]{1,0:T(8,128)(2,1)S(1)} %convolution_convert_fusion.10), channel_id=1, source_target_pairs={{0,24},{8,16},{16,8},{24,0},{1,25},{9,17},{17,9},{25,1},{2,26},{10... | collective-permute-start | bytes 3538952 | tf_op jit(solution)/shard_map/ppermute | solution.py:272
  257.5 54.0 %collective-permute-start.14 = (bf16[256,2304]{1,0:T(8,128)(2,1)}, bf16[256,2304]{1,0:T(8,128)(2,1)}, u32[]{:S(2)}, u32[]{:S(2)}) collective-permute-start(bf16[256,2304]{1,0:T(8,128)(2,1)} %get-tuple-element.202), channel_id=1, source_target_pairs={{0,8},{8,0},{16,24},{24,16},{1,9},{9,1},{17,25},{25,17},{2,10},{10... | collective-permute-start | bytes 3538952 | tf_op jit(solution)/shard_map/ppermute | solution.py:272
  259.0 54.9 %collective-permute-start.15 = (bf16[256,2304]{1,0:T(8,128)(2,1)}, bf16[256,2304]{1,0:T(8,128)(2,1)}, u32[]{:S(2)}, u32[]{:S(2)}) collective-permute-start(bf16[256,2304]{1,0:T(8,128)(2,1)} %get-tuple-element.202), channel_id=1, source_target_pairs={{0,16},{8,24},{16,0},{24,8},{1,17},{9,25},{17,1},{25,9},{2,18},{10... | collective-permute-start | bytes 3538952 | tf_op jit(solution)/shard_map/ppermute | solution.py:272
  260.7 27.9 %collective-permute-start.20 = (bf16[72,640]{1,0:T(8,128)(2,1)S(1)}, bf16[72,640]{1,0:T(8,128)(2,1)S(1)}, u32[]{:S(2)}, u32[]{:S(2)}) collective-permute-start(bf16[72,640]{1,0:T(8,128)(2,1)S(1)} %get-tuple-element.161), channel_id=1, source_target_pairs={{0,8},{8,0},{16,24},{24,16},{1,9},{9,1},{17,25},{25,17},{2,10},{10... | collective-permute-start | bytes 276488 | tf_op jit(solution)/shard_map/ppermute | solution.py:272
  262.4 48.2 %collective-permute-start.21 = (bf16[72,640]{1,0:T(8,128)(2,1)S(1)}, bf16[72,640]{1,0:T(8,128)(2,1)S(1)}, u32[]{:S(2)}, u32[]{:S(2)}) collective-permute-start(bf16[72,640]{1,0:T(8,128)(2,1)S(1)} %get-tuple-element.160), channel_id=1, source_target_pairs={{0,16},{8,24},{16,0},{24,8},{1,17},{9,25},{17,1},{25,9},{2,18},{10... | collective-permute-start | bytes 276488 | tf_op jit(solution)/shard_map/ppermute | solution.py:272
  262.7 53.5 %collective-permute-start.16 = (bf16[256,2304]{1,0:T(8,128)(2,1)}, bf16[256,2304]{1,0:T(8,128)(2,1)}, u32[]{:S(2)}, u32[]{:S(2)}) collective-permute-start(bf16[256,2304]{1,0:T(8,128)(2,1)} %get-tuple-element.202), channel_id=1, source_target_pairs={{0,24},{8,16},{16,8},{24,0},{1,25},{9,17},{17,9},{25,1},{2,26},{10... | collective-permute-start | bytes 3538952 | tf_op jit(solution)/shard_map/ppermute | solution.py:272
  288.6 22.1 %collective-permute-start.22 = (bf16[72,640]{1,0:T(8,128)(2,1)S(1)}, bf16[72,640]{1,0:T(8,128)(2,1)S(1)}, u32[]{:S(2)}, u32[]{:S(2)}) collective-permute-start(bf16[72,640]{1,0:T(8,128)(2,1)S(1)} %get-tuple-element.159), channel_id=1, source_target_pairs={{0,24},{8,16},{16,8},{24,0},{1,25},{9,17},{17,9},{25,1},{2,26},{10... | collective-permute-start | bytes 276488 | tf_op jit(solution)/shard_map/ppermute | solution.py:272
  311.5 539.7 %reduce-scatter.9.cloned.1.call-start = ((), (), s32[]{:S(2)}) async-start(), calls=%async_computation.11 | async-start | bytes 3317760 | tf_op jit(solution)/shard_map/reduce_scatter | solution.py:321
  368.6 59.2 %collective-permute-start.31 = (bf16[256,1664]{1,0:T(8,128)(2,1)}, bf16[256,1664]{1,0:T(8,128)(2,1)S(1)}, u32[]{:S(2)}, u32[]{:S(2)}) collective-permute-start(bf16[256,1664]{1,0:T(8,128)(2,1)} %convolution_convert_fusion.11), channel_id=1, source_target_pairs={{0,8},{8,0},{16,24},{24,16},{1,9},{9,1},{17,25},{25,17},{2,10},{10... | collective-permute-start | bytes 2555912 | tf_op jit(solution)/shard_map/ppermute | solution.py:272
  373.3 54.5 %collective-permute-start.30 = (bf16[256,1664]{1,0:T(8,128)(2,1)}, bf16[256,1664]{1,0:T(8,128)(2,1)}, u32[]{:S(2)}, u32[]{:S(2)}) collective-permute-start(bf16[256,1664]{1,0:T(8,128)(2,1)} %convolution_convert_fusion.12), channel_id=1, source_target_pairs={{0,16},{8,24},{16,0},{24,8},{1,17},{9,25},{17,1},{25,9},{2,18},{10... | collective-permute-start | bytes 2555912 | tf_op jit(solution)/shard_map/ppermute | solution.py:272
  378.0 49.8 %collective-permute-start.29 = (bf16[256,1664]{1,0:T(8,128)(2,1)}, bf16[256,1664]{1,0:T(8,128)(2,1)}, u32[]{:S(2)}, u32[]{:S(2)}) collective-permute-start(bf16[256,1664]{1,0:T(8,128)(2,1)} %convolution_convert_fusion.13), channel_id=1, source_target_pairs={{0,24},{8,16},{16,8},{24,0},{1,25},{9,17},{17,9},{25,1},{2,26},{10... | collective-permute-start | bytes 2555912 | tf_op jit(solution)/shard_map/ppermute | solution.py:272
  402.4 12.9 %collective-permute-start.25 = (bf16[256,640]{1,0:T(8,128)(2,1)S(1)}, bf16[256,640]{1,0:T(8,128)(2,1)S(1)}, u32[]{:S(2)}, u32[]{:S(2)}) collective-permute-start(bf16[256,640]{1,0:T(8,128)(2,1)S(1)} %convolution_convert_fusion.17), channel_id=1, source_target_pairs={{0,8},{8,0},{16,24},{24,16},{1,9},{9,1},{17,25},{25,17},{2,10},{10... | collective-permute-start | bytes 983048 | tf_op jit(solution)/shard_map/ppermute | solution.py:272
  407.4 19.3 %collective-permute-start.24 = (bf16[256,640]{1,0:T(8,128)(2,1)S(1)}, bf16[256,640]{1,0:T(8,128)(2,1)S(1)}, u32[]{:S(2)}, u32[]{:S(2)}) collective-permute-start(bf16[256,640]{1,0:T(8,128)(2,1)S(1)} %convolution_convert_fusion.18), channel_id=1, source_target_pairs={{0,16},{8,24},{16,0},{24,8},{1,17},{9,25},{17,1},{25,9},{2,18},{10... | collective-permute-start | bytes 983048 | tf_op jit(solution)/shard_map/ppermute | solution.py:272
  415.2 11.4 collective-permute-start.23
  436.9 10.6 collective-permute-start.32
  437.8 16.7 %collective-permute-start.33 = (bf16[256,640]{1,0:T(8,128)(2,1)S(1)}, bf16[256,640]{1,0:T(8,128)(2,1)S(1)}, u32[]{:S(2)}, u32[]{:S(2)}) collective-permute-start(bf16[256,640]{1,0:T(8,128)(2,1)S(1)} %get-tuple-element.136), channel_id=1, source_target_pairs={{0,16},{8,24},{16,0},{24,8},{1,17},{9,25},{17,1},{25,9},{2,18},{10... | collective-permute-start | bytes 983048 | tf_op jit(solution)/shard_map/ppermute | solution.py:272
  439.3 16.2 %collective-permute-start.34 = (bf16[256,640]{1,0:T(8,128)(2,1)S(1)}, bf16[256,640]{1,0:T(8,128)(2,1)S(1)}, u32[]{:S(2)}, u32[]{:S(2)}) collective-permute-start(bf16[256,640]{1,0:T(8,128)(2,1)S(1)} %get-tuple-element.136), channel_id=1, source_target_pairs={{0,24},{8,16},{16,8},{24,0},{1,25},{9,17},{17,9},{25,1},{2,26},{10... | collective-permute-start | bytes 983048 | tf_op jit(solution)/shard_map/ppermute | solution.py:272
  443.5 29.5 %collective-permute-start.35 = (bf16[256,1664]{1,0:T(8,128)(2,1)}, bf16[256,1664]{1,0:T(8,128)(2,1)}, u32[]{:S(2)}, u32[]{:S(2)}) collective-permute-start(bf16[256,1664]{1,0:T(8,128)(2,1)} %get-tuple-element.134), channel_id=1, source_target_pairs={{0,8},{8,0},{16,24},{24,16},{1,9},{9,1},{17,25},{25,17},{2,10},{10... | collective-permute-start | bytes 2555912 | tf_op jit(solution)/shard_map/ppermute | solution.py:272
  444.3 44.8 %collective-permute-start.36 = (bf16[256,1664]{1,0:T(8,128)(2,1)}, bf16[256,1664]{1,0:T(8,128)(2,1)}, u32[]{:S(2)}, u32[]{:S(2)}) collective-permute-start(bf16[256,1664]{1,0:T(8,128)(2,1)} %get-tuple-element.134), channel_id=1, source_target_pairs={{0,16},{8,24},{16,0},{24,8},{1,17},{9,25},{17,1},{25,9},{2,18},{10... | collective-permute-start | bytes 2555912 | tf_op jit(solution)/shard_map/ppermute | solution.py:272
  447.6 43.7 %collective-permute-start.37 = (bf16[256,1664]{1,0:T(8,128)(2,1)}, bf16[256,1664]{1,0:T(8,128)(2,1)}, u32[]{:S(2)}, u32[]{:S(2)}) collective-permute-start(bf16[256,1664]{1,0:T(8,128)(2,1)} %get-tuple-element.134), channel_id=1, source_target_pairs={{0,24},{8,16},{16,8},{24,0},{1,25},{9,17},{17,9},{25,1},{2,26},{10... | collective-permute-start | bytes 2555912 | tf_op jit(solution)/shard_map/ppermute | solution.py:272
  462.0 397.5 %reduce-scatter.11.cloned.1.call-start = ((), (), s32[]{:S(2)}) async-start(), calls=%async_computation.12 | async-start | bytes 8626176 | tf_op jit(solution)/shard_map/reduce_scatter | solution.py:321
  579.6 295.1 %reduce-scatter.13.cloned.1.call-start = ((), (), s32[]{:S(2)}) async-start(), calls=%async_computation.13 | async-start | bytes 7962624 | tf_op jit(solution)/shard_map/reduce_scatter | solution.py:321
  614.2 28.9 %collective-permute-start.40 = (bf16[256,2304]{1,0:T(8,128)(2,1)S(1)}, bf16[256,2304]{1,0:T(8,128)(2,1)S(1)}, u32[]{:S(2)}, u32[]{:S(2)}) collective-permute-start(bf16[256,2304]{1,0:T(8,128)(2,1)S(1)} %get-tuple-element.107), channel_id=1, source_target_pairs={{0,8},{8,0},{16,24},{24,16},{1,9},{9,1},{17,25},{25,17},{2,10},{10... | collective-permute-start | bytes 3538952 | tf_op jit(solution)/shard_map/ppermute | solution.py:272
  614.6 50.4 %collective-permute-start.39 = (bf16[256,2304]{1,0:T(8,128)(2,1)S(1)}, bf16[256,2304]{1,0:T(8,128)(2,1)S(1)}, u32[]{:S(2)}, u32[]{:S(2)}) collective-permute-start(bf16[256,2304]{1,0:T(8,128)(2,1)S(1)} %get-tuple-element.108), channel_id=1, source_target_pairs={{0,16},{8,24},{16,0},{24,8},{1,17},{9,25},{17,1},{25,9},{2,18},{10... | collective-permute-start | bytes 3538952 | tf_op jit(solution)/shard_map/ppermute | solution.py:272
  617.6 47.4 %collective-permute-start.38 = (bf16[256,2304]{1,0:T(8,128)(2,1)S(1)}, bf16[256,2304]{1,0:T(8,128)(2,1)S(1)}, u32[]{:S(2)}, u32[]{:S(2)}) collective-permute-start(bf16[256,2304]{1,0:T(8,128)(2,1)S(1)} %get-tuple-element.106), channel_id=1, source_target_pairs={{0,24},{8,16},{16,8},{24,0},{1,25},{9,17},{17,9},{25,1},{2,26},{10... | collective-permute-start | bytes 3538952 | tf_op jit(solution)/shard_map/ppermute | solution.py:272
  675.7 28.8 %collective-permute-start.41 = (bf16[256,2304]{1,0:T(8,128)(2,1)S(1)}, bf16[256,2304]{1,0:T(8,128)(2,1)S(1)}, u32[]{:S(2)}, u32[]{:S(2)}) collective-permute-start(bf16[256,2304]{1,0:T(8,128)(2,1)S(1)} %get-tuple-element.100), channel_id=1, source_target_pairs={{0,8},{8,0},{16,24},{24,16},{1,9},{9,1},{17,25},{25,17},{2,10},{10... | collective-permute-start | bytes 3538952 | tf_op jit(solution)/shard_map/ppermute | solution.py:272
  676.3 48.9 %collective-permute-start.42 = (bf16[256,2304]{1,0:T(8,128)(2,1)S(1)}, bf16[256,2304]{1,0:T(8,128)(2,1)S(1)}, u32[]{:S(2)}, u32[]{:S(2)}) collective-permute-start(bf16[256,2304]{1,0:T(8,128)(2,1)S(1)} %get-tuple-element.100), channel_id=1, source_target_pairs={{0,16},{8,24},{16,0},{24,8},{1,17},{9,25},{17,1},{25,9},{2,18},{10... | collective-permute-start | bytes 3538952 | tf_op jit(solution)/shard_map/ppermute | solution.py:272
  677.4 47.9 %collective-permute-start.43 = (bf16[256,2304]{1,0:T(8,128)(2,1)S(1)}, bf16[256,2304]{1,0:T(8,128)(2,1)S(1)}, u32[]{:S(2)}, u32[]{:S(2)}) collective-permute-start(bf16[256,2304]{1,0:T(8,128)(2,1)S(1)} %get-tuple-element.100), channel_id=1, source_target_pairs={{0,24},{8,16},{16,8},{24,0},{1,25},{9,17},{17,9},{25,1},{2,26},{10... | collective-permute-start | bytes 3538952 | tf_op jit(solution)/shard_map/ppermute | solution.py:272
  778.2 286.4 %reduce-scatter.7.cloned.1.call-start = ((), (), s32[]{:S(2)}) async-start(), calls=%async_computation.10 | async-start | bytes 23887872 | tf_op jit(solution)/shard_map/reduce_scatter | solution.py:321
  783.9 29.2 %collective-permute-start.46 = (bf16[256,2304]{1,0:T(8,128)(2,1)}, bf16[256,2304]{1,0:T(8,128)(2,1)}, u32[]{:S(2)}, u32[]{:S(2)}) collective-permute-start(bf16[256,2304]{1,0:T(8,128)(2,1)} %convolution_convert_fusion.5), channel_id=1, source_target_pairs={{0,8},{8,0},{16,24},{24,16},{1,9},{9,1},{17,25},{25,17},{2,10},{10... | collective-permute-start | bytes 3538952 | tf_op jit(solution)/shard_map/ppermute | solution.py:272
  790.0 49.4 %collective-permute-start.45 = (bf16[256,2304]{1,0:T(8,128)(2,1)}, bf16[256,2304]{1,0:T(8,128)(2,1)}, u32[]{:S(2)}, u32[]{:S(2)}) collective-permute-start(bf16[256,2304]{1,0:T(8,128)(2,1)} %convolution_convert_fusion.6), channel_id=1, source_target_pairs={{0,16},{8,24},{16,0},{24,8},{1,17},{9,25},{17,1},{25,9},{2,18},{10... | collective-permute-start | bytes 3538952 | tf_op jit(solution)/shard_map/ppermute | solution.py:272
  793.4 46.0 %collective-permute-start.44 = (bf16[256,2304]{1,0:T(8,128)(2,1)}, bf16[256,2304]{1,0:T(8,128)(2,1)}, u32[]{:S(2)}, u32[]{:S(2)}) collective-permute-start(bf16[256,2304]{1,0:T(8,128)(2,1)} %convolution_convert_fusion.7), channel_id=1, source_target_pairs={{0,24},{8,16},{16,8},{24,0},{1,25},{9,17},{17,9},{25,1},{2,26},{10... | collective-permute-start | bytes 3538952 | tf_op jit(solution)/shard_map/ppermute | solution.py:272
  852.3 5.0 collective-permute-start.53
  852.5 4.8 collective-permute-start.55
  852.8 6.6 collective-permute-start.57
  861.3 6.2 collective-permute-start.54
  863.0 8.6 collective-permute-start.56
  864.8 9.8 collective-permute-start.58
  876.8 228.8 %collective-permute-start.47 = (bf16[72,1536]{1,0:T(8,128)(2,1)}, bf16[72,1536]{1,0:T(8,128)(2,1)S(1)}, u32[]{:S(2)}, u32[]{:S(2)}) collective-permute-start(bf16[72,1536]{1,0:T(8,128)(2,1)} %get-tuple-element.147), channel_id=1, source_target_pairs={{0,8},{8,0},{16,24},{24,16},{1,9},{9,1},{17,25},{25,17},{2,10},{10... | collective-permute-start | bytes 663560 | tf_op jit(solution)/shard_map/ppermute | solution.py:272
  877.9 227.6 %collective-permute-start.48 = (bf16[72,1536]{1,0:T(8,128)(2,1)}, bf16[72,1536]{1,0:T(8,128)(2,1)S(1)}, u32[]{:S(2)}, u32[]{:S(2)}) collective-permute-start(bf16[72,1536]{1,0:T(8,128)(2,1)} %get-tuple-element.146), channel_id=1, source_target_pairs={{0,16},{8,24},{16,0},{24,8},{1,17},{9,25},{17,1},{25,9},{2,18},{10... | collective-permute-start | bytes 663560 | tf_op jit(solution)/shard_map/ppermute | solution.py:272
  877.9 227.6 %collective-permute-start.49 = (bf16[72,1536]{1,0:T(8,128)(2,1)}, bf16[72,1536]{1,0:T(8,128)(2,1)S(1)}, u32[]{:S(2)}, u32[]{:S(2)}) collective-permute-start(bf16[72,1536]{1,0:T(8,128)(2,1)} %get-tuple-element.148), channel_id=1, source_target_pairs={{0,24},{8,16},{16,8},{24,0},{1,25},{9,17},{17,9},{25,1},{2,26},{10... | collective-permute-start | bytes 663560 | tf_op jit(solution)/shard_map/ppermute | solution.py:272
  1066.2 14.8 %collective-permute-start.50 = (bf16[72,4608]{1,0:T(8,128)(2,1)S(1)}, bf16[72,4608]{1,0:T(8,128)(2,1)S(1)}, u32[]{:S(2)}, u32[]{:S(2)}) collective-permute-start(bf16[72,4608]{1,0:T(8,128)(2,1)S(1)} %get-tuple-element.123), channel_id=1, source_target_pairs={{0,8},{8,0},{16,24},{24,16},{1,9},{9,1},{17,25},{25,17},{2,10},{10... | collective-permute-start | bytes 1990664 | tf_op jit(solution)/shard_map/ppermute | solution.py:272
  1067.7 28.7 %collective-permute-start.51 = (bf16[72,4608]{1,0:T(8,128)(2,1)S(1)}, bf16[72,4608]{1,0:T(8,128)(2,1)S(1)}, u32[]{:S(2)}, u32[]{:S(2)}) collective-permute-start(bf16[72,4608]{1,0:T(8,128)(2,1)S(1)} %get-tuple-element.122), channel_id=1, source_target_pairs={{0,16},{8,24},{16,0},{24,8},{1,17},{9,25},{17,1},{25,9},{2,18},{10... | collective-permute-start | bytes 1990664 | tf_op jit(solution)/shard_map/ppermute | solution.py:272
  1081.0 15.5 %collective-permute-start.52 = (bf16[72,4608]{1,0:T(8,128)(2,1)S(1)}, bf16[72,4608]{1,0:T(8,128)(2,1)S(1)}, u32[]{:S(2)}, u32[]{:S(2)}) collective-permute-start(bf16[72,4608]{1,0:T(8,128)(2,1)S(1)} %get-tuple-element.121), channel_id=1, source_target_pairs={{0,24},{8,16},{16,8},{24,0},{1,25},{9,17},{17,9},{25,1},{2,26},{10... | collective-permute-start | bytes 1990664 | tf_op jit(solution)/shard_map/ppermute | solution.py:272
  1111.7 90.9 %all-to-all-start = ((bf16[896,8,256]{2,1,0:T(8,128)(2,1)}), bf16[896,8,256]{2,1,0:T(8,128)(2,1)}, u32[]{:S(2)}, u32[]{:S(2)}) async-start(bf16[896,8,256]{2,1,0:T(8,128)(2,1)} %get-tuple-element.32), calls=%async_computation.3 | async-start | bytes 7340032 | tf_op jit(solution)/shard_map/all_to_all | solution.py:592
  1202.6 38.8 %all-to-all-start.1 = ((bf16[352,8,256]{2,1,0:T(8,128)(2,1)}), bf16[352,8,256]{2,1,0:T(8,128)(2,1)S(1)}, u32[]{:S(2)}, u32[]{:S(2)}) async-start(bf16[352,8,256]{2,1,0:T(8,128)(2,1)} %get-tuple-element.33), calls=%async_computation.4 | async-start | bytes 2883584 | tf_op jit(solution)/shard_map/all_to_all | solution.py:592
  (74 other events, 1330.6 us)
Sparse Core Ops, SparseCore 0:
  25.2 71.5 all-gather.4
  98.9 186.2 all-gather.6
  287.4 74.2 all-gather.10
  363.8 35.0 all-gather.8
  462.1 36.9 reduce-scatter.8
  579.7 81.6 reduce-scatter.10
  778.3 75.2 reduce-scatter.12
  856.0 208.5 reduce-scatter.6

commit v4 on v3

--- a/solution.py
+++ b/solution.py
@@ -4,6 +4,7 @@
 import jax.numpy as jnp
 from jax import lax
 from jax.experimental import pallas as pl
+from jax.experimental.layout import Layout, with_layout_constraint
 from jax.experimental.pallas import tpu as pltpu
 from jax.sharding import PartitionSpec as P
 
@@ -25,6 +26,7 @@
 STEP_RATE = 0.05
 TINY_ADD = 1e-08
 CLIP_NORM = 1.0
+
 
 F32 = jnp.float32
 BF16 = jnp.bfloat16
@@ -301,11 +303,12 @@
         received = {turn: swap(value, turn) for turn in range(seq_count - 1, 0, -1)}
         return assemble([value] + [received[turn] for turn in range(1, seq_count)])
 
-    def scatter_rows(part_of):
+    def scatter_rows(part_of, own_part_of=None):
         received = []
         for turn in range(seq_count - 1, 0, -1):
-            received.append(swap(part_of(owner_of(turn)).astype(BF16), turn))
-        result = part_of(seq_index)
+            part = part_of(owner_of(turn)).astype(BF16)
+            received.append(swap(part, turn))
+        result = (own_part_of or part_of)(seq_index)
         for value in received:
             result = result + value.astype(F32)
         return result
@@ -415,10 +418,16 @@
     product = (jax.nn.gelu(gate, approximate=True) * upper).astype(BF16)
 
     def branch_columns(weight):
-        def part_of(owner):
-            return dot(pick(product, owner, rows, 0), weight)
-
-        return scatter_rows(part_of)
+        def part_named():
+            def part_of(owner):
+                return dot(pick(product, owner, rows, 0), weight)
+
+            return part_of
+
+        own_part_of = part_named()
+        return scatter_rows(
+            part_named(), lambda owner: lax.optimization_barrier(own_part_of(owner))
+        )
 
     branch_late = branch_columns(down_late)
     branch = jnp.concatenate([branch_columns(down_early), branch_late], axis=1)
@@ -444,7 +453,6 @@
     gate_up_grad = jnp.concatenate([grad_gate, grad_upper], axis=1).astype(BF16)
     geglu_term = dot_tn(ffn_all, gate_up_grad).astype(BF16)
     geglu_sums = collect(geglu_term)
-    (gate_up_grad,) = after([gate_up_grad], [geglu_term])
     ffn_total = dot_nt(gate_up_grad, geglu_full)
 
     def ffn_part(owner):
@@ -461,14 +469,18 @@
     out_blocks = jnp.transpose(
         out_term.reshape(-1, heads, share, d_groups, BLK), (0, 3, 2, 1, 4)
     ).reshape(D, query_slice)
-    (grad_mixed, out_blocks) = after([grad_mixed, out_blocks], [])
+    out_blocks = with_layout_constraint(out_blocks, Layout((0, 1)))
     grad_merged = attention_backward(merged, grad_mixed, seq_lengths, prefix_lengths, heads)
     qkv_term = dot_tn(normed_all, grad_merged).astype(BF16)
+    qkv_term = with_layout_constraint(qkv_term, Layout((0, 1)))
     heads_sums = collect(jnp.concatenate([qkv_term, out_blocks], axis=1))
-    grad_normed = dot_nt(
-        scatter_rows(lambda owner: dot_nt(pick(grad_merged, owner, rows, 0), qkv_slice_full)).astype(BF16),
-        wide_order,
-    )
+    (sent_merged,) = after([grad_merged], down_sums[0] + down_sums[1])
+    (own_merged,) = after([grad_merged], geglu_sums)
+    grad_normed = scatter_rows(
+        lambda owner: dot_nt(pick(sent_merged, owner, rows, 0), qkv_slice_full),
+        lambda owner: dot_nt(pick(own_merged, owner, rows, 0), qkv_slice_full),
+    )
+    grad_normed = dot_nt(grad_normed.astype(BF16), wide_order)
     grad_input_norm, gain_one = norm_backward(inputs, inverse_one, gains[:, 0], grad_normed)
     token_grad = grad_hidden + grad_input_norm
 

time: 1270 us -> 1260 us (level)
    reduce_scatter x4, waiting for transfers between devices: 184 us -> 212 us  [collect(): summed = lax.psum_scatter(gradient, 'dp', scatter_dimension=0, tiled=True)]
    ppermute x54, waiting for transfers between devices: 394 us -> 374 us  [swap(): lax.ppermute(value, 'seq', [(at, at ^ turn) for at in range(seq_count)])]
    unnamed x159, local copies, waits for them, and re-layouts: 35.8 us -> 21.7 us
  transfers between devices with their start and end apart: 69 -> 69, of which waited for: 42 -> 43; matrix products, arithmetic and copies ran while one was open for 30% -> 30% of each run, Pallas kernels for 3% -> 3%
where the time goes in v4:
time: 1260 us; the launch traced here: 1250 us
  waiting for transfers between devices  683 us (54%)
  matrix products  265 us (21%)
  local copies, waits for them, and re-layouts  94.3 us (7%)
  starting transfers between devices  85.1 us (7%)
  Pallas kernels  53.5 us (4%)
  other arithmetic  50 us (4%)
  between operations  17.8 us (1%)
    ppermute x54, waiting for transfers between devices, swap(): lax.ppermute(value, 'seq', [(at, at ^ turn) for at in range(seq_count)])  374 us
    reduce_scatter x4, waiting for transfers between devices, collect(): summed = lax.psum_scatter(gradient, 'dp', scatter_dimension=0, tiled=True)  212 us
    dot_general x10, matrix products, dot_nt(): lax.dot_general(left, right, (((1,), (1,)), ((), ())), preferred_element_...  110 us
    dot_general x18, matrix products, dot(): return jnp.dot(left, right, preferred_element_type=F32)  95.4 us
    ppermute x54, starting transfers between devices, swap(): lax.ppermute(value, 'seq', [(at, at ^ turn) for at in range(seq_count)])  69 us
    all_to_all x2, waiting for transfers between devices, exchange(): moved = lax.all_to_all(value, ALL, split_axis=0, concat_axis=0, tiled=True)  64.8 us
    dot_general x5, matrix products, dot_tn(): lax.dot_general(left, right, (((0,), (0,)), ((), ())), preferred_element_...  60.2 us
    pallas_call x2, Pallas kernels, soap(): pl.pallas_call(functools.partial(soap_kernel, group), grid=(count // grou...  35.9 us
  transfers between devices with their start and end apart: 69, of which 43 were waited for; matrix products, arithmetic and copies ran while one was open for 30% of the time, Pallas kernels for 3%

profile of v4, /device:TPU:0, one launch (start us, length us, event | category | flops | bytes accessed | tf_op | source)
XLA Modules:
  0.0 1249.4 jit_solution(10005803604322283880)
XLA Ops:
  14.4 4.2 collective-permute-done.8
  18.6 5.5 collective-permute-done.9
  28.9 8.7 fusion.21
  41.9 13.8 %collective-permute-done.17 = bf16[72,4608]{1,0:T(8,128)(2,1)S(1)} collective-permute-done((bf16[72,4608]{1,0:T(8,128)(2,1)S(1)}, bf16[72,4608]{1,0:T(8,128)(2,1)S(1)}, u32[]{:S(2)}, u32[]{:S(2)}) %collective-permute-start.17) | collective-permute-done | bytes 663584 | tf_op jit(solution)/shard_map/ppermute | solution.py:274
  55.8 13.1 %collective-permute-done.18 = bf16[72,4608]{1,0:T(8,128)(2,1)S(1)} collective-permute-done((bf16[72,4608]{1,0:T(8,128)(2,1)S(1)}, bf16[72,4608]{1,0:T(8,128)(2,1)S(1)}, u32[]{:S(2)}, u32[]{:S(2)}) %collective-permute-start.18) | collective-permute-done | bytes 663584 | tf_op jit(solution)/shard_map/ppermute | solution.py:274
  78.1 4.7 collective-permute-done.26
  110.7 5.5 constant_dynamic-update-slice_fusion.37
  121.0 24.0 %collective-permute-done.5 = bf16[256,2304]{1,0:T(8,128)(2,1)S(1)} collective-permute-done((bf16[256,2304]{1,0:T(8,128)(2,1)S(1)}, bf16[256,2304]{1,0:T(8,128)(2,1)S(1)}, u32[]{:S(2)}, u32[]{:S(2)}) %collective-permute-start.5) | collective-permute-done | bytes 1179680 | tf_op jit(solution)/shard_map/ppermute | solution.py:274
  146.1 20.6 %collective-permute-done.6 = bf16[256,2304]{1,0:T(8,128)(2,1)S(1)} collective-permute-done((bf16[256,2304]{1,0:T(8,128)(2,1)S(1)}, bf16[256,2304]{1,0:T(8,128)(2,1)S(1)}, u32[]{:S(2)}, u32[]{:S(2)}) %collective-permute-start.6) | collective-permute-done | bytes 1179680 | tf_op jit(solution)/shard_map/ppermute | solution.py:274
  169.0 3.2 slice.228
  172.2 5.4 reshape.435
  177.9 9.1 fusion.54.merged_ref
  187.1 3.8 shard_map.230
  197.6 25.4 %collective-permute-done.13 = bf16[256,2304]{1,0:T(8,128)(2,1)S(1)} collective-permute-done((bf16[256,2304]{1,0:T(8,128)(2,1)S(1)}, bf16[256,2304]{1,0:T(8,128)(2,1)S(1)}, u32[]{:S(2)}, u32[]{:S(2)}) %collective-permute-start.13) | collective-permute-done | bytes 1179680 | tf_op jit(solution)/shard_map/ppermute | solution.py:274
  222.9 18.9 %collective-permute-done.12 = bf16[256,2304]{1,0:T(8,128)(2,1)S(1)} collective-permute-done((bf16[256,2304]{1,0:T(8,128)(2,1)S(1)}, bf16[256,2304]{1,0:T(8,128)(2,1)S(1)}, u32[]{:S(2)}, u32[]{:S(2)}) %collective-permute-start.12) | collective-permute-done | bytes 1179680 | tf_op jit(solution)/shard_map/ppermute | solution.py:274
  247.4 10.5 constant_dynamic-update-slice_fusion.30
  264.5 24.5 %collective-permute-done.20 = bf16[72,640]{1,0:T(8,128)(2,1)S(1)} collective-permute-done((bf16[72,640]{1,0:T(8,128)(2,1)S(1)}, bf16[72,640]{1,0:T(8,128)(2,1)S(1)}, u32[]{:S(2)}, u32[]{:S(2)}) %collective-permute-start.20) | collective-permute-done | bytes 92192 | tf_op jit(solution)/shard_map/ppermute | solution.py:274
  290.2 20.5 %collective-permute-done.21 = bf16[72,640]{1,0:T(8,128)(2,1)S(1)} collective-permute-done((bf16[72,640]{1,0:T(8,128)(2,1)S(1)}, bf16[72,640]{1,0:T(8,128)(2,1)S(1)}, u32[]{:S(2)}, u32[]{:S(2)}) %collective-permute-start.21) | collective-permute-done | bytes 92192 | tf_op jit(solution)/shard_map/ppermute | solution.py:274
  318.7 28.2 %fusion.168 = f32[1024,4608]{1,0:T(8,128)} fusion(bf16[1024,2304]{1,0:T(8,128)(2,1)} %constant_dynamic-update-slice_fusion.27, bf16[2304,4608]{1,0:T(8,128)(2,1)} %all-gather.7.cloned.1.call-done), kind=kOutput, calls=%fused_computation.417 | convolution fusion | flops 21743271936 | bytes 44826624 | tf_op jit(solution)/shard_map/dot_general | solution.py:51
  347.0 10.5 multiply_convert_fusion.1
  357.4 4.3 all-gather.11.cloned.1.call-done
  361.7 6.9 convolution_convert_fusion.11
  370.1 3.2 convolution_convert_fusion.12
  378.5 20.4 %all-gather.9.cloned.1.call-done = bf16[2304,640]{1,0:T(8,128)(2,1)} async-done(((bf16[288,640]{1,0:T(8,128)(2,1)}), bf16[2304,640]{1,0:T(8,128)(2,1)}) %all-gather.9.cloned.1.call-update) | async-done | bytes 2949136 | tf_op jit(solution)/shard_map/all_gather | solution.py:321
  398.9 3.4 convolution_convert_fusion.17
  403.9 3.3 convolution_convert_fusion.18
  411.1 4.1 collective-permute-done.25
  417.6 5.5 fusion.70
  438.5 7.1 collective-permute-done.32
  445.6 4.9 collective-permute-done.33
  452.8 5.3 convolution_convert_fusion.3
  463.1 18.3 %collective-permute-done.35 = bf16[256,1664]{1,0:T(8,128)(2,1)S(1)} collective-permute-done((bf16[256,1664]{1,0:T(8,128)(2,1)S(1)}, bf16[256,1664]{1,0:T(8,128)(2,1)S(1)}, u32[]{:S(2)}, u32[]{:S(2)}) %collective-permute-start.35) | collective-permute-done | bytes 852000 | tf_op jit(solution)/shard_map/ppermute | solution.py:274
  481.6 16.5 %collective-permute-done.36 = bf16[256,1664]{1,0:T(8,128)(2,1)S(1)} collective-permute-done((bf16[256,1664]{1,0:T(8,128)(2,1)S(1)}, bf16[256,1664]{1,0:T(8,128)(2,1)S(1)}, u32[]{:S(2)}, u32[]{:S(2)}) %collective-permute-start.36) | collective-permute-done | bytes 852000 | tf_op jit(solution)/shard_map/ppermute | solution.py:274
  500.1 10.8 convolution_convert_fusion.1
  511.0 15.7 %fusion.169 = f32[1024,2304]{1,0:T(8,128)} fusion(bf16[1024,1664]{1,0:T(8,128)(2,1)} %copy-done.26, bf16[2304,1664]{1,0:T(8,128)(2,1)} %all-gather.11.cloned.1.call-done), kind=kOutput, calls=%fused_computation.418 | convolution fusion | flops 7851737088 | bytes 20512768 | tf_op jit(solution)/shard_map/dot_general | solution.py:55
  526.7 18.9 %fusion.18 = (bf16[1024,2304]{1,0:T(8,128)(2,1)}, bf16[1024,2304]{1,0:T(8,128)(2,1)}) fusion(f32[1024,4608]{1,0:T(8,128)} %fusion.168, f32[1024,2304]{1,0:T(8,128)} %fusion.169, bf16[1024,640]{1,0:T(8,128)(2,1)S(1)} %copy-done.31, bf16[2304,640]{1,0:T(8,128)(2,1)} %all-gather.9.cloned.1.call-done), kind=kOutput, calls=%fused_computation.23 | convolution fusion | flops 3078881280 | bytes 42008576 | tf_op jit(solution)/shard_map/dot_general | solution.py:55
  545.6 30.2 %fusion.20 = f32[1024,2304]{1,0:T(8,128)} fusion(bf16[2304,4608]{1,0:T(8,128)(2,1)} %all-gather.7.cloned.1.call-done, bf16[1024,2304]{1,0:T(8,128)(2,1)} %get-tuple-element.92, bf16[1024,2304]{1,0:T(8,128)(2,1)} %get-tuple-element.91), kind=kOutput, calls=%fused_computation.33 | convolution fusion | flops 21762146304 | bytes 40108032 | tf_op jit(solution)/shard_map/dot_general | solution.py:55
  575.8 3.5 dynamic-slice_convert_fusion.2
  583.0 25.3 %collective-permute-done.40 = bf16[256,2304]{1,0:T(8,128)(2,1)S(1)} collective-permute-done((bf16[256,2304]{1,0:T(8,128)(2,1)S(1)}, bf16[256,2304]{1,0:T(8,128)(2,1)S(1)}, u32[]{:S(2)}, u32[]{:S(2)}) %collective-permute-start.40) | collective-permute-done | bytes 1179680 | tf_op jit(solution)/shard_map/ppermute | solution.py:274
  608.3 20.2 %collective-permute-done.39 = bf16[256,2304]{1,0:T(8,128)(2,1)S(1)} collective-permute-done((bf16[256,2304]{1,0:T(8,128)(2,1)S(1)}, bf16[256,2304]{1,0:T(8,128)(2,1)S(1)}, u32[]{:S(2)}, u32[]{:S(2)}) %collective-permute-start.39) | collective-permute-done | bytes 1179680 | tf_op jit(solution)/shard_map/ppermute | solution.py:274
  629.2 7.6 multiply_reduce_fusion
  643.3 25.4 %collective-permute-done.41 = bf16[256,2304]{1,0:T(8,128)(2,1)S(1)} collective-permute-done((bf16[256,2304]{1,0:T(8,128)(2,1)S(1)}, bf16[256,2304]{1,0:T(8,128)(2,1)S(1)}, u32[]{:S(2)}, u32[]{:S(2)}) %collective-permute-start.41) | collective-permute-done | bytes 1179680 | tf_op jit(solution)/shard_map/ppermute | solution.py:274
  668.8 22.2 %collective-permute-done.42 = bf16[256,2304]{1,0:T(8,128)(2,1)S(1)} collective-permute-done((bf16[256,2304]{1,0:T(8,128)(2,1)S(1)}, bf16[256,2304]{1,0:T(8,128)(2,1)S(1)}, u32[]{:S(2)}, u32[]{:S(2)}) %collective-permute-start.42) | collective-permute-done | bytes 1179680 | tf_op jit(solution)/shard_map/ppermute | solution.py:274
  691.3 3.3 convolution_convert_fusion.4
  697.1 5.5 convolution_convert_fusion.14.upstream_ref
  704.2 7.3 shard_map.231
  711.6 10.1 convolution_convert_fusion.2
  721.7 6.0 pad_maximum_fusion.1
  727.7 30.7 %convolution_convert_fusion = bf16[2304,4608]{1,0:T(8,128)(2,1)} fusion(bf16[1024,2304]{1,0:T(8,128)(2,1)} %constant_dynamic-update-slice_fusion.27, bf16[1024,2304]{1,0:T(8,128)(2,1)} %get-tuple-element.92, bf16[1024,2304]{1,0:T(8,128)(2,1)} %get-tuple-element.91), kind=kOutput, calls=%fused_computation | convolution fusion | flops 21772763136 | bytes 35389440 | tf_op jit(solution)/shard_map/dot_general | solution.py:59
  781.9 5.0 convolution_convert_fusion.5
  788.0 4.8 convolution_convert_fusion.6
  797.7 4.3 reduce-scatter.11.cloned.1.call-done
  805.8 207.2 %reduce-scatter.5.cloned.1.call-done = bf16[288,4608]{1,0:T(8,128)(2,1)} async-done(((bf16[2304,4608]{1,0:T(8,128)(2,1)}), bf16[288,4608]{1,0:T(8,128)(2,1)}) %reduce-scatter.5.cloned.1.call-update) | async-done | bytes 2654224 | tf_op jit(solution)/shard_map/reduce_scatter | solution.py:324
  1018.2 11.3 collective-permute-done.44
  1031.1 19.5 %collective-permute-done.45 = bf16[72,4608]{1,0:T(8,128)(2,1)S(1)} collective-permute-done((bf16[72,4608]{1,0:T(8,128)(2,1)S(1)}, bf16[72,4608]{1,0:T(8,128)(2,1)S(1)}, u32[]{:S(2)}, u32[]{:S(2)}) %collective-permute-start.45) | collective-permute-done | bytes 663584 | tf_op jit(solution)/shard_map/ppermute | solution.py:274
  1053.0 9.2 collective-permute-done.46
  1063.8 7.7 fusion.22
  1074.7 11.8 fusion.43
  1097.0 6.5 shard_map.232
  1103.5 5.0 all-to-all-start
  1128.7 63.5 %all-to-all-done = bf16[896,8,256]{2,1,0:T(8,128)(2,1)} async-done(((bf16[896,8,256]{2,1,0:T(8,128)(2,1)}), bf16[896,8,256]{2,1,0:T(8,128)(2,1)}, u32[]{:S(2)}, u32[]{:S(2)}) %all-to-all-start) | async-done | bytes 3670048 | tf_op jit(solution)/shard_map/all_to_all | solution.py:604
  1197.0 4.9 convert_element_type.336
  1204.0 25.8 %shard_map.233 = (f32[38,256,256]{2,1,0:T(8,128)}, f32[38,256,256]{2,1,0:T(8,128)}, f32[38,256,256]{2,1,0:T(8,128)}) custom-call(bf16[32,28,8,256]{3,2,1,0:T(8,128)(2,1)} %bitcast.90.incoming, f32[38,256,256]{2,1,0:T(8,128)} %first.3, f32[38,256,256]{2,1,0:T(8,128)} %second.3, f32[38,256,256]{2,1,0:T(8,128)} %left.3, f32[38,256,256]{2,1,0:T(8,128)} %right.3, ...), custom_call_target="tpu_custom_call" | custom-call | flops 3758096384 | bytes 62390272 | tf_op jit(solution)/shard_map/pallas_call | solution.py:224
  1232.0 10.1 shard_map.234
  (444 shorter events, 228.8 us)
Async XLA Ops:
  7.2 161.8 %all-gather.5.cloned.1.call-start = ((), (), s32[]{:S(2)}) async-start(), calls=%async_computation.6 | async-start | bytes 7962624 | tf_op jit(solution)/shard_map/all_gather | solution.py:321
  9.2 9.3 collective-permute-start.8
  12.4 11.7 collective-permute-start.9
  14.0 10.0 collective-permute-start.10
  25.1 293.7 %all-gather.7.cloned.1.call-start = ((), (), s32[]{:S(2)}) async-start(), calls=%async_computation.7 | async-start | bytes 23887872 | tf_op jit(solution)/shard_map/all_gather | solution.py:321
  37.9 17.8 %collective-permute-start.17 = (bf16[72,4608]{1,0:T(8,128)(2,1)S(1)}, bf16[72,4608]{1,0:T(8,128)(2,1)S(1)}, u32[]{:S(2)}, u32[]{:S(2)}) collective-permute-start(bf16[72,4608]{1,0:T(8,128)(2,1)S(1)} %pad_maximum_fusion.5), channel_id=1, source_target_pairs={{0,8},{8,0},{16,24},{24,16},{1,9},{9,1},{17,25},{25,17},{2,10},{10... | collective-permute-start | bytes 1990664 | tf_op jit(solution)/shard_map/ppermute | solution.py:274
  39.1 29.8 %collective-permute-start.18 = (bf16[72,4608]{1,0:T(8,128)(2,1)S(1)}, bf16[72,4608]{1,0:T(8,128)(2,1)S(1)}, u32[]{:S(2)}, u32[]{:S(2)}) collective-permute-start(bf16[72,4608]{1,0:T(8,128)(2,1)S(1)} %pad_maximum_fusion.6), channel_id=1, source_target_pairs={{0,16},{8,24},{16,0},{24,8},{1,17},{9,25},{17,1},{25,9},{2,18},{10... | collective-permute-start | bytes 1990664 | tf_op jit(solution)/shard_map/ppermute | solution.py:274
  40.2 28.7 %collective-permute-start.19 = (bf16[72,4608]{1,0:T(8,128)(2,1)S(1)}, bf16[72,4608]{1,0:T(8,128)(2,1)S(1)}, u32[]{:S(2)}, u32[]{:S(2)}) collective-permute-start(bf16[72,4608]{1,0:T(8,128)(2,1)S(1)} %pad_maximum_fusion.7), channel_id=1, source_target_pairs={{0,24},{8,16},{16,8},{24,0},{1,25},{9,17},{17,9},{25,1},{2,26},{10... | collective-permute-start | bytes 1990664 | tf_op jit(solution)/shard_map/ppermute | solution.py:274
  70.5 291.2 %all-gather.11.cloned.1.call-start = ((), (), s32[]{:S(2)}) async-start(), calls=%async_computation.9 | async-start | bytes 8626176 | tf_op jit(solution)/shard_map/all_gather | solution.py:321
  74.5 8.3 collective-permute-start.26
  75.1 10.6 collective-permute-start.27
  76.7 9.9 collective-permute-start.28
  87.6 311.3 %all-gather.9.cloned.1.call-start = ((), (), s32[]{:S(2)}) async-start(), calls=%async_computation.8 | async-start | bytes 3317760 | tf_op jit(solution)/shard_map/all_gather | solution.py:321
  93.1 4.6 collective-permute-start.2
  116.2 28.8 %collective-permute-start.5 = (bf16[256,2304]{1,0:T(8,128)(2,1)S(1)}, bf16[256,2304]{1,0:T(8,128)(2,1)S(1)}, u32[]{:S(2)}, u32[]{:S(2)}) collective-permute-start(bf16[256,2304]{1,0:T(8,128)(2,1)S(1)} %get-tuple-element.185), channel_id=1, source_target_pairs={{0,8},{8,0},{16,24},{24,16},{1,9},{9,1},{17,25},{25,17},{2,10},{10... | collective-permute-start | bytes 3538952 | tf_op jit(solution)/shard_map/ppermute | solution.py:274
  117.7 49.1 %collective-permute-start.6 = (bf16[256,2304]{1,0:T(8,128)(2,1)S(1)}, bf16[256,2304]{1,0:T(8,128)(2,1)S(1)}, u32[]{:S(2)}, u32[]{:S(2)}) collective-permute-start(bf16[256,2304]{1,0:T(8,128)(2,1)S(1)} %get-tuple-element.185), channel_id=1, source_target_pairs={{0,16},{8,24},{16,0},{24,8},{1,17},{9,25},{17,1},{25,9},{2,18},{10... | collective-permute-start | bytes 3538952 | tf_op jit(solution)/shard_map/ppermute | solution.py:274
  117.9 50.0 %collective-permute-start.7 = (bf16[256,2304]{1,0:T(8,128)(2,1)S(1)}, bf16[256,2304]{1,0:T(8,128)(2,1)S(1)}, u32[]{:S(2)}, u32[]{:S(2)}) collective-permute-start(bf16[256,2304]{1,0:T(8,128)(2,1)S(1)} %get-tuple-element.185), channel_id=1, source_target_pairs={{0,24},{8,16},{16,8},{24,0},{1,25},{9,17},{17,9},{25,1},{2,26},{10... | collective-permute-start | bytes 3538952 | tf_op jit(solution)/shard_map/ppermute | solution.py:274
  194.0 28.9 %collective-permute-start.13 = (bf16[256,2304]{1,0:T(8,128)(2,1)S(1)}, bf16[256,2304]{1,0:T(8,128)(2,1)S(1)}, u32[]{:S(2)}, u32[]{:S(2)}) collective-permute-start(bf16[256,2304]{1,0:T(8,128)(2,1)S(1)} %convolution_convert_fusion.8), channel_id=1, source_target_pairs={{0,8},{8,0},{16,24},{24,16},{1,9},{9,1},{17,25},{25,17},{2,10},{10... | collective-permute-start | bytes 3538952 | tf_op jit(solution)/shard_map/ppermute | solution.py:274
  194.6 47.2 %collective-permute-start.12 = (bf16[256,2304]{1,0:T(8,128)(2,1)S(1)}, bf16[256,2304]{1,0:T(8,128)(2,1)S(1)}, u32[]{:S(2)}, u32[]{:S(2)}) collective-permute-start(bf16[256,2304]{1,0:T(8,128)(2,1)S(1)} %convolution_convert_fusion.9), channel_id=1, source_target_pairs={{0,16},{8,24},{16,0},{24,8},{1,17},{9,25},{17,1},{25,9},{2,18},{10... | collective-permute-start | bytes 3538952 | tf_op jit(solution)/shard_map/ppermute | solution.py:274
  194.8 47.0 %collective-permute-start.11 = (bf16[256,2304]{1,0:T(8,128)(2,1)S(1)}, bf16[256,2304]{1,0:T(8,128)(2,1)S(1)}, u32[]{:S(2)}, u32[]{:S(2)}) collective-permute-start(bf16[256,2304]{1,0:T(8,128)(2,1)S(1)} %convolution_convert_fusion.10), channel_id=1, source_target_pairs={{0,24},{8,16},{16,8},{24,0},{1,25},{9,17},{17,9},{25,1},{2,26},{10... | collective-permute-start | bytes 3538952 | tf_op jit(solution)/shard_map/ppermute | solution.py:274
  258.0 53.6 %collective-permute-start.14 = (bf16[256,2304]{1,0:T(8,128)(2,1)}, bf16[256,2304]{1,0:T(8,128)(2,1)}, u32[]{:S(2)}, u32[]{:S(2)}) collective-permute-start(bf16[256,2304]{1,0:T(8,128)(2,1)} %get-tuple-element.189), channel_id=1, source_target_pairs={{0,8},{8,0},{16,24},{24,16},{1,9},{9,1},{17,25},{25,17},{2,10},{10... | collective-permute-start | bytes 3538952 | tf_op jit(solution)/shard_map/ppermute | solution.py:274
  259.0 55.0 %collective-permute-start.15 = (bf16[256,2304]{1,0:T(8,128)(2,1)}, bf16[256,2304]{1,0:T(8,128)(2,1)}, u32[]{:S(2)}, u32[]{:S(2)}) collective-permute-start(bf16[256,2304]{1,0:T(8,128)(2,1)} %get-tuple-element.189), channel_id=1, source_target_pairs={{0,16},{8,24},{16,0},{24,8},{1,17},{9,25},{17,1},{25,9},{2,18},{10... | collective-permute-start | bytes 3538952 | tf_op jit(solution)/shard_map/ppermute | solution.py:274
  260.8 28.2 %collective-permute-start.20 = (bf16[72,640]{1,0:T(8,128)(2,1)S(1)}, bf16[72,640]{1,0:T(8,128)(2,1)S(1)}, u32[]{:S(2)}, u32[]{:S(2)}) collective-permute-start(bf16[72,640]{1,0:T(8,128)(2,1)S(1)} %get-tuple-element.148), channel_id=1, source_target_pairs={{0,8},{8,0},{16,24},{24,16},{1,9},{9,1},{17,25},{25,17},{2,10},{10... | collective-permute-start | bytes 276488 | tf_op jit(solution)/shard_map/ppermute | solution.py:274
  262.5 48.3 %collective-permute-start.21 = (bf16[72,640]{1,0:T(8,128)(2,1)S(1)}, bf16[72,640]{1,0:T(8,128)(2,1)S(1)}, u32[]{:S(2)}, u32[]{:S(2)}) collective-permute-start(bf16[72,640]{1,0:T(8,128)(2,1)S(1)} %get-tuple-element.147), channel_id=1, source_target_pairs={{0,16},{8,24},{16,0},{24,8},{1,17},{9,25},{17,1},{25,9},{2,18},{10... | collective-permute-start | bytes 276488 | tf_op jit(solution)/shard_map/ppermute | solution.py:274
  263.2 53.1 %collective-permute-start.16 = (bf16[256,2304]{1,0:T(8,128)(2,1)}, bf16[256,2304]{1,0:T(8,128)(2,1)}, u32[]{:S(2)}, u32[]{:S(2)}) collective-permute-start(bf16[256,2304]{1,0:T(8,128)(2,1)} %get-tuple-element.189), channel_id=1, source_target_pairs={{0,24},{8,16},{16,8},{24,0},{1,25},{9,17},{17,9},{25,1},{2,26},{10... | collective-permute-start | bytes 3538952 | tf_op jit(solution)/shard_map/ppermute | solution.py:274
  289.0 21.7 %collective-permute-start.22 = (bf16[72,640]{1,0:T(8,128)(2,1)S(1)}, bf16[72,640]{1,0:T(8,128)(2,1)S(1)}, u32[]{:S(2)}, u32[]{:S(2)}) collective-permute-start(bf16[72,640]{1,0:T(8,128)(2,1)S(1)} %get-tuple-element.146), channel_id=1, source_target_pairs={{0,24},{8,16},{16,8},{24,0},{1,25},{9,17},{17,9},{25,1},{2,26},{10... | collective-permute-start | bytes 276488 | tf_op jit(solution)/shard_map/ppermute | solution.py:274
  311.5 448.2 %reduce-scatter.7.cloned.1.call-start = ((), (), s32[]{:S(2)}) async-start(), calls=%async_computation.11 | async-start | bytes 3317760 | tf_op jit(solution)/shard_map/reduce_scatter | solution.py:324
  368.6 58.2 %collective-permute-start.31 = (bf16[256,1664]{1,0:T(8,128)(2,1)}, bf16[256,1664]{1,0:T(8,128)(2,1)S(1)}, u32[]{:S(2)}, u32[]{:S(2)}) collective-permute-start(bf16[256,1664]{1,0:T(8,128)(2,1)} %convolution_convert_fusion.11), channel_id=1, source_target_pairs={{0,8},{8,0},{16,24},{24,16},{1,9},{9,1},{17,25},{25,17},{2,10},{10... | collective-permute-start | bytes 2555912 | tf_op jit(solution)/shard_map/ppermute | solution.py:274
  373.3 53.5 %collective-permute-start.30 = (bf16[256,1664]{1,0:T(8,128)(2,1)}, bf16[256,1664]{1,0:T(8,128)(2,1)}, u32[]{:S(2)}, u32[]{:S(2)}) collective-permute-start(bf16[256,1664]{1,0:T(8,128)(2,1)} %convolution_convert_fusion.12), channel_id=1, source_target_pairs={{0,16},{8,24},{16,0},{24,8},{1,17},{9,25},{17,1},{25,9},{2,18},{10... | collective-permute-start | bytes 2555912 | tf_op jit(solution)/shard_map/ppermute | solution.py:274
  378.0 48.8 %collective-permute-start.29 = (bf16[256,1664]{1,0:T(8,128)(2,1)}, bf16[256,1664]{1,0:T(8,128)(2,1)}, u32[]{:S(2)}, u32[]{:S(2)}) collective-permute-start(bf16[256,1664]{1,0:T(8,128)(2,1)} %convolution_convert_fusion.13), channel_id=1, source_target_pairs={{0,24},{8,16},{16,8},{24,0},{1,25},{9,17},{17,9},{25,1},{2,26},{10... | collective-permute-start | bytes 2555912 | tf_op jit(solution)/shard_map/ppermute | solution.py:274
  402.4 12.9 %collective-permute-start.25 = (bf16[256,640]{1,0:T(8,128)(2,1)S(1)}, bf16[256,640]{1,0:T(8,128)(2,1)S(1)}, u32[]{:S(2)}, u32[]{:S(2)}) collective-permute-start(bf16[256,640]{1,0:T(8,128)(2,1)S(1)} %convolution_convert_fusion.17), channel_id=1, source_target_pairs={{0,8},{8,0},{16,24},{24,16},{1,9},{9,1},{17,25},{25,17},{2,10},{10... | collective-permute-start | bytes 983048 | tf_op jit(solution)/shard_map/ppermute | solution.py:274
  407.2 19.4 %collective-permute-start.24 = (bf16[256,640]{1,0:T(8,128)(2,1)S(1)}, bf16[256,640]{1,0:T(8,128)(2,1)S(1)}, u32[]{:S(2)}, u32[]{:S(2)}) collective-permute-start(bf16[256,640]{1,0:T(8,128)(2,1)S(1)} %convolution_convert_fusion.18), channel_id=1, source_target_pairs={{0,16},{8,24},{16,0},{24,8},{1,17},{9,25},{17,1},{25,9},{2,18},{10... | collective-permute-start | bytes 983048 | tf_op jit(solution)/shard_map/ppermute | solution.py:274
  415.2 11.4 collective-permute-start.23
  435.0 10.6 collective-permute-start.32
  435.9 14.7 %collective-permute-start.33 = (bf16[256,640]{1,0:T(8,128)(2,1)S(1)}, bf16[256,640]{1,0:T(8,128)(2,1)S(1)}, u32[]{:S(2)}, u32[]{:S(2)}) collective-permute-start(bf16[256,640]{1,0:T(8,128)(2,1)S(1)} %get-tuple-element.123), channel_id=1, source_target_pairs={{0,16},{8,24},{16,0},{24,8},{1,17},{9,25},{17,1},{25,9},{2,18},{10... | collective-permute-start | bytes 983048 | tf_op jit(solution)/shard_map/ppermute | solution.py:274
  437.3 14.3 %collective-permute-start.34 = (bf16[256,640]{1,0:T(8,128)(2,1)S(1)}, bf16[256,640]{1,0:T(8,128)(2,1)S(1)}, u32[]{:S(2)}, u32[]{:S(2)}) collective-permute-start(bf16[256,640]{1,0:T(8,128)(2,1)S(1)} %get-tuple-element.123), channel_id=1, source_target_pairs={{0,24},{8,16},{16,8},{24,0},{1,25},{9,17},{17,9},{25,1},{2,26},{10... | collective-permute-start | bytes 983048 | tf_op jit(solution)/shard_map/ppermute | solution.py:274
  458.1 312.2 %reduce-scatter.9.cloned.1.call-start = ((), (), s32[]{:S(2)}) async-start(), calls=%async_computation.12 | async-start | bytes 8626176 | tf_op jit(solution)/shard_map/reduce_scatter | solution.py:324
  459.6 21.9 %collective-permute-start.35 = (bf16[256,1664]{1,0:T(8,128)(2,1)S(1)}, bf16[256,1664]{1,0:T(8,128)(2,1)S(1)}, u32[]{:S(2)}, u32[]{:S(2)}) collective-permute-start(bf16[256,1664]{1,0:T(8,128)(2,1)S(1)} %get-tuple-element.121), channel_id=1, source_target_pairs={{0,8},{8,0},{16,24},{24,16},{1,9},{9,1},{17,25},{25,17},{2,10},{10... | collective-permute-start | bytes 2555912 | tf_op jit(solution)/shard_map/ppermute | solution.py:274
  460.8 37.4 %collective-permute-start.36 = (bf16[256,1664]{1,0:T(8,128)(2,1)S(1)}, bf16[256,1664]{1,0:T(8,128)(2,1)S(1)}, u32[]{:S(2)}, u32[]{:S(2)}) collective-permute-start(bf16[256,1664]{1,0:T(8,128)(2,1)S(1)} %get-tuple-element.121), channel_id=1, source_target_pairs={{0,16},{8,24},{16,0},{24,8},{1,17},{9,25},{17,1},{25,9},{2,18},{10... | collective-permute-start | bytes 2555912 | tf_op jit(solution)/shard_map/ppermute | solution.py:274
  462.0 36.2 %collective-permute-start.37 = (bf16[256,1664]{1,0:T(8,128)(2,1)S(1)}, bf16[256,1664]{1,0:T(8,128)(2,1)S(1)}, u32[]{:S(2)}, u32[]{:S(2)}) collective-permute-start(bf16[256,1664]{1,0:T(8,128)(2,1)S(1)} %get-tuple-element.121), channel_id=1, source_target_pairs={{0,24},{8,16},{16,8},{24,0},{1,25},{9,17},{17,9},{25,1},{2,26},{10... | collective-permute-start | bytes 2555912 | tf_op jit(solution)/shard_map/ppermute | solution.py:274
  510.9 291.2 %reduce-scatter.11.cloned.1.call-start = ((), (), s32[]{:S(2)}) async-start(), calls=%async_computation.13 | async-start | bytes 7962624 | tf_op jit(solution)/shard_map/reduce_scatter | solution.py:324
  579.4 28.9 %collective-permute-start.40 = (bf16[256,2304]{1,0:T(8,128)(2,1)S(1)}, bf16[256,2304]{1,0:T(8,128)(2,1)S(1)}, u32[]{:S(2)}, u32[]{:S(2)}) collective-permute-start(bf16[256,2304]{1,0:T(8,128)(2,1)S(1)} %get-tuple-element.94), channel_id=1, source_target_pairs={{0,8},{8,0},{16,24},{24,16},{1,9},{9,1},{17,25},{25,17},{2,10},{10... | collective-permute-start | bytes 3538952 | tf_op jit(solution)/shard_map/ppermute | solution.py:274
  579.4 49.0 %collective-permute-start.39 = (bf16[256,2304]{1,0:T(8,128)(2,1)S(1)}, bf16[256,2304]{1,0:T(8,128)(2,1)S(1)}, u32[]{:S(2)}, u32[]{:S(2)}) collective-permute-start(bf16[256,2304]{1,0:T(8,128)(2,1)S(1)} %get-tuple-element.95), channel_id=1, source_target_pairs={{0,16},{8,24},{16,0},{24,8},{1,17},{9,25},{17,1},{25,9},{2,18},{10... | collective-permute-start | bytes 3538952 | tf_op jit(solution)/shard_map/ppermute | solution.py:274
  580.3 48.8 %collective-permute-start.38 = (bf16[256,2304]{1,0:T(8,128)(2,1)S(1)}, bf16[256,2304]{1,0:T(8,128)(2,1)S(1)}, u32[]{:S(2)}, u32[]{:S(2)}) collective-permute-start(bf16[256,2304]{1,0:T(8,128)(2,1)S(1)} %get-tuple-element.93), channel_id=1, source_target_pairs={{0,24},{8,16},{16,8},{24,0},{1,25},{9,17},{17,9},{25,1},{2,26},{10... | collective-permute-start | bytes 3538952 | tf_op jit(solution)/shard_map/ppermute | solution.py:274
  639.8 28.8 %collective-permute-start.41 = (bf16[256,2304]{1,0:T(8,128)(2,1)S(1)}, bf16[256,2304]{1,0:T(8,128)(2,1)S(1)}, u32[]{:S(2)}, u32[]{:S(2)}) collective-permute-start(bf16[256,2304]{1,0:T(8,128)(2,1)S(1)} %get-tuple-element.87), channel_id=1, source_target_pairs={{0,8},{8,0},{16,24},{24,16},{1,9},{9,1},{17,25},{25,17},{2,10},{10... | collective-permute-start | bytes 3538952 | tf_op jit(solution)/shard_map/ppermute | solution.py:274
  641.3 49.7 %collective-permute-start.42 = (bf16[256,2304]{1,0:T(8,128)(2,1)S(1)}, bf16[256,2304]{1,0:T(8,128)(2,1)S(1)}, u32[]{:S(2)}, u32[]{:S(2)}) collective-permute-start(bf16[256,2304]{1,0:T(8,128)(2,1)S(1)} %get-tuple-element.87), channel_id=1, source_target_pairs={{0,16},{8,24},{16,0},{24,8},{1,17},{9,25},{17,1},{25,9},{2,18},{10... | collective-permute-start | bytes 3538952 | tf_op jit(solution)/shard_map/ppermute | solution.py:274
  642.1 49.1 %collective-permute-start.43 = (bf16[256,2304]{1,0:T(8,128)(2,1)S(1)}, bf16[256,2304]{1,0:T(8,128)(2,1)S(1)}, u32[]{:S(2)}, u32[]{:S(2)}) collective-permute-start(bf16[256,2304]{1,0:T(8,128)(2,1)S(1)} %get-tuple-element.87), channel_id=1, source_target_pairs={{0,24},{8,16},{16,8},{24,0},{1,25},{9,17},{17,9},{25,1},{2,26},{10... | collective-permute-start | bytes 3538952 | tf_op jit(solution)/shard_map/ppermute | solution.py:274
  727.7 285.4 %reduce-scatter.5.cloned.1.call-start = ((), (), s32[]{:S(2)}) async-start(), calls=%async_computation.10 | async-start | bytes 23887872 | tf_op jit(solution)/shard_map/reduce_scatter | solution.py:324
  760.8 5.5 collective-permute-start.47
  763.8 6.4 collective-permute-start.49
  771.7 6.2 collective-permute-start.50
  772.8 8.3 collective-permute-start.51
  774.8 7.0 collective-permute-start.52
  786.9 286.4 %collective-permute-start.55 = (bf16[256,2304]{1,0:T(8,128)(2,1)}, bf16[256,2304]{1,0:T(8,128)(2,1)}, u32[]{:S(2)}, u32[]{:S(2)}) collective-permute-start(bf16[256,2304]{1,0:T(8,128)(2,1)} %convolution_convert_fusion.5), channel_id=1, source_target_pairs={{0,8},{8,0},{16,24},{24,16},{1,9},{9,1},{17,25},{25,17},{2,10},{10... | collective-permute-start | bytes 3538952 | tf_op jit(solution)/shard_map/ppermute | solution.py:274
  792.8 281.9 %collective-permute-start.54 = (bf16[256,2304]{1,0:T(8,128)(2,1)}, bf16[256,2304]{1,0:T(8,128)(2,1)}, u32[]{:S(2)}, u32[]{:S(2)}) collective-permute-start(bf16[256,2304]{1,0:T(8,128)(2,1)} %convolution_convert_fusion.6), channel_id=1, source_target_pairs={{0,16},{8,24},{16,0},{24,8},{1,17},{9,25},{17,1},{25,9},{2,18},{10... | collective-permute-start | bytes 3538952 | tf_op jit(solution)/shard_map/ppermute | solution.py:274
  796.0 278.7 %collective-permute-start.53 = (bf16[256,2304]{1,0:T(8,128)(2,1)}, bf16[256,2304]{1,0:T(8,128)(2,1)}, u32[]{:S(2)}, u32[]{:S(2)}) collective-permute-start(bf16[256,2304]{1,0:T(8,128)(2,1)} %convolution_convert_fusion.7), channel_id=1, source_target_pairs={{0,24},{8,16},{16,8},{24,0},{1,25},{9,17},{17,9},{25,1},{2,26},{10... | collective-permute-start | bytes 3538952 | tf_op jit(solution)/shard_map/ppermute | solution.py:274
  804.3 289.7 %collective-permute-start.56 = (bf16[72,1536]{1,0:T(8,128)(2,1)}, bf16[72,1536]{1,0:T(8,128)(2,1)S(1)}, u32[]{:S(2)}, u32[]{:S(2)}) collective-permute-start(bf16[72,1536]{1,0:T(8,128)(2,1)} %get-tuple-element.135), channel_id=1, source_target_pairs={{0,8},{8,0},{16,24},{24,16},{1,9},{9,1},{17,25},{25,17},{2,10},{10... | collective-permute-start | bytes 663560 | tf_op jit(solution)/shard_map/ppermute | solution.py:274
  1014.7 14.8 %collective-permute-start.44 = (bf16[72,4608]{1,0:T(8,128)(2,1)S(1)}, bf16[72,4608]{1,0:T(8,128)(2,1)S(1)}, u32[]{:S(2)}, u32[]{:S(2)}) collective-permute-start(bf16[72,4608]{1,0:T(8,128)(2,1)S(1)} %get-tuple-element.110), channel_id=1, source_target_pairs={{0,8},{8,0},{16,24},{24,16},{1,9},{9,1},{17,25},{25,17},{2,10},{10... | collective-permute-start | bytes 1990664 | tf_op jit(solution)/shard_map/ppermute | solution.py:274
  1029.5 21.0 %collective-permute-start.45 = (bf16[72,4608]{1,0:T(8,128)(2,1)S(1)}, bf16[72,4608]{1,0:T(8,128)(2,1)S(1)}, u32[]{:S(2)}, u32[]{:S(2)}) collective-permute-start(bf16[72,4608]{1,0:T(8,128)(2,1)S(1)} %get-tuple-element.109), channel_id=1, source_target_pairs={{0,16},{8,24},{16,0},{24,8},{1,17},{9,25},{17,1},{25,9},{2,18},{10... | collective-permute-start | bytes 1990664 | tf_op jit(solution)/shard_map/ppermute | solution.py:274
  1050.5 11.7 collective-permute-start.46
  1062.2 31.8 %collective-permute-start.57 = (bf16[72,1536]{1,0:T(8,128)(2,1)}, bf16[72,1536]{1,0:T(8,128)(2,1)}, u32[]{:S(2)}, u32[]{:S(2)}) collective-permute-start(bf16[72,1536]{1,0:T(8,128)(2,1)} %get-tuple-element.134), channel_id=1, source_target_pairs={{0,16},{8,24},{16,0},{24,8},{1,17},{9,25},{17,1},{25,9},{2,18},{10... | collective-permute-start | bytes 663560 | tf_op jit(solution)/shard_map/ppermute | solution.py:274
  1073.2 20.8 %collective-permute-start.58 = (bf16[72,1536]{1,0:T(8,128)(2,1)}, bf16[72,1536]{1,0:T(8,128)(2,1)}, u32[]{:S(2)}, u32[]{:S(2)}) collective-permute-start(bf16[72,1536]{1,0:T(8,128)(2,1)} %get-tuple-element.133), channel_id=1, source_target_pairs={{0,24},{8,16},{16,8},{24,0},{1,25},{9,17},{17,9},{25,1},{2,26},{10... | collective-permute-start | bytes 663560 | tf_op jit(solution)/shard_map/ppermute | solution.py:274
  1103.5 88.7 %all-to-all-start = ((bf16[896,8,256]{2,1,0:T(8,128)(2,1)}), bf16[896,8,256]{2,1,0:T(8,128)(2,1)}, u32[]{:S(2)}, u32[]{:S(2)}) async-start(bf16[896,8,256]{2,1,0:T(8,128)(2,1)} %get-tuple-element.30), calls=%async_computation.4 | async-start | bytes 7340032 | tf_op jit(solution)/shard_map/all_to_all | solution.py:604
  1192.2 38.9 %all-to-all-start.1 = ((bf16[352,8,256]{2,1,0:T(8,128)(2,1)}), bf16[352,8,256]{2,1,0:T(8,128)(2,1)S(1)}, u32[]{:S(2)}, u32[]{:S(2)}) async-start(bf16[352,8,256]{2,1,0:T(8,128)(2,1)} %get-tuple-element.31), calls=%async_computation.5 | async-start | bytes 2883584 | tf_op jit(solution)/shard_map/all_to_all | solution.py:604
  (75 other events, 1292.6 us)
Sparse Core Ops, SparseCore 0:
  25.2 71.5 all-gather.4
  98.9 186.2 all-gather.6
  287.4 74.2 all-gather.10
  363.8 35.0 all-gather.8
  458.2 37.1 reduce-scatter.6
  511.0 79.8 reduce-scatter.8
  727.8 74.2 reduce-scatter.10
  804.4 208.5 reduce-scatter.4
